TPU v7x, 256 devices: a whole 4x4x8 slice. The times are simulated.
256 devices in a mesh: fsdp: 256 (over y, x, z, core).
Axes of the slice: x: 4, y: 4, z: 8, core: 2. Of those that a mesh axis runs over, the one named last changes fastest.
Arguments:
- tokens: bfloat16 [32768, 2048], P('fsdp'), may hold values from -6 to 6
- member_ids: int32 [256], P('fsdp'), may hold values from 0 to 3
- norm_gain: float32 [2048], replicated, may hold values from 0.1 to 6
- weight: bfloat16 [2048, 1152], P('fsdp'), may hold values from -0.125 to 0.125
- qkv_bias: float32 [1152], replicated, may hold values from -160 to 160
- fast_in: float32 [4, 2048], replicated, may hold values from 0.25 to 1.75
- fast_out: float32 [4, 1152], replicated, may hold values from 0.25 to 1.75
- cotangent: bfloat16 [32768, 896], P('fsdp'), may hold values from -64 to 64
- weight_first: float32 [2048, 1152], P('fsdp'), may hold values from -0.0007324219 to 0.0007324219
- weight_second: float32 [2048, 1152], P('fsdp'), may hold values from 1e-09 to 1e-07
- in_first: float32 [4, 2048], replicated, may hold values from -0.015625 to 0.015625
- in_second: float32 [4, 2048], replicated, may hold values from 1e-07 to 1e-05
- out_first: float32 [4, 1152], replicated, may hold values from -0.015625 to 0.015625
- out_second: float32 [4, 1152], replicated, may hold values from 1e-07 to 1e-05
Outputs:
- weight_step: float32 [2048, 1152], P('fsdp')
- in_step: float32 [4, 2048], replicated
- out_step: float32 [4, 1152], replicated
All inputs are finite; a program needn't handle non-finite values.
Results may differ from a plain program's by a relative error of at most 0.0045.
The roundings to bfloat16 on the way count: a program that leaves them out, or rounds other values in their place, can miss the bound.
Values may be sent and summed in bfloat16 or wider, within the bound.
No kernel may reach another device: no remote copies, remote signals or barrier semaphores. Data moves between devices by JAX's collectives and lax.ppermute only.
A program may use at most 128 MiB of HBM per device.

v0:
```python
import math

import jax
import jax.numpy as jnp
from jax import lax
from jax.experimental import pallas as pl
from jax.experimental.pallas import tpu as pltpu
from jax.sharding import PartitionSpec as P


AXIS = "fsdp"
NY, NX, NZ = 4, 4, 8
HEAD_DIM = 64
GROUP_Q = 448
LANES = 640
SEQ = 128
FEATURES = 2048
TILES = FEATURES // 128

norm_eps = 1e-06
clip_limit = 1.0
beta_one = 0.9
beta_two = 0.95
adam_eps = 1e-08
rope_base = 1000000.0
step_number = 10.0


f32 = jnp.float32
bf16 = jnp.bfloat16


def device_of(y, x, z, c):
    return ((y * NX + x) * NZ + z) * 2 + c


COLUMNS = [
    [device_of(y, x, z, c) for z in range(NZ) for c in range(2)] for y in range(NY) for x in range(NX)
]
PAIRS = [
    [device_of(y, x, z, c) for c in range(2)] for y in range(NY) for x in range(NX) for z in range(NZ)
]
INNER_RINGS = [
    [device_of(y, x, z, 0) for x in range(NX)] for y in range(NY) for z in range(NZ)
] + [[device_of(y, x, z, 1) for y in range(NY)] for x in range(NX) for z in range(NZ)]
OUTER_RINGS = [
    [device_of(y, x, z, 0) for y in range(NY)] for x in range(NX) for z in range(NZ)
] + [[device_of(y, x, z, 1) for x in range(NX)] for y in range(NY) for z in range(NZ)]


def shift(array, rings, step):
    pairs = [(ring[i], ring[(i + step) % len(ring)]) for ring in rings for i in range(len(ring))]
    return lax.ppermute(array, AXIS, pairs)


def rope_tables():
    half_width = HEAD_DIM // 2
    spacing = jnp.arange(half_width, dtype=f32) * (2.0 / HEAD_DIM)
    frequency = jnp.exp(-math.log(rope_base) * spacing)
    angles = jnp.arange(SEQ, dtype=f32)[:, None] * frequency[None, :]
    cosine, sine = jnp.cos(angles), jnp.sin(angles)
    return (
        jnp.concatenate([cosine] * 4, axis=1),
        jnp.concatenate([-sine, sine, -sine, sine], axis=1),
    )


def dot(left, right, left_dim, right_dim):
    return lax.dot_general(
        left, right, (((left_dim,), (right_dim,)), ((), ())), preferred_element_type=f32
    )


def scale_kernel(tile_of, own, partner, gain, rates, *scaled):
    for part, tokens in enumerate((own, partner)):
        rows = slice(part * SEQ, (part + 1) * SEQ)
        wide = tokens[...].astype(f32)
        inv = lax.rsqrt(jnp.mean(wide * wide, axis=1, keepdims=True) + norm_eps)
        for i in range(TILES):
            lanes = pl.ds(pl.multiple_of(tile_of[i] * 128, 128), 128)
            normed = tokens[:, lanes].astype(f32) * inv * gain[:, lanes]
            spot = slice(i % 4 * 128, (i % 4 + 1) * 128)
            scaled[i // 4][rows, spot] = (normed * rates[part : part + 1, lanes]).astype(bf16)


def project_kernel(scaled0, scaled1, scaled3, near, right, left, partial):
    partial[...] = (
        dot(scaled0[...], near[...], 1, 0)
        + dot(scaled1[...], right[...], 1, 0)
        + dot(scaled3[...], left[...], 1, 0)
    )


def attention_kernel(
    members, scaled2, partial, far_a, far_b, slopes, bias, cosine_ref, sine_ref, cot_own, cot_partner, down
):
    cosine = cosine_ref[...]
    sine = sine_ref[...]
    lane = lax.broadcasted_iota(jnp.int32, (SEQ, 128), 1)
    row = lax.broadcasted_iota(jnp.int32, (SEQ, 128), 0)
    low = lane < 64
    first = (lane & 63) < 32
    causal = row >= lane
    score_scale = 1.0 / math.sqrt(HEAD_DIM)

    def swap(tile):
        return jnp.where(first, pltpu.roll(tile, 96, 1), pltpu.roll(tile, 32, 1))

    def half_turn(tile):
        return pltpu.roll(tile, 64, 1)

    projected = (
        partial[...]
        + dot(scaled2[:, :256], far_a[...], 1, 0)
        + dot(scaled2[:, 256:], far_b[...], 1, 0)
    )
    totals = []
    for part, cot in enumerate((cot_own, cot_partner)):
        rows = slice(part * SEQ, (part + 1) * SEQ)
        raw = projected[rows]
        slope = slopes[part : part + 1, :]
        biased = raw * slope + bias[...]
        turned = []
        for t in range(4):
            tile = biased[:, t * 128 : (t + 1) * 128]
            turned.append(tile * cosine + swap(tile) * sine)
        keys = turned[3]
        values = biased[:, 512:640]
        key_pair = jnp.concatenate(
            [jnp.where(low, half_turn(keys), 0.0), jnp.where(low, 0.0, keys)], axis=0
        ).astype(bf16)
        value_pair = jnp.concatenate(
            [jnp.where(low, values, 0.0), jnp.where(low, 0.0, half_turn(values))], axis=0
        ).astype(bf16)
        grads = []
        key_sum = jnp.zeros((2 * SEQ, 128), f32)
        value_sum = jnp.zeros((2 * SEQ, 128), f32)
        for t in range(4):
            query = turned[t].astype(bf16)
            upstream = cot[:, t * 128 : (t + 1) * 128]
            scores = dot(query, key_pair, 1, 1) * score_scale
            grad_probs = dot(upstream, value_pair, 1, 1)
            probs_bf, grads_bf = [], []
            for h in range(2):
                side = slice(h * SEQ, (h + 1) * SEQ)
                masked = jnp.where(causal, scores[:, side], -jnp.inf)
                raised = jnp.exp(masked - jnp.max(masked, axis=1, keepdims=True))
                probs = raised / jnp.sum(raised, axis=1, keepdims=True)
                gp = grad_probs[:, side]
                centre = jnp.sum(gp * probs, axis=1, keepdims=True)
                probs_bf.append(probs.astype(bf16))
                grads_bf.append((probs * (gp - centre) * score_scale).astype(bf16))
            probs_pair = jnp.concatenate(probs_bf, axis=1)
            grad_pair = jnp.concatenate(grads_bf, axis=1)
            grads.append(dot(grad_pair, key_pair, 1, 0))
            key_sum += dot(grad_pair, query, 0, 0)
            value_sum += dot(probs_pair, upstream, 0, 0)
        grad_key = jnp.where(low, 0.0, half_turn(key_sum[:SEQ]) + key_sum[SEQ:])
        grad_value = jnp.where(low, value_sum[:SEQ] + half_turn(value_sum[SEQ:]), 0.0)
        grads[3] = jnp.where(low, grads[3], grad_key)
        grads = [g * cosine - swap(g) * sine for g in grads] + [grad_value]
        grad_biased = jnp.concatenate(grads, axis=1)
        totals.append(jnp.sum(raw * grad_biased, axis=0, keepdims=True))
        down[rows, :] = (grad_biased * slope).astype(bf16)
    spread = jnp.zeros((SEQ, 128), f32)
    for part in range(2):
        for t in range(5):
            spread += jnp.where(
                row == 64 + 4 * t + members[part], totals[part][:, t * 128 : (t + 1) * 128], 0.0
            )
    spread = spread.T
    high = spread.astype(bf16).astype(f32)
    spread = high + pltpu.roll(spread - high, 20, 1)
    for part in range(2):
        rows = slice(part * SEQ, (part + 1) * SEQ)
        tail = jnp.where(lane == 127, members[part].astype(f32), 0.0)
        if part == 0:
            tail = jnp.where(lane == 127, tail, spread)
        last = down[rows, 512:640].astype(f32)
        down[rows, 512:640] = jnp.where(low, last, tail).astype(bf16)


def weight_terms(scaled, down, plane, carry):
    grads, totals, tails = carry
    back = dot(down, plane, 1, 1)
    grads = grads + dot(scaled, down, 0, 0)
    row = lax.broadcasted_iota(jnp.int32, (8, 512), 0)
    for part in range(scaled.shape[0] // SEQ):
        rows = slice(part * SEQ, (part + 1) * SEQ)
        member = down[part * SEQ : part * SEQ + 1, 639:640].astype(f32).astype(jnp.int32)
        total = jnp.sum(scaled[rows].astype(f32) * back[rows], axis=0, keepdims=True)
        totals = totals + jnp.where(row == member, total, 0.0)
    return grads, totals, tails


def near_kernel(scaled, down, plane, grads, totals, tails):
    zero = (jnp.zeros((512, LANES), f32), jnp.zeros((8, 512), f32), None)
    total = weight_terms(scaled[...], down[...], plane[...], zero)
    grads[...], totals[...] = total[:2]
    tails[...] = down[:SEQ, 512:].astype(f32)


def middle_kernel(
    scaled1, down1, scaled3, down3, plane, grads_in, totals_in, tails_in, grads, totals, tails
):
    total = (grads_in[...], totals_in[...], None)
    for scaled, down in ((scaled1, down1), (scaled3, down3)):
        total = weight_terms(scaled[...], down[...], plane[...], total)
    grads[...], totals[...] = total[:2]
    tails[...] = tails_in[...] + down1[:SEQ, 512:].astype(f32) + down3[:SEQ, 512:].astype(f32)


def last_kernel(
    tile_of, scaled, down_a, down_b, plane, grads_in, totals_in, tails_in, rates, part0, part1, part2, part3
):
    total = (grads_in[...], totals_in[...], None)
    total = weight_terms(scaled[:SEQ, :], down_a[...], plane[...], total)
    grads, totals, _ = weight_terms(scaled[SEQ:, :], down_b[...], plane[...], total)
    tails = tails_in[...] + down_a[:, 512:].astype(f32)
    tails = tails + pltpu.roll(tails, 108, 1)
    lane = lax.broadcasted_iota(jnp.int32, (SEQ, 128), 1)
    for i, result in enumerate((part0, part1, part2, part3)):
        tile = tile_of[i]
        here = slice(i * 128, (i + 1) * 128)
        shares = totals[:, here] / rates[:, pl.ds(pl.multiple_of(tile * 128, 128), 128)]
        extra = jnp.concatenate([jnp.zeros((64, 128), f32), shares, jnp.zeros((56, 128), f32)], axis=0).T
        for t in range(5):
            moved = pltpu.roll(tails, (4 - 4 * t) % 128, 1)
            extra = jnp.where((lane >= 68) & (lane < 72) & (tile == t), moved, extra)
        result[:, :512] = grads[here, :512].astype(result.dtype)
        result[:, 512:] = jnp.where(lane < 64, grads[here, 512:], extra).astype(result.dtype)


def split_kernel(weight, spread):
    rows = weight[...]
    for core in range(2):
        cols = pad_lanes(group_columns(rows, core), LANES)
        for z in range(NZ):
            spread[2 * z + core, :, :] = cols


def exact_dot(values, picks):
    high = values.astype(bf16)
    rest = values - high.astype(f32)
    middle = rest.astype(bf16)
    low = (rest - middle.astype(f32)).astype(bf16)
    return dot(high, picks, 1, 0) + dot(middle, picks, 1, 0) + dot(low, picks, 1, 0)


def pack_kernel(pieces, grad_rows, packed):
    wide = pieces[...].astype(f32)
    sums = [sum(wide[2 * z + core] for z in range(NZ)) for core in range(2)]
    grads = whole_columns(*sums)
    grad_rows[...] = grads
    square = jnp.sum(jnp.sum(grads * grads, axis=1, keepdims=True), axis=0, keepdims=True)
    tails = [s[:, 512:] for s in sums]
    source = lax.broadcasted_iota(jnp.int32, (128, 128), 0)
    target = lax.broadcasted_iota(jnp.int32, (128, 128), 1)
    field = target // 8
    from_in = ((source == 64 + field) & (field < 4)).astype(bf16)
    from_zero = ((source == 64 + field) & (field >= 4) & (field < 8)).astype(bf16)
    from_one = ((source == 60 + field) & (field >= 8) & (field < 12)).astype(bf16)
    moved = (
        exact_dot(tails[0] + tails[1], from_in)
        + exact_dot(tails[0], from_zero)
        + exact_dot(tails[1], from_one)
    )
    row = lax.broadcasted_iota(jnp.int32, (8, 128), 0)
    lane = lax.broadcasted_iota(jnp.int32, (8, 128), 1)
    line = jnp.sum(jnp.where(row == (lane & 7), moved, 0.0), axis=0, keepdims=True)
    packed[...] = jnp.where(lane[:1] == 96, square, line)


def finish_kernel(
    everyone, grad_rows, weight_first, weight_second, in_first, in_second, out_first, out_second,
    weight_step, in_step, out_step,
):
    shares = everyone[...]
    lane = lax.broadcasted_iota(jnp.int32, (256, 128), 1)
    row = lax.broadcasted_iota(jnp.int32, (256, 128), 0)
    source = lax.broadcasted_iota(jnp.int32, (128, 128), 0)
    target = lax.broadcasted_iota(jnp.int32, (128, 128), 1)
    mine = (row & 15) == lane // 8
    fields = []
    for field in range(12):
        picks = (source == 8 * field + (target & 7)).astype(bf16)
        moved = jnp.where(mine, exact_dot(shares, picks), 0.0)
        fields.append(jnp.sum(moved.reshape(16, 16, 128), axis=1))

    def as_rows(start, tiles):
        return jnp.concatenate(
            [jnp.concatenate([f[t : t + 1] for t in range(tiles)], axis=1) for f in fields[start : start + 4]],
            axis=0,
        )

    in_grad = as_rows(0, TILES)
    out_grad = whole_columns(as_rows(4, 5), as_rows(8, 5))

    def total(values):
        return jnp.sum(jnp.sum(values, axis=1, keepdims=True), axis=0, keepdims=True)

    squared = (
        total(jnp.where(lane == 96, shares, 0.0)) + total(in_grad * in_grad) + total(out_grad * out_grad)
    )
    clip_scale = clip_limit / jnp.maximum(jnp.sqrt(squared), clip_limit)
    weight_step[...] = adam_direction(grad_rows[...], weight_first[...], weight_second[...], clip_scale)
    in_step[...] = adam_direction(in_grad, in_first[...], in_second[...], clip_scale)
    out_step[...] = adam_direction(out_grad, out_first[...], out_second[...], clip_scale)


SMEM = pl.BlockSpec(memory_space=pltpu.SMEM)
VMEM = pl.BlockSpec(memory_space=pltpu.VMEM)


def call(kernel, scalars, arrays, out_shape):
    single = not isinstance(out_shape, (list, tuple))
    return pl.pallas_call(
        kernel,
        in_specs=[SMEM] * len(scalars) + [VMEM] * len(arrays),
        out_specs=VMEM if single else [VMEM] * len(out_shape),
        out_shape=out_shape,
        compiler_params=pltpu.CompilerParams(vmem_limit_bytes=48 * 1024 * 1024),
    )(*scalars, *arrays)


def group_columns(array, group):
    pieces = [
        array[:, group * GROUP_Q : (group + 1) * GROUP_Q],
        array[:, 896 + group * 64 : 960 + group * 64],
        array[:, 1024 + group * 64 : 1088 + group * 64],
    ]
    return jnp.concatenate(pieces, axis=1)


def whole_columns(zero, one):
    return jnp.concatenate(
        [
            zero[:, :448],
            one[:, :448],
            zero[:, 448:512],
            one[:, 448:512],
            zero[:, 512:576],
            one[:, 512:576],
        ],
        axis=1,
    )


def pad_lanes(array, width):
    return jnp.pad(array, ((0, 0), (0, width - array.shape[1])))


def adam_direction(gradient, moment_one, moment_two, clip_scale):
    clipped = gradient * clip_scale
    first_new = beta_one * moment_one + (1.0 - beta_one) * clipped
    second_new = beta_two * moment_two + (1.0 - beta_two) * clipped * clipped
    first_hat = first_new / (1.0 - beta_one**step_number)
    second_hat = second_new / (1.0 - beta_two**step_number)
    return first_hat / (jnp.sqrt(second_hat) + adam_eps)


def per_device(
    tokens,
    member_ids,
    norm_gain,
    weight,
    qkv_bias,
    fast_in,
    fast_out,
    cotangent,
    weight_first,
    weight_second,
    in_first,
    in_second,
    out_first,
    out_second,
):
    here = lax.axis_index(AXIS)
    core = here % 2
    x_spot = (here // (2 * NZ)) % NX
    y_spot = here // (2 * NZ * NX)
    is_zero = core == 0

    spread = call(split_kernel, [], [weight], jax.ShapeDtypeStruct((2 * NZ, 8, LANES), bf16))
    column = lax.all_to_all(
        spread, AXIS, split_axis=0, concat_axis=0, tiled=True, axis_index_groups=COLUMNS
    ).reshape(NZ * 16, LANES)
    column, tokens, cotangent, member_ids = lax.optimization_barrier(
        (column, tokens, cotangent, member_ids)
    )
    plane = jnp.concatenate([column] + [shift(column, INNER_RINGS, j) for j in (1, 2, 3)], axis=0)
    right = shift(plane, OUTER_RINGS, 1)
    left = shift(plane, OUTER_RINGS, -1)
    far_a = shift(right[:256], OUTER_RINGS, 1)
    far_b = shift(left[256:], OUTER_RINGS, -1)

    partner_tokens = shift(tokens, PAIRS, 1)
    cot_zero = pad_lanes(cotangent[:, :GROUP_Q], 512)
    cot_one = pad_lanes(cotangent[:, GROUP_Q:], 512)
    cot_own = jnp.where(is_zero, cot_zero, cot_one)
    cot_partner = shift(jnp.where(is_zero, cot_one, cot_zero), PAIRS, 1)
    member_tile = jnp.broadcast_to(member_ids.astype(f32)[:, None], (8, 128))
    partner_member = shift(member_tile, PAIRS, 1)[0, 0].astype(jnp.int32)
    members = jnp.stack([member_ids[0], partner_member])
    pick = (members[:, None] == jnp.arange(4, dtype=jnp.int32)[None, :]).astype(f32)
    rates = jnp.sum(pick[:, :, None] * fast_in[None], axis=1)
    slopes_all = jnp.sum(pick[:, :, None] * fast_out[None], axis=1)
    slopes = pad_lanes(
        jnp.where(is_zero, group_columns(slopes_all, 0), group_columns(slopes_all, 1)), LANES
    )
    bias_all = qkv_bias[None, :]
    bias = pad_lanes(jnp.where(is_zero, group_columns(bias_all, 0), group_columns(bias_all, 1)), LANES)
    gain = norm_gain[None, :]
    factors = jnp.concatenate([fast_in, jnp.ones((4, FEATURES), f32)])
    cosine, sine = rope_tables()

    turn = jnp.arange(TILES, dtype=jnp.int32)
    outer, inner = turn // 4, turn % 4
    y_back = jnp.where(is_zero, outer, inner)
    x_back = jnp.where(is_zero, inner, outer)
    tile_of = ((y_spot - y_back) % NY) * NX + (x_spot - x_back) % NX

    scaled = call(
        scale_kernel, [tile_of], [tokens, partner_tokens, gain, rates], [jax.ShapeDtypeStruct((2 * SEQ, 512), bf16)] * 4
    )
    partial = call(
        project_kernel,
        [],
        [scaled[0], scaled[1], scaled[3], plane, right, left],
        jax.ShapeDtypeStruct((2 * SEQ, LANES), f32),
    )
    far_scaled = [shift(scaled[j], OUTER_RINGS, -j) for j in (1, 2, 3)]
    down = call(
        attention_kernel,
        [members],
        [scaled[2], partial, far_a, far_b, slopes, bias, cosine, sine, cot_own, cot_partner],
        jax.ShapeDtypeStruct((2 * SEQ, LANES), bf16),
    )
    down_back = shift(down, OUTER_RINGS, 1)
    down_ahead = shift(down, OUTER_RINGS, -1)
    sums = [
        jax.ShapeDtypeStruct((512, LANES), f32),
        jax.ShapeDtypeStruct((8, 512), f32),
        jax.ShapeDtypeStruct((SEQ, 128), f32),
    ]
    near = call(near_kernel, [], [scaled[0], down, plane], sums)
    down_far_a = shift(down_back[:SEQ], OUTER_RINGS, 1)
    down_far_b = shift(down_ahead[SEQ:], OUTER_RINGS, -1)
    middle = call(middle_kernel, [], [far_scaled[0], down_ahead, far_scaled[2], down_back, plane, *near], sums)
    parts = call(
        last_kernel,
        [tile_of],
        [far_scaled[1], down_far_a, down_far_b, plane, *middle, factors],
        [jax.ShapeDtypeStruct((SEQ, LANES), f32)] + [jax.ShapeDtypeStruct((SEQ, LANES), bf16)] * 3,
    )
    got = [shift(parts[j], INNER_RINGS, -j) for j in (2, 1, 3)]
    column_sum = parts[0] + sum(g.astype(f32) for g in got)
    pieces = lax.all_to_all(
        column_sum.astype(bf16).reshape(2 * NZ, 8, LANES),
        AXIS,
        split_axis=0,
        concat_axis=0,
        tiled=True,
        axis_index_groups=COLUMNS,
    )
    grad_rows, packed = call(
        pack_kernel, [], [pieces], [jax.ShapeDtypeStruct((8, 1152), f32), jax.ShapeDtypeStruct((1, 128), f32)]
    )
    everyone = lax.all_to_all(
        jnp.broadcast_to(packed[:, None], (256, 1, 128)), AXIS, split_axis=0, concat_axis=0, tiled=True
    ).reshape(256, 128)
    return tuple(
        call(
            finish_kernel,
            [],
            [everyone, grad_rows, weight_first, weight_second, in_first, in_second, out_first, out_second],
            [
                jax.ShapeDtypeStruct((8, 1152), f32),
                jax.ShapeDtypeStruct((4, FEATURES), f32),
                jax.ShapeDtypeStruct((4, 1152), f32),
            ],
        )
    )


def solution(mesh):
    return jax.shard_map(
        per_device,
        mesh=mesh,
        in_specs=(
            P(AXIS, None),
            P(AXIS),
            P(),
            P(AXIS, None),
            P(),
            P(),
            P(),
            P(AXIS, None),
            P(AXIS, None),
            P(AXIS, None),
            P(),
            P(),
            P(),
            P(),
        ),
        out_specs=(P(AXIS, None), P(), P()),
        check_vma=False,
    )
```

profile of v0, /device:TPU:1, one launch (start us, length us, event | category | flops | bytes accessed | tf_op | source)
XLA Modules:
  0.0 119.6 jit_solution(15387657167418634952)
XLA Ops:
  2.2 10.0 %all-to-all-start = ((bf16[16,8,640]{2,1,0:T(8,128)(2,1)}), bf16[16,8,640]{2,1,0:T(8,128)(2,1)S(1)}, u32[]{:S(2)}, u32[]{:S(2)}) async-start(bf16[16,8,640]{2,1,0:T(8,128)(2,1)} %shard_map.157), calls=%async_computation | async-start | bytes 327680 | tf_op jit(solution)/shard_map/all_to_all | solution.py:385
  15.6 6.1 %all-to-all-done = bf16[16,8,640]{2,1,0:T(8,128)(2,1)S(1)} async-done(((bf16[16,8,640]{2,1,0:T(8,128)(2,1)}), bf16[16,8,640]{2,1,0:T(8,128)(2,1)S(1)}, u32[]{:S(2)}, u32[]{:S(2)}) %all-to-all-start) | async-done | bytes 163872 | tf_op jit(solution)/shard_map/all_to_all | solution.py:385
  21.7 1.3 %collective-permute-start.3 = (bf16[128,640]{1,0:T(8,128)(2,1)S(1)}, bf16[128,640]{1,0:T(8,128)(2,1)S(1)}, u32[]{:S(2)}, u32[]{:S(2)}) collective-permute-start(bf16[128,640]{1,0:T(8,128)(2,1)S(1)} %bitcast.11), channel_id=1, source_target_pairs={{0,16},{16,32},{32,48},{48,0},{2,18},{18,34},{34,50},{50,2},{4,20}... | collective-permute-start | bytes 491528 | tf_op jit(solution)/shard_map/ppermute | solution.py:53
  23.0 2.6 %collective-permute-start.4 = (bf16[128,640]{1,0:T(8,128)(2,1)S(1)}, bf16[128,640]{1,0:T(8,128)(2,1)S(1)}, u32[]{:S(2)}, u32[]{:S(2)}) collective-permute-start(bf16[128,640]{1,0:T(8,128)(2,1)S(1)} %bitcast.12), channel_id=1, source_target_pairs={{0,32},{16,48},{32,0},{48,16},{2,34},{18,50},{34,2},{50,18},{4,36}... | collective-permute-start | bytes 491528 | tf_op jit(solution)/shard_map/ppermute | solution.py:53
  27.4 2.9 %collective-permute-done.4 = bf16[128,640]{1,0:T(8,128)(2,1)S(1)} collective-permute-done((bf16[128,640]{1,0:T(8,128)(2,1)S(1)}, bf16[128,640]{1,0:T(8,128)(2,1)S(1)}, u32[]{:S(2)}, u32[]{:S(2)}) %collective-permute-start.4) | collective-permute-done | bytes 163872 | tf_op jit(solution)/shard_map/ppermute | solution.py:53
  31.6 1.6 %collective-permute-start.7 = (bf16[512,640]{1,0:T(8,128)(2,1)S(1)}, bf16[512,640]{1,0:T(8,128)(2,1)S(1)}, u32[]{:S(2)}, u32[]{:S(2)}) collective-permute-start(bf16[512,640]{1,0:T(8,128)(2,1)S(1)} %constant_dynamic-update-slice_fusion.near.plane), channel_id=1, source_target_pairs={{0,192},{64,0},{128,64},{192,128},{2,194},{66,2},{130,66},{194,130... | collective-permute-start | bytes 1966088 | tf_op jit(solution)/shard_map/ppermute | solution.py:53
  33.4 1.4 %collective-permute-start = (bf16[128,2048]{1,0:T(8,128)(2,1)S(1)}, bf16[128,2048]{1,0:T(8,128)(2,1)S(1)}, u32[]{:S(2)}, u32[]{:S(2)}) collective-permute-start(bf16[128,2048]{1,0:T(8,128)(2,1)S(1)} %copy-done), channel_id=1, source_target_pairs={{0,1},{1,0},{2,3},{3,2},{4,5},{5,4},{6,7},{7,6},{8,9},{9,8},{10,11... | collective-permute-start | bytes 1572872 | tf_op jit(solution)/shard_map/ppermute | solution.py:53
  35.0 6.4 %collective-permute-done.6.right = bf16[512,640]{1,0:T(8,128)(2,1)S(1)} collective-permute-done((bf16[512,640]{1,0:T(8,128)(2,1)S(1)}, bf16[512,640]{1,0:T(8,128)(2,1)S(1)}, u32[]{:S(2)}, u32[]{:S(2)}) %collective-permute-start.6) | collective-permute-done | bytes 655392 | tf_op jit(solution)/shard_map/ppermute | solution.py:53
  41.6 2.7 %collective-permute-start.9 = (bf16[256,640]{1,0:T(8,128)(2,1)S(1)}, bf16[256,640]{1,0:T(8,128)(2,1)S(1)}, u32[]{:S(2)}, u32[]{:S(2)}) collective-permute-start(bf16[256,640]{1,0:T(8,128)(2,1)S(1)} %slice.78), channel_id=1, source_target_pairs={{0,192},{64,0},{128,64},{192,128},{2,194},{66,2},{130,66},{194,130... | collective-permute-start | bytes 983048 | tf_op jit(solution)/shard_map/ppermute | solution.py:53
  44.4 2.5 %collective-permute-start.10 = (bf16[128,512]{1,0:T(8,128)(2,1)S(1)}, bf16[128,512]{1,0:T(8,128)(2,1)S(1)}, u32[]{:S(2)}, u32[]{:S(2)}) collective-permute-start(bf16[128,512]{1,0:T(8,128)(2,1)S(1)} %get-tuple-element.43), channel_id=1, source_target_pairs={{0,1},{1,0},{2,3},{3,2},{4,5},{5,4},{6,7},{7,6},{8,9},{9,8},{10,11... | collective-permute-start | bytes 393224 | tf_op jit(solution)/shard_map/ppermute | solution.py:53
  49.0 5.1 %shard_map.160.down = bf16[256,640]{1,0:T(8,128)(2,1)S(1)} custom-call(s32[2]{0:T(128)S(1)} %pad_add_fusion.members, bf16[256,512]{1,0:T(8,128)(2,1)S(1)} %get-tuple-element.25.scaled2, f32[256,640]{1,0:T(8,128)S(1)} %shard_map.159.partial, bf16[256,640]{1,0:T(8,128)(2,1)S(1)} %collective-permute-done.8.far_a, ...), custom_call_target="tpu_custom_call" | custom-call | tf_op jit(solution)/shard_map/pallas_call | solution.py:317
  54.1 1.4 %collective-permute-start.11 = (bf16[256,640]{1,0:T(8,128)(2,1)S(1)}, bf16[256,640]{1,0:T(8,128)(2,1)S(1)}, u32[]{:S(2)}, u32[]{:S(2)}) collective-permute-start(bf16[256,640]{1,0:T(8,128)(2,1)S(1)} %shard_map.160.down), channel_id=1, source_target_pairs={{0,64},{64,128},{128,192},{192,0},{2,66},{66,130},{130,194},{194,2... | collective-permute-start | bytes 983048 | tf_op jit(solution)/shard_map/ppermute | solution.py:53
  55.5 1.5 %collective-permute-start.13 = (bf16[256,640]{1,0:T(8,128)(2,1)S(1)}, bf16[256,640]{1,0:T(8,128)(2,1)S(1)}, u32[]{:S(2)}, u32[]{:S(2)}) collective-permute-start(bf16[256,640]{1,0:T(8,128)(2,1)S(1)} %shard_map.160.down), channel_id=1, source_target_pairs={{0,192},{64,0},{128,64},{192,128},{2,194},{66,2},{130,66},{194,130... | collective-permute-start | bytes 983048 | tf_op jit(solution)/shard_map/ppermute | solution.py:53
  57.0 1.4 %collective-permute-start.15 = (bf16[256,512]{1,0:T(8,128)(2,1)S(1)}, bf16[256,512]{1,0:T(8,128)(2,1)S(1)}, u32[]{:S(2)}, u32[]{:S(2)}) collective-permute-start(bf16[256,512]{1,0:T(8,128)(2,1)S(1)} %get-tuple-element.27.scaled1), channel_id=1, source_target_pairs={{0,192},{64,0},{128,64},{192,128},{2,194},{66,2},{130,66},{194,130... | collective-permute-start | bytes 786440 | tf_op jit(solution)/shard_map/ppermute | solution.py:53
  59.6 2.1 %collective-permute-done.11.down3 = bf16[256,640]{1,0:T(8,128)(2,1)S(1)} collective-permute-done((bf16[256,640]{1,0:T(8,128)(2,1)S(1)}, bf16[256,640]{1,0:T(8,128)(2,1)S(1)}, u32[]{:S(2)}, u32[]{:S(2)}) %collective-permute-start.11) | collective-permute-done | bytes 327712 | tf_op jit(solution)/shard_map/ppermute | solution.py:53
  61.8 2.7 %collective-permute-start.14 = (bf16[128,640]{1,0:T(8,128)(2,1)S(1)}, bf16[128,640]{1,0:T(8,128)(2,1)S(1)}, u32[]{:S(2)}, u32[]{:S(2)}) collective-permute-start(bf16[128,640]{1,0:T(8,128)(2,1)S(1)} %slice.92), channel_id=1, source_target_pairs={{0,192},{64,0},{128,64},{192,128},{2,194},{66,2},{130,66},{194,130... | collective-permute-start | bytes 491528 | tf_op jit(solution)/shard_map/ppermute | solution.py:53
  66.2 2.0 %collective-permute-done.2.scaled = bf16[256,512]{1,0:T(8,128)(2,1)S(1)} collective-permute-done((bf16[256,512]{1,0:T(8,128)(2,1)S(1)}, bf16[256,512]{1,0:T(8,128)(2,1)S(1)}, u32[]{:S(2)}, u32[]{:S(2)}) %collective-permute-start.2) | collective-permute-done | bytes 262176 | tf_op jit(solution)/shard_map/ppermute | solution.py:53
  68.2 2.0 %collective-permute-done.12.down_a = bf16[128,640]{1,0:T(8,128)(2,1)S(1)} collective-permute-done((bf16[128,640]{1,0:T(8,128)(2,1)S(1)}, bf16[128,640]{1,0:T(8,128)(2,1)S(1)}, u32[]{:S(2)}, u32[]{:S(2)}) %collective-permute-start.12) | collective-permute-done | bytes 163872 | tf_op jit(solution)/shard_map/ppermute | solution.py:53
  70.2 1.4 %shard_map.163 = (f32[128,640]{1,0:T(8,128)S(1)}, bf16[128,640]{1,0:T(8,128)(2,1)S(1)}, bf16[128,640]{1,0:T(8,128)(2,1)S(1)}, bf16[128,640]{1,0:T(8,128)(2,1)S(1)}) custom-call(s32[16]{0:T(128)S(1)} %fusion.4.tile_of, bf16[256,512]{1,0:T(8,128)(2,1)S(1)} %collective-permute-done.2.scaled, bf16[128,640]{1,0:T(8,128)(2,1)S(1)} %collective-permute-done.12.down_a, ...), custom_call_target="tpu_custom_call" | custom-call | tf_op jit(solution)/shard_map/pallas_call | solution.py:317
  71.7 1.6 %collective-permute-start.17 = (bf16[128,640]{1,0:T(8,128)(2,1)S(1)}, bf16[128,640]{1,0:T(8,128)(2,1)S(1)}, u32[]{:S(2)}, u32[]{:S(2)}) collective-permute-start(bf16[128,640]{1,0:T(8,128)(2,1)S(1)} %get-tuple-element.38), channel_id=1, source_target_pairs={{0,32},{16,48},{32,0},{48,16},{2,34},{18,50},{34,2},{50,18},{4,36}... | collective-permute-start | bytes 491528 | tf_op jit(solution)/shard_map/ppermute | solution.py:53
  74.8 2.9 %collective-permute-done.17 = bf16[128,640]{1,0:T(8,128)(2,1)S(1)} collective-permute-done((bf16[128,640]{1,0:T(8,128)(2,1)S(1)}, bf16[128,640]{1,0:T(8,128)(2,1)S(1)}, u32[]{:S(2)}, u32[]{:S(2)}) %collective-permute-start.17) | collective-permute-done | bytes 163872 | tf_op jit(solution)/shard_map/ppermute | solution.py:53
  79.9 19.5 %all_to_all.15.pieces = bf16[16,8,640]{2,1,0:T(8,128)(2,1)S(1)} all-to-all(bf16[16,8,640]{2,1,0:T(8,128)(2,1)S(1)} %fusion), channel_id=1, replica_groups={{0,1,2,3,4,5,6,7,8,9,10,11,12,13,14,15},{16,17,18,19,20,21,22,23,24,25,..., dimensions={0} | all-to-all | bytes 327680 | tf_op jit(solution)/shard_map/all_to_all | solution.py:458
  99.7 18.3 %all_to_all.16 = f32[256,1,128]{2,1,0:T(1,128)S(1)} all-to-all(f32[256,1,128]{2,1,0:T(1,128)S(1)} %broadcast_in_dim.17), channel_id=1, replica_groups=mesh['fsdp'=256] {'fsdp'}, dimensions={0} | all-to-all | bytes 262144 | tf_op jit(solution)/shard_map/all_to_all | solution.py:469
  118.0 1.6 %shard_map.165 = (f32[8,1152]{1,0:T(8,128)}, f32[4,2048]{1,0:T(4,128)}, f32[4,1152]{1,0:T(4,128)}) custom-call(f32[256,128]{1,0:T(8,128)S(1)} %bitcast.8, f32[8,1152]{1,0:T(8,128)S(1)} %get-tuple-element.42.grad_rows, f32[8,1152]{1,0:T(8,128)S(1)} %copy-done.1, f32[8,1152]{1,0:T(8,128)S(1)} %copy-done.2, f32[4,2048]{1,0:T(4,128)S(1)} %copy-done.3, ...), custom_call_target="tpu_custom_call" | custom-call | tf_op jit(solution)/shard_map/pallas_call | solution.py:317
  (87 shorter events, 16.4 us)
Async XLA Ops:
  2.2 19.5 %all-to-all-start = ((bf16[16,8,640]{2,1,0:T(8,128)(2,1)}), bf16[16,8,640]{2,1,0:T(8,128)(2,1)S(1)}, u32[]{:S(2)}, u32[]{:S(2)}) async-start(bf16[16,8,640]{2,1,0:T(8,128)(2,1)} %shard_map.157), calls=%async_computation | async-start | bytes 327680 | tf_op jit(solution)/shard_map/all_to_all | solution.py:385
  12.8 1.6 %collective-permute-start.1 = (f32[8,128]{1,0:T(8,128)S(1)}, f32[8,128]{1,0:T(8,128)S(1)}, u32[]{:S(2)}, u32[]{:S(2)}) collective-permute-start(f32[8,128]{1,0:T(8,128)S(1)} %broadcast_in_dim.14), channel_id=1, source_target_pairs={{0,1},{1,0},{2,3},{3,2},{4,5},{5,4},{6,7},{7,6},{8,9},{9,8},{10,11... | collective-permute-start | bytes 12296 | tf_op jit(solution)/shard_map/ppermute | solution.py:53
  21.7 5.7 %collective-permute-start.3 = (bf16[128,640]{1,0:T(8,128)(2,1)S(1)}, bf16[128,640]{1,0:T(8,128)(2,1)S(1)}, u32[]{:S(2)}, u32[]{:S(2)}) collective-permute-start(bf16[128,640]{1,0:T(8,128)(2,1)S(1)} %bitcast.11), channel_id=1, source_target_pairs={{0,16},{16,32},{32,48},{48,0},{2,18},{18,34},{34,50},{50,2},{4,20}... | collective-permute-start | bytes 491528 | tf_op jit(solution)/shard_map/ppermute | solution.py:53
  23.0 7.3 %collective-permute-start.4 = (bf16[128,640]{1,0:T(8,128)(2,1)S(1)}, bf16[128,640]{1,0:T(8,128)(2,1)S(1)}, u32[]{:S(2)}, u32[]{:S(2)}) collective-permute-start(bf16[128,640]{1,0:T(8,128)(2,1)S(1)} %bitcast.12), channel_id=1, source_target_pairs={{0,32},{16,48},{32,0},{48,16},{2,34},{18,50},{34,2},{50,18},{4,36}... | collective-permute-start | bytes 491528 | tf_op jit(solution)/shard_map/ppermute | solution.py:53
  25.7 4.7 %collective-permute-start.5 = (bf16[128,640]{1,0:T(8,128)(2,1)S(1)}, bf16[128,640]{1,0:T(8,128)(2,1)S(1)}, u32[]{:S(2)}, u32[]{:S(2)}) collective-permute-start(bf16[128,640]{1,0:T(8,128)(2,1)S(1)} %bitcast.14), channel_id=1, source_target_pairs={{0,48},{16,0},{32,16},{48,32},{2,50},{18,2},{34,18},{50,34},{4,52}... | collective-permute-start | bytes 491528 | tf_op jit(solution)/shard_map/ppermute | solution.py:53
  30.4 11.0 %collective-permute-start.6 = (bf16[512,640]{1,0:T(8,128)(2,1)S(1)}, bf16[512,640]{1,0:T(8,128)(2,1)S(1)}, u32[]{:S(2)}, u32[]{:S(2)}) collective-permute-start(bf16[512,640]{1,0:T(8,128)(2,1)S(1)} %constant_dynamic-update-slice_fusion.near.plane), channel_id=1, source_target_pairs={{0,64},{64,128},{128,192},{192,0},{2,66},{66,130},{130,194},{194,2... | collective-permute-start | bytes 1966088 | tf_op jit(solution)/shard_map/ppermute | solution.py:53
  31.6 10.0 %collective-permute-start.7 = (bf16[512,640]{1,0:T(8,128)(2,1)S(1)}, bf16[512,640]{1,0:T(8,128)(2,1)S(1)}, u32[]{:S(2)}, u32[]{:S(2)}) collective-permute-start(bf16[512,640]{1,0:T(8,128)(2,1)S(1)} %constant_dynamic-update-slice_fusion.near.plane), channel_id=1, source_target_pairs={{0,192},{64,0},{128,64},{192,128},{2,194},{66,2},{130,66},{194,130... | collective-permute-start | bytes 1966088 | tf_op jit(solution)/shard_map/ppermute | solution.py:53
  33.4 13.7 %collective-permute-start = (bf16[128,2048]{1,0:T(8,128)(2,1)S(1)}, bf16[128,2048]{1,0:T(8,128)(2,1)S(1)}, u32[]{:S(2)}, u32[]{:S(2)}) collective-permute-start(bf16[128,2048]{1,0:T(8,128)(2,1)S(1)} %copy-done), channel_id=1, source_target_pairs={{0,1},{1,0},{2,3},{3,2},{4,5},{5,4},{6,7},{7,6},{8,9},{9,8},{10,11... | collective-permute-start | bytes 1572872 | tf_op jit(solution)/shard_map/ppermute | solution.py:53
  41.4 7.6 %collective-permute-start.8 = (bf16[256,640]{1,0:T(8,128)(2,1)S(1)}, bf16[256,640]{1,0:T(8,128)(2,1)S(1)}, u32[]{:S(2)}, u32[]{:S(2)}) collective-permute-start(bf16[256,640]{1,0:T(8,128)(2,1)S(1)} %slice.77), channel_id=1, source_target_pairs={{0,64},{64,128},{128,192},{192,0},{2,66},{66,130},{130,194},{194,2... | collective-permute-start | bytes 983048 | tf_op jit(solution)/shard_map/ppermute | solution.py:53
  41.6 7.4 %collective-permute-start.9 = (bf16[256,640]{1,0:T(8,128)(2,1)S(1)}, bf16[256,640]{1,0:T(8,128)(2,1)S(1)}, u32[]{:S(2)}, u32[]{:S(2)}) collective-permute-start(bf16[256,640]{1,0:T(8,128)(2,1)S(1)} %slice.78), channel_id=1, source_target_pairs={{0,192},{64,0},{128,64},{192,128},{2,194},{66,2},{130,66},{194,130... | collective-permute-start | bytes 983048 | tf_op jit(solution)/shard_map/ppermute | solution.py:53
  44.4 4.6 %collective-permute-start.10 = (bf16[128,512]{1,0:T(8,128)(2,1)S(1)}, bf16[128,512]{1,0:T(8,128)(2,1)S(1)}, u32[]{:S(2)}, u32[]{:S(2)}) collective-permute-start(bf16[128,512]{1,0:T(8,128)(2,1)S(1)} %get-tuple-element.43), channel_id=1, source_target_pairs={{0,1},{1,0},{2,3},{3,2},{4,5},{5,4},{6,7},{7,6},{8,9},{9,8},{10,11... | collective-permute-start | bytes 393224 | tf_op jit(solution)/shard_map/ppermute | solution.py:53
  54.1 7.6 %collective-permute-start.11 = (bf16[256,640]{1,0:T(8,128)(2,1)S(1)}, bf16[256,640]{1,0:T(8,128)(2,1)S(1)}, u32[]{:S(2)}, u32[]{:S(2)}) collective-permute-start(bf16[256,640]{1,0:T(8,128)(2,1)S(1)} %shard_map.160.down), channel_id=1, source_target_pairs={{0,64},{64,128},{128,192},{192,0},{2,66},{66,130},{130,194},{194,2... | collective-permute-start | bytes 983048 | tf_op jit(solution)/shard_map/ppermute | solution.py:53
  55.5 6.2 %collective-permute-start.13 = (bf16[256,640]{1,0:T(8,128)(2,1)S(1)}, bf16[256,640]{1,0:T(8,128)(2,1)S(1)}, u32[]{:S(2)}, u32[]{:S(2)}) collective-permute-start(bf16[256,640]{1,0:T(8,128)(2,1)S(1)} %shard_map.160.down), channel_id=1, source_target_pairs={{0,192},{64,0},{128,64},{192,128},{2,194},{66,2},{130,66},{194,130... | collective-permute-start | bytes 983048 | tf_op jit(solution)/shard_map/ppermute | solution.py:53
  57.0 8.2 %collective-permute-start.15 = (bf16[256,512]{1,0:T(8,128)(2,1)S(1)}, bf16[256,512]{1,0:T(8,128)(2,1)S(1)}, u32[]{:S(2)}, u32[]{:S(2)}) collective-permute-start(bf16[256,512]{1,0:T(8,128)(2,1)S(1)} %get-tuple-element.27.scaled1), channel_id=1, source_target_pairs={{0,192},{64,0},{128,64},{192,128},{2,194},{66,2},{130,66},{194,130... | collective-permute-start | bytes 786440 | tf_op jit(solution)/shard_map/ppermute | solution.py:53
  58.4 6.8 %collective-permute-start.16 = (bf16[256,512]{1,0:T(8,128)(2,1)S(1)}, bf16[256,512]{1,0:T(8,128)(2,1)S(1)}, u32[]{:S(2)}, u32[]{:S(2)}) collective-permute-start(bf16[256,512]{1,0:T(8,128)(2,1)S(1)} %get-tuple-element.28.scaled3), channel_id=1, source_target_pairs={{0,64},{64,128},{128,192},{192,0},{2,66},{66,130},{130,194},{194,2... | collective-permute-start | bytes 786440 | tf_op jit(solution)/shard_map/ppermute | solution.py:53
  58.4 9.8 %collective-permute-start.2 = (bf16[256,512]{1,0:T(8,128)(2,1)S(1)}, bf16[256,512]{1,0:T(8,128)(2,1)S(1)}, u32[]{:S(2)}, u32[]{:S(2)}) collective-permute-start(bf16[256,512]{1,0:T(8,128)(2,1)S(1)} %get-tuple-element.25.scaled2), channel_id=1, source_target_pairs={{0,128},{64,192},{128,0},{192,64},{2,130},{66,194},{130,2},{194,66... | collective-permute-start | bytes 786440 | tf_op jit(solution)/shard_map/ppermute | solution.py:53
  61.7 8.5 %collective-permute-start.12 = (bf16[128,640]{1,0:T(8,128)(2,1)S(1)}, bf16[128,640]{1,0:T(8,128)(2,1)S(1)}, u32[]{:S(2)}, u32[]{:S(2)}) collective-permute-start(bf16[128,640]{1,0:T(8,128)(2,1)S(1)} %slice.91), channel_id=1, source_target_pairs={{0,64},{64,128},{128,192},{192,0},{2,66},{66,130},{130,194},{194,2... | collective-permute-start | bytes 491528 | tf_op jit(solution)/shard_map/ppermute | solution.py:53
  61.8 8.4 %collective-permute-start.14 = (bf16[128,640]{1,0:T(8,128)(2,1)S(1)}, bf16[128,640]{1,0:T(8,128)(2,1)S(1)}, u32[]{:S(2)}, u32[]{:S(2)}) collective-permute-start(bf16[128,640]{1,0:T(8,128)(2,1)S(1)} %slice.92), channel_id=1, source_target_pairs={{0,192},{64,0},{128,64},{192,128},{2,194},{66,2},{130,66},{194,130... | collective-permute-start | bytes 491528 | tf_op jit(solution)/shard_map/ppermute | solution.py:53
  71.6 46.3 %copy-start.1 = (f32[8,1152]{1,0:T(8,128)S(1)}, f32[8,1152]{1,0:T(8,128)}, u32[]{:S(2)}) copy-start(f32[8,1152]{1,0:T(8,128)} %weight_first.1) | copy-start | bytes 110596
  71.7 46.3 %copy-start.2 = (f32[8,1152]{1,0:T(8,128)S(1)}, f32[8,1152]{1,0:T(8,128)}, u32[]{:S(2)}) copy-start(f32[8,1152]{1,0:T(8,128)} %weight_second.1) | copy-start | bytes 110596
  71.7 46.3 %copy-start.3 = (f32[4,2048]{1,0:T(4,128)S(1)}, f32[4,2048]{1,0:T(4,128)}, u32[]{:S(2)}) copy-start(f32[4,2048]{1,0:T(4,128)} %in_first.1) | copy-start | bytes 98308
  71.7 6.0 %collective-permute-start.17 = (bf16[128,640]{1,0:T(8,128)(2,1)S(1)}, bf16[128,640]{1,0:T(8,128)(2,1)S(1)}, u32[]{:S(2)}, u32[]{:S(2)}) collective-permute-start(bf16[128,640]{1,0:T(8,128)(2,1)S(1)} %get-tuple-element.38), channel_id=1, source_target_pairs={{0,32},{16,48},{32,0},{48,16},{2,34},{18,50},{34,2},{50,18},{4,36}... | collective-permute-start | bytes 491528 | tf_op jit(solution)/shard_map/ppermute | solution.py:53
  73.4 5.6 %collective-permute-start.18 = (bf16[128,640]{1,0:T(8,128)(2,1)S(1)}, bf16[128,640]{1,0:T(8,128)(2,1)S(1)}, u32[]{:S(2)}, u32[]{:S(2)}) collective-permute-start(bf16[128,640]{1,0:T(8,128)(2,1)S(1)} %get-tuple-element.39), channel_id=1, source_target_pairs={{0,48},{16,0},{32,16},{48,32},{2,50},{18,2},{34,18},{50,34},{4,52}... | collective-permute-start | bytes 491528 | tf_op jit(solution)/shard_map/ppermute | solution.py:53
  74.4 5.4 %collective-permute-start.19 = (bf16[128,640]{1,0:T(8,128)(2,1)S(1)}, bf16[128,640]{1,0:T(8,128)(2,1)S(1)}, u32[]{:S(2)}, u32[]{:S(2)}) collective-permute-start(bf16[128,640]{1,0:T(8,128)(2,1)S(1)} %get-tuple-element.40), channel_id=1, source_target_pairs={{0,16},{16,32},{32,48},{48,0},{2,18},{18,34},{34,50},{50,2},{4,20}... | collective-permute-start | bytes 491528 | tf_op jit(solution)/shard_map/ppermute | solution.py:53
  (10 other events, 289.6 us)
where the time goes:
time: 120 us
  blocking collectives  37.7 us (31%)
  starting transfers between devices  36.1 us (30%)
  waiting for transfers between devices  27 us (22%)
  Pallas kernels  12.6 us (10%)
  local copies, waits for them, and re-layouts  2.73 us (2%)
  between operations  2.33 us (2%)
    ppermute x20, starting transfers between devices, shift(): return lax.ppermute(array, AXIS, pairs)  26.1 us
    ppermute x20, waiting for transfers between devices, shift(): return lax.ppermute(array, AXIS, pairs)  20.9 us
    all_to_all x1, blocking collectives, per_device(): lax.all_to_all(column_sum.astype(bf16).reshape(2 * NZ, 8, LANES), AXIS, s...  19.5 us
    all_to_all x1, blocking collectives, per_device(): lax.all_to_all(jnp.broadcast_to(packed[:, None], (256, 1, 128)), AXIS, sp...  18.3 us
    pallas_call x9, Pallas kernels, call(): pl.pallas_call(kernel, in_specs=[SMEM] * len(scalars) + [VMEM] * len(arra...  12.6 us
    all_to_all x1, starting transfers between devices, per_device(): lax.all_to_all(spread, AXIS, split_axis=0, concat_axis=0, tiled=True, axi...  9.97 us
    all_to_all x1, waiting for transfers between devices, per_device(): lax.all_to_all(spread, AXIS, split_axis=0, concat_axis=0, tiled=True, axi...  6.07 us
  transfers between devices with their start and end apart: 21, of which 10 were waited for; matrix products, arithmetic and copies ran while one was open for 2% of the time, Pallas kernels for 3%

commit v1 on v0

--- a/solution.py
+++ b/solution.py
@@ -1,3 +1,4 @@
+import functools
 import math
 
 import jax
@@ -92,7 +93,7 @@
 
 
 def attention_kernel(
-    members, scaled2, partial, far_a, far_b, slopes, bias, cosine_ref, sine_ref, cot_own, cot_partner, down
+    part, members, scaled2, partial, far_a, far_b, slopes, bias, cosine_ref, sine_ref, cot, down
 ):
     cosine = cosine_ref[...]
     sine = sine_ref[...]
@@ -100,7 +101,7 @@
     row = lax.broadcasted_iota(jnp.int32, (SEQ, 128), 0)
     low = lane < 64
     first = (lane & 63) < 32
-    causal = row >= lane
+    causal = jnp.concatenate([row >= lane] * 4, axis=0)
     score_scale = 1.0 / math.sqrt(HEAD_DIM)
 
     def swap(tile):
@@ -109,79 +110,67 @@
     def half_turn(tile):
         return pltpu.roll(tile, 64, 1)
 
-    projected = (
-        partial[...]
-        + dot(scaled2[:, :256], far_a[...], 1, 0)
-        + dot(scaled2[:, 256:], far_b[...], 1, 0)
-    )
-    totals = []
-    for part, cot in enumerate((cot_own, cot_partner)):
-        rows = slice(part * SEQ, (part + 1) * SEQ)
-        raw = projected[rows]
-        slope = slopes[part : part + 1, :]
-        biased = raw * slope + bias[...]
-        turned = []
-        for t in range(4):
-            tile = biased[:, t * 128 : (t + 1) * 128]
-            turned.append(tile * cosine + swap(tile) * sine)
-        keys = turned[3]
-        values = biased[:, 512:640]
-        key_pair = jnp.concatenate(
-            [jnp.where(low, half_turn(keys), 0.0), jnp.where(low, 0.0, keys)], axis=0
-        ).astype(bf16)
-        value_pair = jnp.concatenate(
-            [jnp.where(low, values, 0.0), jnp.where(low, 0.0, half_turn(values))], axis=0
-        ).astype(bf16)
-        grads = []
-        key_sum = jnp.zeros((2 * SEQ, 128), f32)
-        value_sum = jnp.zeros((2 * SEQ, 128), f32)
-        for t in range(4):
-            query = turned[t].astype(bf16)
-            upstream = cot[:, t * 128 : (t + 1) * 128]
-            scores = dot(query, key_pair, 1, 1) * score_scale
-            grad_probs = dot(upstream, value_pair, 1, 1)
-            probs_bf, grads_bf = [], []
-            for h in range(2):
-                side = slice(h * SEQ, (h + 1) * SEQ)
-                masked = jnp.where(causal, scores[:, side], -jnp.inf)
-                raised = jnp.exp(masked - jnp.max(masked, axis=1, keepdims=True))
-                probs = raised / jnp.sum(raised, axis=1, keepdims=True)
-                gp = grad_probs[:, side]
-                centre = jnp.sum(gp * probs, axis=1, keepdims=True)
-                probs_bf.append(probs.astype(bf16))
-                grads_bf.append((probs * (gp - centre) * score_scale).astype(bf16))
-            probs_pair = jnp.concatenate(probs_bf, axis=1)
-            grad_pair = jnp.concatenate(grads_bf, axis=1)
-            grads.append(dot(grad_pair, key_pair, 1, 0))
-            key_sum += dot(grad_pair, query, 0, 0)
-            value_sum += dot(probs_pair, upstream, 0, 0)
-        grad_key = jnp.where(low, 0.0, half_turn(key_sum[:SEQ]) + key_sum[SEQ:])
-        grad_value = jnp.where(low, value_sum[:SEQ] + half_turn(value_sum[SEQ:]), 0.0)
-        grads[3] = jnp.where(low, grads[3], grad_key)
-        grads = [g * cosine - swap(g) * sine for g in grads] + [grad_value]
-        grad_biased = jnp.concatenate(grads, axis=1)
-        totals.append(jnp.sum(raw * grad_biased, axis=0, keepdims=True))
-        down[rows, :] = (grad_biased * slope).astype(bf16)
+    rows = slice(part * SEQ, (part + 1) * SEQ)
+    raw = (
+        partial[rows, :]
+        + dot(scaled2[rows, :256], far_a[...], 1, 0)
+        + dot(scaled2[rows, 256:], far_b[...], 1, 0)
+    )
+    slope = slopes[part : part + 1, :]
+    biased = raw * slope + bias[...]
+    turned = []
+    for t in range(4):
+        tile = biased[:, t * 128 : (t + 1) * 128]
+        turned.append(tile * cosine + swap(tile) * sine)
+    keys = turned[3]
+    values = biased[:, 512:640]
+    key_pair = jnp.concatenate(
+        [jnp.where(low, half_turn(keys), 0.0), jnp.where(low, 0.0, keys)], axis=0
+    ).astype(bf16)
+    value_pair = jnp.concatenate(
+        [jnp.where(low, values, 0.0), jnp.where(low, 0.0, half_turn(values))], axis=0
+    ).astype(bf16)
+    query = jnp.concatenate([q.astype(bf16) for q in turned], axis=0)
+    upstream = jnp.concatenate([cot[:, t * 128 : (t + 1) * 128] for t in range(4)], axis=0)
+    scores = dot(query, key_pair, 1, 1)
+    grad_probs = dot(upstream, value_pair, 1, 1)
+    probs_bf, grads_bf = [], []
+    for h in range(2):
+        side = slice(h * SEQ, (h + 1) * SEQ)
+        masked = jnp.where(causal, scores[:, side] * score_scale, -jnp.inf)
+        raised = jnp.exp(masked - jnp.max(masked, axis=1, keepdims=True))
+        probs = raised * (1.0 / jnp.sum(raised, axis=1, keepdims=True))
+        gp = grad_probs[:, side]
+        centre = jnp.sum(gp * probs, axis=1, keepdims=True)
+        probs_bf.append(probs.astype(bf16))
+        grads_bf.append((probs * (gp - centre) * score_scale).astype(bf16))
+    probs_pair = jnp.concatenate(probs_bf, axis=1)
+    grad_pair = jnp.concatenate(grads_bf, axis=1)
+    all_grads = dot(grad_pair, key_pair, 1, 0)
+    key_sum = dot(grad_pair, query, 0, 0)
+    value_sum = dot(probs_pair, upstream, 0, 0)
+    grad_key = jnp.where(low, 0.0, half_turn(key_sum[:SEQ]) + key_sum[SEQ:])
+    grad_value = jnp.where(low, value_sum[:SEQ] + half_turn(value_sum[SEQ:]), 0.0)
+    grads = [all_grads[t * SEQ : (t + 1) * SEQ] for t in range(4)]
+    grads[3] = jnp.where(low, grads[3], grad_key)
+    grads = [g * cosine - swap(g) * sine for g in grads] + [grad_value]
+    grad_biased = jnp.concatenate(grads, axis=1)
+    total = jnp.sum(raw * grad_biased, axis=0, keepdims=True)
+    member = members[part]
     spread = jnp.zeros((SEQ, 128), f32)
-    for part in range(2):
-        for t in range(5):
-            spread += jnp.where(
-                row == 64 + 4 * t + members[part], totals[part][:, t * 128 : (t + 1) * 128], 0.0
-            )
+    for t in range(5):
+        spread += jnp.where(row == 64 + 4 * t + member, total[:, t * 128 : (t + 1) * 128], 0.0)
     spread = spread.T
     high = spread.astype(bf16).astype(f32)
     spread = high + pltpu.roll(spread - high, 20, 1)
-    for part in range(2):
-        rows = slice(part * SEQ, (part + 1) * SEQ)
-        tail = jnp.where(lane == 127, members[part].astype(f32), 0.0)
-        if part == 0:
-            tail = jnp.where(lane == 127, tail, spread)
-        last = down[rows, 512:640].astype(f32)
-        down[rows, 512:640] = jnp.where(low, last, tail).astype(bf16)
+    tail = jnp.where(lane == 127, member.astype(f32), spread)
+    grad_down = grad_biased * slope
+    down[:, :512] = grad_down[:, :512].astype(bf16)
+    down[:, 512:] = jnp.where(low, grad_down[:, 512:], tail).astype(bf16)
 
 
 def weight_terms(scaled, down, plane, carry):
-    grads, totals, tails = carry
+    grads, totals = carry
     back = dot(down, plane, 1, 1)
     grads = grads + dot(scaled, down, 0, 0)
     row = lax.broadcasted_iota(jnp.int32, (8, 512), 0)
@@ -190,33 +179,38 @@
         member = down[part * SEQ : part * SEQ + 1, 639:640].astype(f32).astype(jnp.int32)
         total = jnp.sum(scaled[rows].astype(f32) * back[rows], axis=0, keepdims=True)
         totals = totals + jnp.where(row == member, total, 0.0)
-    return grads, totals, tails
-
-
-def near_kernel(scaled, down, plane, grads, totals, tails):
-    zero = (jnp.zeros((512, LANES), f32), jnp.zeros((8, 512), f32), None)
-    total = weight_terms(scaled[...], down[...], plane[...], zero)
-    grads[...], totals[...] = total[:2]
-    tails[...] = down[:SEQ, 512:].astype(f32)
+    return grads, totals
+
+
+def joined(first, second):
+    return jnp.concatenate([first[...], second[...]], axis=0)
+
+
+def tail_sum(*downs):
+    return sum(down[:, 512:].astype(f32) for down in downs)
+
+
+def near_kernel(scaled, down0, down1, plane, grads, totals, tails):
+    zero = (jnp.zeros((512, LANES), f32), jnp.zeros((8, 512), f32))
+    grads[...], totals[...] = weight_terms(scaled[...], joined(down0, down1), plane[...], zero)
+    tails[...] = tail_sum(down0, down1)
 
 
 def middle_kernel(
-    scaled1, down1, scaled3, down3, plane, grads_in, totals_in, tails_in, grads, totals, tails
+    scaled1, ahead0, ahead1, scaled3, back0, back1, plane, grads_in, totals_in, tails_in, grads, totals, tails
 ):
-    total = (grads_in[...], totals_in[...], None)
-    for scaled, down in ((scaled1, down1), (scaled3, down3)):
-        total = weight_terms(scaled[...], down[...], plane[...], total)
-    grads[...], totals[...] = total[:2]
-    tails[...] = tails_in[...] + down1[:SEQ, 512:].astype(f32) + down3[:SEQ, 512:].astype(f32)
+    total = (grads_in[...], totals_in[...])
+    total = weight_terms(scaled1[...], joined(ahead0, ahead1), plane[...], total)
+    grads[...], totals[...] = weight_terms(scaled3[...], joined(back0, back1), plane[...], total)
+    tails[...] = tails_in[...] + tail_sum(ahead0, ahead1, back0, back1)
 
 
 def last_kernel(
     tile_of, scaled, down_a, down_b, plane, grads_in, totals_in, tails_in, rates, part0, part1, part2, part3
 ):
-    total = (grads_in[...], totals_in[...], None)
-    total = weight_terms(scaled[:SEQ, :], down_a[...], plane[...], total)
-    grads, totals, _ = weight_terms(scaled[SEQ:, :], down_b[...], plane[...], total)
-    tails = tails_in[...] + down_a[:, 512:].astype(f32)
+    total = (grads_in[...], totals_in[...])
+    grads, totals = weight_terms(scaled[...], joined(down_a, down_b), plane[...], total)
+    tails = tails_in[...] + tail_sum(down_a, down_b)
     tails = tails + pltpu.roll(tails, 108, 1)
     lane = lax.broadcasted_iota(jnp.int32, (SEQ, 128), 1)
     for i, result in enumerate((part0, part1, part2, part3)):
@@ -430,23 +424,27 @@
         jax.ShapeDtypeStruct((2 * SEQ, LANES), f32),
     )
     far_scaled = [shift(scaled[j], OUTER_RINGS, -j) for j in (1, 2, 3)]
-    down = call(
-        attention_kernel,
-        [members],
-        [scaled[2], partial, far_a, far_b, slopes, bias, cosine, sine, cot_own, cot_partner],
-        jax.ShapeDtypeStruct((2 * SEQ, LANES), bf16),
-    )
-    down_back = shift(down, OUTER_RINGS, 1)
-    down_ahead = shift(down, OUTER_RINGS, -1)
+    downs, backs, aheads = [], [], []
+    for part, cot in enumerate((cot_own, cot_partner)):
+        downs.append(
+            call(
+                functools.partial(attention_kernel, part),
+                [members],
+                [scaled[2], partial, far_a, far_b, slopes, bias, cosine, sine, cot],
+                jax.ShapeDtypeStruct((SEQ, LANES), bf16),
+            )
+        )
+        backs.append(shift(downs[part], OUTER_RINGS, 1))
+        aheads.append(shift(downs[part], OUTER_RINGS, -1))
     sums = [
         jax.ShapeDtypeStruct((512, LANES), f32),
         jax.ShapeDtypeStruct((8, 512), f32),
         jax.ShapeDtypeStruct((SEQ, 128), f32),
     ]
-    near = call(near_kernel, [], [scaled[0], down, plane], sums)
-    down_far_a = shift(down_back[:SEQ], OUTER_RINGS, 1)
-    down_far_b = shift(down_ahead[SEQ:], OUTER_RINGS, -1)
-    middle = call(middle_kernel, [], [far_scaled[0], down_ahead, far_scaled[2], down_back, plane, *near], sums)
+    near = call(near_kernel, [], [scaled[0], *downs, plane], sums)
+    down_far_a = shift(backs[0], OUTER_RINGS, 1)
+    down_far_b = shift(aheads[1], OUTER_RINGS, -1)
+    middle = call(middle_kernel, [], [far_scaled[0], *aheads, far_scaled[2], *backs, plane, *near], sums)
     parts = call(
         last_kernel,
         [tile_of],

time: 120 us -> 121 us (level)
  waiting for transfers between devices: 27 us -> 29.6 us
    ppermute x20 -> x22, waiting for transfers between devices: 20.9 us -> 23.5 us  [shift(): return lax.ppermute(array, AXIS, pairs)]
    pallas_call x9 -> x10, Pallas kernels: 12.6 us -> 11.9 us  [call(): pl.pallas_call(kernel, in_specs=[SMEM] * len(scalars) + [VMEM] * len(arra...]
    ppermute x20 -> x22, starting transfers between devices: 26.1 us -> 25.8 us  [shift(): return lax.ppermute(array, AXIS, pairs)]
  transfers between devices with their start and end apart: 21 -> 23, of which waited for: 10 -> 9; matrix products, arithmetic and copies ran while one was open for 2% -> 2% of each run, Pallas kernels for 3% -> 7%
where the time goes in v1:
time: 121 us; the launch traced here: 120 us
  blocking collectives  37.1 us (31%)
  starting transfers between devices  35.8 us (30%)
  waiting for transfers between devices  29.6 us (24%)
  Pallas kernels  11.9 us (10%)
  local copies, waits for them, and re-layouts  2.7 us (2%)
  between operations  2.32 us (2%)
    ppermute x22, starting transfers between devices, shift(): return lax.ppermute(array, AXIS, pairs)  25.8 us
    ppermute x22, waiting for transfers between devices, shift(): return lax.ppermute(array, AXIS, pairs)  23.5 us
    all_to_all x1, blocking collectives, per_device(): lax.all_to_all(column_sum.astype(bf16).reshape(2 * NZ, 8, LANES), AXIS, s...  19.4 us
    all_to_all x1, blocking collectives, per_device(): lax.all_to_all(jnp.broadcast_to(packed[:, None], (256, 1, 128)), AXIS, sp...  17.7 us
    pallas_call x10, Pallas kernels, call(): pl.pallas_call(kernel, in_specs=[SMEM] * len(scalars) + [VMEM] * len(arra...  11.9 us
    all_to_all x1, starting transfers between devices, per_device(): lax.all_to_all(spread, AXIS, split_axis=0, concat_axis=0, tiled=True, axi...  9.97 us
    all_to_all x1, waiting for transfers between devices, per_device(): lax.all_to_all(spread, AXIS, split_axis=0, concat_axis=0, tiled=True, axi...  6.07 us
  transfers between devices with their start and end apart: 23, of which 9 were waited for; matrix products, arithmetic and copies ran while one was open for 2% of the time, Pallas kernels for 7%

profile of v1, /device:TPU:1, one launch (start us, length us, event | category | flops | bytes accessed | tf_op | source)
XLA Modules:
  0.0 120.5 jit_solution(3671223393886203909)
XLA Ops:
  2.2 10.0 %all-to-all-start = ((bf16[16,8,640]{2,1,0:T(8,128)(2,1)}), bf16[16,8,640]{2,1,0:T(8,128)(2,1)S(1)}, u32[]{:S(2)}, u32[]{:S(2)}) async-start(bf16[16,8,640]{2,1,0:T(8,128)(2,1)} %shard_map.157), calls=%async_computation | async-start | bytes 327680 | tf_op jit(solution)/shard_map/all_to_all | solution.py:379
  15.6 6.1 %all-to-all-done = bf16[16,8,640]{2,1,0:T(8,128)(2,1)S(1)} async-done(((bf16[16,8,640]{2,1,0:T(8,128)(2,1)}), bf16[16,8,640]{2,1,0:T(8,128)(2,1)S(1)}, u32[]{:S(2)}, u32[]{:S(2)}) %all-to-all-start) | async-done | bytes 163872 | tf_op jit(solution)/shard_map/all_to_all | solution.py:379
  21.7 1.3 %collective-permute-start.3 = (bf16[128,640]{1,0:T(8,128)(2,1)S(1)}, bf16[128,640]{1,0:T(8,128)(2,1)S(1)}, u32[]{:S(2)}, u32[]{:S(2)}) collective-permute-start(bf16[128,640]{1,0:T(8,128)(2,1)S(1)} %bitcast.11), channel_id=1, source_target_pairs={{0,16},{16,32},{32,48},{48,0},{2,18},{18,34},{34,50},{50,2},{4,20}... | collective-permute-start | bytes 491528 | tf_op jit(solution)/shard_map/ppermute | solution.py:54
  23.0 2.6 %collective-permute-start.4 = (bf16[128,640]{1,0:T(8,128)(2,1)S(1)}, bf16[128,640]{1,0:T(8,128)(2,1)S(1)}, u32[]{:S(2)}, u32[]{:S(2)}) collective-permute-start(bf16[128,640]{1,0:T(8,128)(2,1)S(1)} %bitcast.12), channel_id=1, source_target_pairs={{0,32},{16,48},{32,0},{48,16},{2,34},{18,50},{34,2},{50,18},{4,36}... | collective-permute-start | bytes 491528 | tf_op jit(solution)/shard_map/ppermute | solution.py:54
  27.4 2.9 %collective-permute-done.4 = bf16[128,640]{1,0:T(8,128)(2,1)S(1)} collective-permute-done((bf16[128,640]{1,0:T(8,128)(2,1)S(1)}, bf16[128,640]{1,0:T(8,128)(2,1)S(1)}, u32[]{:S(2)}, u32[]{:S(2)}) %collective-permute-start.4) | collective-permute-done | bytes 163872 | tf_op jit(solution)/shard_map/ppermute | solution.py:54
  31.6 1.6 %collective-permute-start.7 = (bf16[512,640]{1,0:T(8,128)(2,1)S(1)}, bf16[512,640]{1,0:T(8,128)(2,1)S(1)}, u32[]{:S(2)}, u32[]{:S(2)}) collective-permute-start(bf16[512,640]{1,0:T(8,128)(2,1)S(1)} %constant_dynamic-update-slice_fusion.near.plane), channel_id=1, source_target_pairs={{0,192},{64,0},{128,64},{192,128},{2,194},{66,2},{130,66},{194,130... | collective-permute-start | bytes 1966088 | tf_op jit(solution)/shard_map/ppermute | solution.py:54
  33.4 1.4 %collective-permute-start = (bf16[128,2048]{1,0:T(8,128)(2,1)S(1)}, bf16[128,2048]{1,0:T(8,128)(2,1)S(1)}, u32[]{:S(2)}, u32[]{:S(2)}) collective-permute-start(bf16[128,2048]{1,0:T(8,128)(2,1)S(1)} %copy-done), channel_id=1, source_target_pairs={{0,1},{1,0},{2,3},{3,2},{4,5},{5,4},{6,7},{7,6},{8,9},{9,8},{10,11... | collective-permute-start | bytes 1572872 | tf_op jit(solution)/shard_map/ppermute | solution.py:54
  35.0 6.4 %collective-permute-done.6.right = bf16[512,640]{1,0:T(8,128)(2,1)S(1)} collective-permute-done((bf16[512,640]{1,0:T(8,128)(2,1)S(1)}, bf16[512,640]{1,0:T(8,128)(2,1)S(1)}, u32[]{:S(2)}, u32[]{:S(2)}) %collective-permute-start.6) | collective-permute-done | bytes 655392 | tf_op jit(solution)/shard_map/ppermute | solution.py:54
  41.6 2.7 %collective-permute-start.9 = (bf16[256,640]{1,0:T(8,128)(2,1)S(1)}, bf16[256,640]{1,0:T(8,128)(2,1)S(1)}, u32[]{:S(2)}, u32[]{:S(2)}) collective-permute-start(bf16[256,640]{1,0:T(8,128)(2,1)S(1)} %slice.70), channel_id=1, source_target_pairs={{0,192},{64,0},{128,64},{192,128},{2,194},{66,2},{130,66},{194,130... | collective-permute-start | bytes 983048 | tf_op jit(solution)/shard_map/ppermute | solution.py:54
  44.4 2.3 %collective-permute-start.12 = (bf16[128,512]{1,0:T(8,128)(2,1)S(1)}, bf16[128,512]{1,0:T(8,128)(2,1)S(1)}, u32[]{:S(2)}, u32[]{:S(2)}) collective-permute-start(bf16[128,512]{1,0:T(8,128)(2,1)S(1)} %get-tuple-element.43), channel_id=1, source_target_pairs={{0,1},{1,0},{2,3},{3,2},{4,5},{5,4},{6,7},{7,6},{8,9},{9,8},{10,11... | collective-permute-start | bytes 393224 | tf_op jit(solution)/shard_map/ppermute | solution.py:54
  47.9 2.4 %collective-permute-start.15 = (bf16[256,512]{1,0:T(8,128)(2,1)S(1)}, bf16[256,512]{1,0:T(8,128)(2,1)S(1)}, u32[]{:S(2)}, u32[]{:S(2)}) collective-permute-start(bf16[256,512]{1,0:T(8,128)(2,1)S(1)} %get-tuple-element.27.scaled1), channel_id=1, source_target_pairs={{0,192},{64,0},{128,64},{192,128},{2,194},{66,2},{130,66},{194,130... | collective-permute-start | bytes 786440 | tf_op jit(solution)/shard_map/ppermute | solution.py:54
  51.3 2.3 %shard_map.161.down1 = bf16[128,640]{1,0:T(8,128)(2,1)S(1)} custom-call(s32[2]{0:T(128)S(1)} %pad_add_fusion.members, bf16[256,512]{1,0:T(8,128)(2,1)S(1)} %get-tuple-element.25.scaled2, f32[256,640]{1,0:T(8,128)S(1)} %shard_map.159.partial, bf16[256,640]{1,0:T(8,128)(2,1)S(1)} %collective-permute-done.8.far_a, ...), custom_call_target="tpu_custom_call" | custom-call | tf_op jit(solution)/shard_map/pallas_call | solution.py:311
  53.5 2.8 %collective-permute-start.13 = (bf16[128,640]{1,0:T(8,128)(2,1)S(1)}, bf16[128,640]{1,0:T(8,128)(2,1)S(1)}, u32[]{:S(2)}, u32[]{:S(2)}) collective-permute-start(bf16[128,640]{1,0:T(8,128)(2,1)S(1)} %shard_map.161.down1), channel_id=1, source_target_pairs={{0,192},{64,0},{128,64},{192,128},{2,194},{66,2},{130,66},{194,130... | collective-permute-start | bytes 491528 | tf_op jit(solution)/shard_map/ppermute | solution.py:54
  56.3 2.3 %shard_map.160.down0 = bf16[128,640]{1,0:T(8,128)(2,1)S(1)} custom-call(s32[2]{0:T(128)S(1)} %pad_add_fusion.members, bf16[256,512]{1,0:T(8,128)(2,1)S(1)} %get-tuple-element.25.scaled2, f32[256,640]{1,0:T(8,128)S(1)} %shard_map.159.partial, bf16[256,640]{1,0:T(8,128)(2,1)S(1)} %collective-permute-done.8.far_a, ...), custom_call_target="tpu_custom_call" | custom-call | tf_op jit(solution)/shard_map/pallas_call | solution.py:311
  58.7 1.2 collective-permute-start.2
  59.9 2.1 %collective-permute-start.18 = (bf16[128,640]{1,0:T(8,128)(2,1)S(1)}, bf16[128,640]{1,0:T(8,128)(2,1)S(1)}, u32[]{:S(2)}, u32[]{:S(2)}) collective-permute-start(bf16[128,640]{1,0:T(8,128)(2,1)S(1)} %shard_map.161.down1), channel_id=1, source_target_pairs={{0,64},{64,128},{128,192},{192,0},{2,66},{66,130},{130,194},{194,2... | collective-permute-start | bytes 491528 | tf_op jit(solution)/shard_map/ppermute | solution.py:54
  62.8 4.3 %collective-permute-done.10.back0 = bf16[128,640]{1,0:T(8,128)(2,1)S(1)} collective-permute-done((bf16[128,640]{1,0:T(8,128)(2,1)S(1)}, bf16[128,640]{1,0:T(8,128)(2,1)S(1)}, u32[]{:S(2)}, u32[]{:S(2)}) %collective-permute-start.10) | collective-permute-done | bytes 163872 | tf_op jit(solution)/shard_map/ppermute | solution.py:54
  70.0 2.5 %collective-permute-done.11.down_a = bf16[128,640]{1,0:T(8,128)(2,1)S(1)} collective-permute-done((bf16[128,640]{1,0:T(8,128)(2,1)S(1)}, bf16[128,640]{1,0:T(8,128)(2,1)S(1)}, u32[]{:S(2)}, u32[]{:S(2)}) %collective-permute-start.11) | collective-permute-done | bytes 163872 | tf_op jit(solution)/shard_map/ppermute | solution.py:54
  72.5 1.2 shard_map.164
  75.7 4.0 %collective-permute-done.19 = bf16[128,640]{1,0:T(8,128)(2,1)S(1)} collective-permute-done((bf16[128,640]{1,0:T(8,128)(2,1)S(1)}, bf16[128,640]{1,0:T(8,128)(2,1)S(1)}, u32[]{:S(2)}, u32[]{:S(2)}) %collective-permute-start.19) | collective-permute-done | bytes 163872 | tf_op jit(solution)/shard_map/ppermute | solution.py:54
  79.6 1.7 %collective-permute-done.21 = bf16[128,640]{1,0:T(8,128)(2,1)S(1)} collective-permute-done((bf16[128,640]{1,0:T(8,128)(2,1)S(1)}, bf16[128,640]{1,0:T(8,128)(2,1)S(1)}, u32[]{:S(2)}, u32[]{:S(2)}) %collective-permute-start.21) | collective-permute-done | bytes 163872 | tf_op jit(solution)/shard_map/ppermute | solution.py:54
  81.4 19.4 %all_to_all.15.pieces = bf16[16,8,640]{2,1,0:T(8,128)(2,1)S(1)} all-to-all(bf16[16,8,640]{2,1,0:T(8,128)(2,1)S(1)} %fusion), channel_id=1, replica_groups={{0,1,2,3,4,5,6,7,8,9,10,11,12,13,14,15},{16,17,18,19,20,21,22,23,24,25,..., dimensions={0} | all-to-all | bytes 327680 | tf_op jit(solution)/shard_map/all_to_all | solution.py:456
  101.1 17.7 %all_to_all.16 = f32[256,1,128]{2,1,0:T(1,128)S(1)} all-to-all(f32[256,1,128]{2,1,0:T(1,128)S(1)} %broadcast_in_dim.17), channel_id=1, replica_groups=mesh['fsdp'=256] {'fsdp'}, dimensions={0} | all-to-all | bytes 262144 | tf_op jit(solution)/shard_map/all_to_all | solution.py:467
  118.9 1.6 %shard_map.166 = (f32[8,1152]{1,0:T(8,128)}, f32[4,2048]{1,0:T(4,128)}, f32[4,1152]{1,0:T(4,128)}) custom-call(f32[256,128]{1,0:T(8,128)S(1)} %bitcast.8, f32[8,1152]{1,0:T(8,128)S(1)} %get-tuple-element.42.grad_rows, f32[8,1152]{1,0:T(8,128)S(1)} %copy-done.1, f32[8,1152]{1,0:T(8,128)S(1)} %copy-done.2, f32[4,2048]{1,0:T(4,128)S(1)} %copy-done.3, ...), custom_call_target="tpu_custom_call" | custom-call | tf_op jit(solution)/shard_map/pallas_call | solution.py:311
  (90 shorter events, 15.5 us)
Async XLA Ops:
  2.2 19.5 %all-to-all-start = ((bf16[16,8,640]{2,1,0:T(8,128)(2,1)}), bf16[16,8,640]{2,1,0:T(8,128)(2,1)S(1)}, u32[]{:S(2)}, u32[]{:S(2)}) async-start(bf16[16,8,640]{2,1,0:T(8,128)(2,1)} %shard_map.157), calls=%async_computation | async-start | bytes 327680 | tf_op jit(solution)/shard_map/all_to_all | solution.py:379
  12.8 1.6 %collective-permute-start.1 = (f32[8,128]{1,0:T(8,128)S(1)}, f32[8,128]{1,0:T(8,128)S(1)}, u32[]{:S(2)}, u32[]{:S(2)}) collective-permute-start(f32[8,128]{1,0:T(8,128)S(1)} %broadcast_in_dim.14), channel_id=1, source_target_pairs={{0,1},{1,0},{2,3},{3,2},{4,5},{5,4},{6,7},{7,6},{8,9},{9,8},{10,11... | collective-permute-start | bytes 12296 | tf_op jit(solution)/shard_map/ppermute | solution.py:54
  21.7 5.7 %collective-permute-start.3 = (bf16[128,640]{1,0:T(8,128)(2,1)S(1)}, bf16[128,640]{1,0:T(8,128)(2,1)S(1)}, u32[]{:S(2)}, u32[]{:S(2)}) collective-permute-start(bf16[128,640]{1,0:T(8,128)(2,1)S(1)} %bitcast.11), channel_id=1, source_target_pairs={{0,16},{16,32},{32,48},{48,0},{2,18},{18,34},{34,50},{50,2},{4,20}... | collective-permute-start | bytes 491528 | tf_op jit(solution)/shard_map/ppermute | solution.py:54
  23.0 7.3 %collective-permute-start.4 = (bf16[128,640]{1,0:T(8,128)(2,1)S(1)}, bf16[128,640]{1,0:T(8,128)(2,1)S(1)}, u32[]{:S(2)}, u32[]{:S(2)}) collective-permute-start(bf16[128,640]{1,0:T(8,128)(2,1)S(1)} %bitcast.12), channel_id=1, source_target_pairs={{0,32},{16,48},{32,0},{48,16},{2,34},{18,50},{34,2},{50,18},{4,36}... | collective-permute-start | bytes 491528 | tf_op jit(solution)/shard_map/ppermute | solution.py:54
  25.7 4.7 %collective-permute-start.5 = (bf16[128,640]{1,0:T(8,128)(2,1)S(1)}, bf16[128,640]{1,0:T(8,128)(2,1)S(1)}, u32[]{:S(2)}, u32[]{:S(2)}) collective-permute-start(bf16[128,640]{1,0:T(8,128)(2,1)S(1)} %bitcast.14), channel_id=1, source_target_pairs={{0,48},{16,0},{32,16},{48,32},{2,50},{18,2},{34,18},{50,34},{4,52}... | collective-permute-start | bytes 491528 | tf_op jit(solution)/shard_map/ppermute | solution.py:54
  30.4 11.0 %collective-permute-start.6 = (bf16[512,640]{1,0:T(8,128)(2,1)S(1)}, bf16[512,640]{1,0:T(8,128)(2,1)S(1)}, u32[]{:S(2)}, u32[]{:S(2)}) collective-permute-start(bf16[512,640]{1,0:T(8,128)(2,1)S(1)} %constant_dynamic-update-slice_fusion.near.plane), channel_id=1, source_target_pairs={{0,64},{64,128},{128,192},{192,0},{2,66},{66,130},{130,194},{194,2... | collective-permute-start | bytes 1966088 | tf_op jit(solution)/shard_map/ppermute | solution.py:54
  31.6 10.0 %collective-permute-start.7 = (bf16[512,640]{1,0:T(8,128)(2,1)S(1)}, bf16[512,640]{1,0:T(8,128)(2,1)S(1)}, u32[]{:S(2)}, u32[]{:S(2)}) collective-permute-start(bf16[512,640]{1,0:T(8,128)(2,1)S(1)} %constant_dynamic-update-slice_fusion.near.plane), channel_id=1, source_target_pairs={{0,192},{64,0},{128,64},{192,128},{2,194},{66,2},{130,66},{194,130... | collective-permute-start | bytes 1966088 | tf_op jit(solution)/shard_map/ppermute | solution.py:54
  33.4 13.4 %collective-permute-start = (bf16[128,2048]{1,0:T(8,128)(2,1)S(1)}, bf16[128,2048]{1,0:T(8,128)(2,1)S(1)}, u32[]{:S(2)}, u32[]{:S(2)}) collective-permute-start(bf16[128,2048]{1,0:T(8,128)(2,1)S(1)} %copy-done), channel_id=1, source_target_pairs={{0,1},{1,0},{2,3},{3,2},{4,5},{5,4},{6,7},{7,6},{8,9},{9,8},{10,11... | collective-permute-start | bytes 1572872 | tf_op jit(solution)/shard_map/ppermute | solution.py:54
  41.4 9.8 %collective-permute-start.8 = (bf16[256,640]{1,0:T(8,128)(2,1)S(1)}, bf16[256,640]{1,0:T(8,128)(2,1)S(1)}, u32[]{:S(2)}, u32[]{:S(2)}) collective-permute-start(bf16[256,640]{1,0:T(8,128)(2,1)S(1)} %slice.69), channel_id=1, source_target_pairs={{0,64},{64,128},{128,192},{192,0},{2,66},{66,130},{130,194},{194,2... | collective-permute-start | bytes 983048 | tf_op jit(solution)/shard_map/ppermute | solution.py:54
  41.6 9.7 %collective-permute-start.9 = (bf16[256,640]{1,0:T(8,128)(2,1)S(1)}, bf16[256,640]{1,0:T(8,128)(2,1)S(1)}, u32[]{:S(2)}, u32[]{:S(2)}) collective-permute-start(bf16[256,640]{1,0:T(8,128)(2,1)S(1)} %slice.70), channel_id=1, source_target_pairs={{0,192},{64,0},{128,64},{192,128},{2,194},{66,2},{130,66},{194,130... | collective-permute-start | bytes 983048 | tf_op jit(solution)/shard_map/ppermute | solution.py:54
  44.4 6.9 %collective-permute-start.12 = (bf16[128,512]{1,0:T(8,128)(2,1)S(1)}, bf16[128,512]{1,0:T(8,128)(2,1)S(1)}, u32[]{:S(2)}, u32[]{:S(2)}) collective-permute-start(bf16[128,512]{1,0:T(8,128)(2,1)S(1)} %get-tuple-element.43), channel_id=1, source_target_pairs={{0,1},{1,0},{2,3},{3,2},{4,5},{5,4},{6,7},{7,6},{8,9},{9,8},{10,11... | collective-permute-start | bytes 393224 | tf_op jit(solution)/shard_map/ppermute | solution.py:54
  47.9 11.9 %collective-permute-start.15 = (bf16[256,512]{1,0:T(8,128)(2,1)S(1)}, bf16[256,512]{1,0:T(8,128)(2,1)S(1)}, u32[]{:S(2)}, u32[]{:S(2)}) collective-permute-start(bf16[256,512]{1,0:T(8,128)(2,1)S(1)} %get-tuple-element.27.scaled1), channel_id=1, source_target_pairs={{0,192},{64,0},{128,64},{192,128},{2,194},{66,2},{130,66},{194,130... | collective-permute-start | bytes 786440 | tf_op jit(solution)/shard_map/ppermute | solution.py:54
  50.4 11.5 %collective-permute-start.17 = (bf16[256,512]{1,0:T(8,128)(2,1)S(1)}, bf16[256,512]{1,0:T(8,128)(2,1)S(1)}, u32[]{:S(2)}, u32[]{:S(2)}) collective-permute-start(bf16[256,512]{1,0:T(8,128)(2,1)S(1)} %get-tuple-element.28.scaled3), channel_id=1, source_target_pairs={{0,64},{64,128},{128,192},{192,0},{2,66},{66,130},{130,194},{194,2... | collective-permute-start | bytes 786440 | tf_op jit(solution)/shard_map/ppermute | solution.py:54
  53.5 9.0 %collective-permute-start.13 = (bf16[128,640]{1,0:T(8,128)(2,1)S(1)}, bf16[128,640]{1,0:T(8,128)(2,1)S(1)}, u32[]{:S(2)}, u32[]{:S(2)}) collective-permute-start(bf16[128,640]{1,0:T(8,128)(2,1)S(1)} %shard_map.161.down1), channel_id=1, source_target_pairs={{0,192},{64,0},{128,64},{192,128},{2,194},{66,2},{130,66},{194,130... | collective-permute-start | bytes 491528 | tf_op jit(solution)/shard_map/ppermute | solution.py:54
  58.6 8.6 %collective-permute-start.10 = (bf16[128,640]{1,0:T(8,128)(2,1)S(1)}, bf16[128,640]{1,0:T(8,128)(2,1)S(1)}, u32[]{:S(2)}, u32[]{:S(2)}) collective-permute-start(bf16[128,640]{1,0:T(8,128)(2,1)S(1)} %shard_map.160.down0), channel_id=1, source_target_pairs={{0,64},{64,128},{128,192},{192,0},{2,66},{66,130},{130,194},{194,2... | collective-permute-start | bytes 491528 | tf_op jit(solution)/shard_map/ppermute | solution.py:54
  58.7 11.3 %collective-permute-start.2 = (bf16[256,512]{1,0:T(8,128)(2,1)S(1)}, bf16[256,512]{1,0:T(8,128)(2,1)S(1)}, u32[]{:S(2)}, u32[]{:S(2)}) collective-permute-start(bf16[256,512]{1,0:T(8,128)(2,1)S(1)} %get-tuple-element.25.scaled2), channel_id=1, source_target_pairs={{0,128},{64,192},{128,0},{192,64},{2,130},{66,194},{130,2},{194,66... | collective-permute-start | bytes 786440 | tf_op jit(solution)/shard_map/ppermute | solution.py:54
  59.9 9.0 %collective-permute-start.18 = (bf16[128,640]{1,0:T(8,128)(2,1)S(1)}, bf16[128,640]{1,0:T(8,128)(2,1)S(1)}, u32[]{:S(2)}, u32[]{:S(2)}) collective-permute-start(bf16[128,640]{1,0:T(8,128)(2,1)S(1)} %shard_map.161.down1), channel_id=1, source_target_pairs={{0,64},{64,128},{128,192},{192,0},{2,66},{66,130},{130,194},{194,2... | collective-permute-start | bytes 491528 | tf_op jit(solution)/shard_map/ppermute | solution.py:54
  61.9 7.0 %collective-permute-start.16 = (bf16[128,640]{1,0:T(8,128)(2,1)S(1)}, bf16[128,640]{1,0:T(8,128)(2,1)S(1)}, u32[]{:S(2)}, u32[]{:S(2)}) collective-permute-start(bf16[128,640]{1,0:T(8,128)(2,1)S(1)} %shard_map.160.down0), channel_id=1, source_target_pairs={{0,192},{64,0},{128,64},{192,128},{2,194},{66,2},{130,66},{194,130... | collective-permute-start | bytes 491528 | tf_op jit(solution)/shard_map/ppermute | solution.py:54
  62.5 7.4 %collective-permute-start.14 = (bf16[128,640]{1,0:T(8,128)(2,1)S(1)}, bf16[128,640]{1,0:T(8,128)(2,1)S(1)}, u32[]{:S(2)}, u32[]{:S(2)}) collective-permute-start(bf16[128,640]{1,0:T(8,128)(2,1)S(1)} %collective-permute-done.13.ahead1), channel_id=1, source_target_pairs={{0,192},{64,0},{128,64},{192,128},{2,194},{66,2},{130,66},{194,130... | collective-permute-start | bytes 491528 | tf_op jit(solution)/shard_map/ppermute | solution.py:54
  67.1 5.4 %collective-permute-start.11 = (bf16[128,640]{1,0:T(8,128)(2,1)S(1)}, bf16[128,640]{1,0:T(8,128)(2,1)S(1)}, u32[]{:S(2)}, u32[]{:S(2)}) collective-permute-start(bf16[128,640]{1,0:T(8,128)(2,1)S(1)} %collective-permute-done.10.back0), channel_id=1, source_target_pairs={{0,64},{64,128},{128,192},{192,0},{2,66},{66,130},{130,194},{194,2... | collective-permute-start | bytes 491528 | tf_op jit(solution)/shard_map/ppermute | solution.py:54
  73.7 45.1 %copy-start.1 = (f32[8,1152]{1,0:T(8,128)S(1)}, f32[8,1152]{1,0:T(8,128)}, u32[]{:S(2)}) copy-start(f32[8,1152]{1,0:T(8,128)} %weight_first.1) | copy-start | bytes 110596
  73.8 5.9 %collective-permute-start.19 = (bf16[128,640]{1,0:T(8,128)(2,1)S(1)}, bf16[128,640]{1,0:T(8,128)(2,1)S(1)}, u32[]{:S(2)}, u32[]{:S(2)}) collective-permute-start(bf16[128,640]{1,0:T(8,128)(2,1)S(1)} %get-tuple-element.38), channel_id=1, source_target_pairs={{0,32},{16,48},{32,0},{48,16},{2,34},{18,50},{34,2},{50,18},{4,36}... | collective-permute-start | bytes 491528 | tf_op jit(solution)/shard_map/ppermute | solution.py:54
  74.2 5.4 %collective-permute-start.20 = (bf16[128,640]{1,0:T(8,128)(2,1)S(1)}, bf16[128,640]{1,0:T(8,128)(2,1)S(1)}, u32[]{:S(2)}, u32[]{:S(2)}) collective-permute-start(bf16[128,640]{1,0:T(8,128)(2,1)S(1)} %get-tuple-element.39), channel_id=1, source_target_pairs={{0,48},{16,0},{32,16},{48,32},{2,50},{18,2},{34,18},{50,34},{4,52}... | collective-permute-start | bytes 491528 | tf_op jit(solution)/shard_map/ppermute | solution.py:54
  75.0 6.3 %collective-permute-start.21 = (bf16[128,640]{1,0:T(8,128)(2,1)S(1)}, bf16[128,640]{1,0:T(8,128)(2,1)S(1)}, u32[]{:S(2)}, u32[]{:S(2)}) collective-permute-start(bf16[128,640]{1,0:T(8,128)(2,1)S(1)} %get-tuple-element.40), channel_id=1, source_target_pairs={{0,16},{16,32},{32,48},{48,0},{2,18},{18,34},{34,50},{50,2},{4,20}... | collective-permute-start | bytes 491528 | tf_op jit(solution)/shard_map/ppermute | solution.py:54
  (12 other events, 375.7 us)

commit v2 on v0

--- a/solution.py
+++ b/solution.py
@@ -83,11 +83,12 @@
             scaled[i // 4][rows, spot] = (normed * rates[part : part + 1, lanes]).astype(bf16)
 
 
-def project_kernel(scaled0, scaled1, scaled3, near, right, left, partial):
-    partial[...] = (
-        dot(scaled0[...], near[...], 1, 0)
-        + dot(scaled1[...], right[...], 1, 0)
-        + dot(scaled3[...], left[...], 1, 0)
+def project_kernel(scaled0, scaled1, scaled3, *refs):
+    halves, partial = refs[:-1], refs[-1]
+    partial[...] = sum(
+        dot(scaled[:, half * 256 : (half + 1) * 256], halves[2 * j + half][...], 1, 0)
+        for j, scaled in enumerate((scaled0, scaled1, scaled3))
+        for half in range(2)
     )
 
 
@@ -100,7 +101,7 @@
     row = lax.broadcasted_iota(jnp.int32, (SEQ, 128), 0)
     low = lane < 64
     first = (lane & 63) < 32
-    causal = row >= lane
+    causal = jnp.concatenate([row >= lane] * 4, axis=0)
     score_scale = 1.0 / math.sqrt(HEAD_DIM)
 
     def swap(tile):
@@ -132,31 +133,28 @@
         value_pair = jnp.concatenate(
             [jnp.where(low, values, 0.0), jnp.where(low, 0.0, half_turn(values))], axis=0
         ).astype(bf16)
-        grads = []
-        key_sum = jnp.zeros((2 * SEQ, 128), f32)
-        value_sum = jnp.zeros((2 * SEQ, 128), f32)
-        for t in range(4):
-            query = turned[t].astype(bf16)
-            upstream = cot[:, t * 128 : (t + 1) * 128]
-            scores = dot(query, key_pair, 1, 1) * score_scale
-            grad_probs = dot(upstream, value_pair, 1, 1)
-            probs_bf, grads_bf = [], []
-            for h in range(2):
-                side = slice(h * SEQ, (h + 1) * SEQ)
-                masked = jnp.where(causal, scores[:, side], -jnp.inf)
-                raised = jnp.exp(masked - jnp.max(masked, axis=1, keepdims=True))
-                probs = raised / jnp.sum(raised, axis=1, keepdims=True)
-                gp = grad_probs[:, side]
-                centre = jnp.sum(gp * probs, axis=1, keepdims=True)
-                probs_bf.append(probs.astype(bf16))
-                grads_bf.append((probs * (gp - centre) * score_scale).astype(bf16))
-            probs_pair = jnp.concatenate(probs_bf, axis=1)
-            grad_pair = jnp.concatenate(grads_bf, axis=1)
-            grads.append(dot(grad_pair, key_pair, 1, 0))
-            key_sum += dot(grad_pair, query, 0, 0)
-            value_sum += dot(probs_pair, upstream, 0, 0)
+        query = jnp.concatenate([q.astype(bf16) for q in turned], axis=0)
+        upstream = jnp.concatenate([cot[:, t * 128 : (t + 1) * 128] for t in range(4)], axis=0)
+        scores = dot(query, key_pair, 1, 1)
+        grad_probs = dot(upstream, value_pair, 1, 1)
+        probs_bf, grads_bf = [], []
+        for h in range(2):
+            side = slice(h * SEQ, (h + 1) * SEQ)
+            masked = jnp.where(causal, scores[:, side] * score_scale, -jnp.inf)
+            raised = jnp.exp(masked - jnp.max(masked, axis=1, keepdims=True))
+            probs = raised * (1.0 / jnp.sum(raised, axis=1, keepdims=True))
+            gp = grad_probs[:, side]
+            centre = jnp.sum(gp * probs, axis=1, keepdims=True)
+            probs_bf.append(probs.astype(bf16))
+            grads_bf.append((probs * (gp - centre) * score_scale).astype(bf16))
+        probs_pair = jnp.concatenate(probs_bf, axis=1)
+        grad_pair = jnp.concatenate(grads_bf, axis=1)
+        all_grads = dot(grad_pair, key_pair, 1, 0)
+        key_sum = dot(grad_pair, query, 0, 0)
+        value_sum = dot(probs_pair, upstream, 0, 0)
         grad_key = jnp.where(low, 0.0, half_turn(key_sum[:SEQ]) + key_sum[SEQ:])
         grad_value = jnp.where(low, value_sum[:SEQ] + half_turn(value_sum[SEQ:]), 0.0)
+        grads = [all_grads[t * SEQ : (t + 1) * SEQ] for t in range(4)]
         grads[3] = jnp.where(low, grads[3], grad_key)
         grads = [g * cosine - swap(g) * sine for g in grads] + [grad_value]
         grad_biased = jnp.concatenate(grads, axis=1)
@@ -180,9 +178,9 @@
         down[rows, 512:640] = jnp.where(low, last, tail).astype(bf16)
 
 
-def weight_terms(scaled, down, plane, carry):
+def weight_terms(scaled, down, planes, carry):
     grads, totals, tails = carry
-    back = dot(down, plane, 1, 1)
+    back = jnp.concatenate([dot(down, plane[...], 1, 1) for plane in planes], axis=1)
     grads = grads + dot(scaled, down, 0, 0)
     row = lax.broadcasted_iota(jnp.int32, (8, 512), 0)
     for part in range(scaled.shape[0] // SEQ):
@@ -193,33 +191,33 @@
     return grads, totals, tails
 
 
-def near_kernel(scaled, down, plane, grads, totals, tails):
+def near_kernel(scaled, down, plane_a, plane_b, grads, totals, tails):
     zero = (jnp.zeros((512, LANES), f32), jnp.zeros((8, 512), f32), None)
-    total = weight_terms(scaled[...], down[...], plane[...], zero)
+    total = weight_terms(scaled[...], down[...], (plane_a, plane_b), zero)
     grads[...], totals[...] = total[:2]
     tails[...] = down[:SEQ, 512:].astype(f32)
 
 
 def middle_kernel(
-    scaled1, down1, scaled3, down3, plane, grads_in, totals_in, tails_in, grads, totals, tails
+    scaled1, down1, scaled3, down3, plane_a, plane_b, grads_in, totals_in, tails_in, grads, totals, tails
 ):
     total = (grads_in[...], totals_in[...], None)
     for scaled, down in ((scaled1, down1), (scaled3, down3)):
-        total = weight_terms(scaled[...], down[...], plane[...], total)
+        total = weight_terms(scaled[...], down[...], (plane_a, plane_b), total)
     grads[...], totals[...] = total[:2]
     tails[...] = tails_in[...] + down1[:SEQ, 512:].astype(f32) + down3[:SEQ, 512:].astype(f32)
 
 
 def last_kernel(
-    tile_of, scaled, down_a, down_b, plane, grads_in, totals_in, tails_in, rates, part0, part1, part2, part3
+    tile_of, scaled, down_a, down_b, plane_a, plane_b, grads_in, totals_in, tails_in, rates, *parts
 ):
     total = (grads_in[...], totals_in[...], None)
-    total = weight_terms(scaled[:SEQ, :], down_a[...], plane[...], total)
-    grads, totals, _ = weight_terms(scaled[SEQ:, :], down_b[...], plane[...], total)
+    down = jnp.concatenate([down_a[...], down_b[...]], axis=0)
+    grads, totals, _ = weight_terms(scaled[...], down, (plane_a, plane_b), total)
     tails = tails_in[...] + down_a[:, 512:].astype(f32)
     tails = tails + pltpu.roll(tails, 108, 1)
     lane = lax.broadcasted_iota(jnp.int32, (SEQ, 128), 1)
-    for i, result in enumerate((part0, part1, part2, part3)):
+    for i, result in enumerate(parts):
         tile = tile_of[i]
         here = slice(i * 128, (i + 1) * 128)
         shares = totals[:, here] / rates[:, pl.ds(pl.multiple_of(tile * 128, 128), 128)]
@@ -388,11 +386,15 @@
     column, tokens, cotangent, member_ids = lax.optimization_barrier(
         (column, tokens, cotangent, member_ids)
     )
-    plane = jnp.concatenate([column] + [shift(column, INNER_RINGS, j) for j in (1, 2, 3)], axis=0)
-    right = shift(plane, OUTER_RINGS, 1)
-    left = shift(plane, OUTER_RINGS, -1)
-    far_a = shift(right[:256], OUTER_RINGS, 1)
-    far_b = shift(left[256:], OUTER_RINGS, -1)
+    others = [shift(column, INNER_RINGS, j) for j in (1, 2, 3)]
+    plane_a = jnp.concatenate([column, others[0]], axis=0)
+    plane_b = jnp.concatenate(others[1:], axis=0)
+    right_a = shift(plane_a, OUTER_RINGS, 1)
+    left_b = shift(plane_b, OUTER_RINGS, -1)
+    right_b = shift(plane_b, OUTER_RINGS, 1)
+    left_a = shift(plane_a, OUTER_RINGS, -1)
+    far_a = shift(right_a, OUTER_RINGS, 1)
+    far_b = shift(left_b, OUTER_RINGS, -1)
 
     partner_tokens = shift(tokens, PAIRS, 1)
     cot_zero = pad_lanes(cotangent[:, :GROUP_Q], 512)
@@ -426,7 +428,7 @@
     partial = call(
         project_kernel,
         [],
-        [scaled[0], scaled[1], scaled[3], plane, right, left],
+        [scaled[0], scaled[1], scaled[3], plane_a, plane_b, right_a, right_b, left_a, left_b],
         jax.ShapeDtypeStruct((2 * SEQ, LANES), f32),
     )
     far_scaled = [shift(scaled[j], OUTER_RINGS, -j) for j in (1, 2, 3)]
@@ -443,14 +445,16 @@
         jax.ShapeDtypeStruct((8, 512), f32),
         jax.ShapeDtypeStruct((SEQ, 128), f32),
     ]
-    near = call(near_kernel, [], [scaled[0], down, plane], sums)
+    near = call(near_kernel, [], [scaled[0], down, plane_a, plane_b], sums)
     down_far_a = shift(down_back[:SEQ], OUTER_RINGS, 1)
     down_far_b = shift(down_ahead[SEQ:], OUTER_RINGS, -1)
-    middle = call(middle_kernel, [], [far_scaled[0], down_ahead, far_scaled[2], down_back, plane, *near], sums)
+    middle = call(
+        middle_kernel, [], [far_scaled[0], down_ahead, far_scaled[2], down_back, plane_a, plane_b, *near], sums
+    )
     parts = call(
         last_kernel,
         [tile_of],
-        [far_scaled[1], down_far_a, down_far_b, plane, *middle, factors],
+        [far_scaled[1], down_far_a, down_far_b, plane_a, plane_b, *middle, factors],
         [jax.ShapeDtypeStruct((SEQ, LANES), f32)] + [jax.ShapeDtypeStruct((SEQ, LANES), bf16)] * 3,
     )
     got = [shift(parts[j], INNER_RINGS, -j) for j in (2, 1, 3)]

time: 120 us -> 118 us (0.983)
  waiting for transfers between devices: 27 us -> 23.1 us
  blocking collectives: 37.7 us -> 40 us
  Pallas kernels: 12.6 us -> 11.3 us
    ppermute x20 -> x22, waiting for transfers between devices: 20.9 us -> 17.2 us  [shift(): return lax.ppermute(array, AXIS, pairs)]
    pallas_call x9, Pallas kernels: 12.6 us -> 11.3 us  [call(): pl.pallas_call(kernel, in_specs=[SMEM] * len(scalars) + [VMEM] * len(arra...]
    all_to_all x1, blocking collectives: 19.5 us -> 20.7 us  [per_device(): lax.all_to_all(column_sum.astype(bf16).reshape(2 * NZ, 8, LANES), AXIS, s...]
    ppermute x20 -> x22, starting transfers between devices: 26.1 us -> 26.4 us  [shift(): return lax.ppermute(array, AXIS, pairs)]
  transfers between devices with their start and end apart: 21 -> 23, of which waited for: 10 -> 13; matrix products, arithmetic and copies ran while one was open for 2% -> 3% of each run, Pallas kernels for 3% -> 3%
where the time goes in v2:
time: 118 us
  blocking collectives  40 us (34%)
  starting transfers between devices  36.5 us (31%)
  waiting for transfers between devices  23.1 us (20%)
  Pallas kernels  11.3 us (10%)
  local copies, waits for them, and re-layouts  2.65 us (2%)
  between operations  2.29 us (2%)
  other arithmetic  1.84 us (2%)
    ppermute x22, starting transfers between devices, shift(): return lax.ppermute(array, AXIS, pairs)  26.4 us
    all_to_all x1, blocking collectives, per_device(): lax.all_to_all(column_sum.astype(bf16).reshape(2 * NZ, 8, LANES), AXIS, s...  20.7 us
    all_to_all x1, blocking collectives, per_device(): lax.all_to_all(jnp.broadcast_to(packed[:, None], (256, 1, 128)), AXIS, sp...  19.3 us
    ppermute x22, waiting for transfers between devices, shift(): return lax.ppermute(array, AXIS, pairs)  17.2 us
    pallas_call x9, Pallas kernels, call(): pl.pallas_call(kernel, in_specs=[SMEM] * len(scalars) + [VMEM] * len(arra...  11.3 us
    all_to_all x1, starting transfers between devices, per_device(): lax.all_to_all(spread, AXIS, split_axis=0, concat_axis=0, tiled=True, axi...  10.1 us
    all_to_all x1, waiting for transfers between devices, per_device(): lax.all_to_all(spread, AXIS, split_axis=0, concat_axis=0, tiled=True, axi...  5.9 us
  transfers between devices with their start and end apart: 23, of which 13 were waited for; matrix products, arithmetic and copies ran while one was open for 3% of the time, Pallas kernels for 3%

profile of v2, /device:TPU:1, one launch (start us, length us, event | category | flops | bytes accessed | tf_op | source)
XLA Modules:
  0.0 117.7 jit_solution(17781793267932211079)
XLA Ops:
  2.2 10.1 %all-to-all-start = ((bf16[16,8,640]{2,1,0:T(8,128)(2,1)}), bf16[16,8,640]{2,1,0:T(8,128)(2,1)S(1)}, u32[]{:S(2)}, u32[]{:S(2)}) async-start(bf16[16,8,640]{2,1,0:T(8,128)(2,1)} %shard_map.157), calls=%async_computation | async-start | bytes 327680 | tf_op jit(solution)/shard_map/all_to_all | solution.py:383
  15.9 5.9 %all-to-all-done = bf16[16,8,640]{2,1,0:T(8,128)(2,1)S(1)} async-done(((bf16[16,8,640]{2,1,0:T(8,128)(2,1)}), bf16[16,8,640]{2,1,0:T(8,128)(2,1)S(1)}, u32[]{:S(2)}, u32[]{:S(2)}) %all-to-all-start) | async-done | bytes 163872 | tf_op jit(solution)/shard_map/all_to_all | solution.py:383
  21.8 2.9 %collective-permute-start.4 = (bf16[128,640]{1,0:T(8,128)(2,1)S(1)}, bf16[128,640]{1,0:T(8,128)(2,1)S(1)}, u32[]{:S(2)}, u32[]{:S(2)}) collective-permute-start(bf16[128,640]{1,0:T(8,128)(2,1)S(1)} %bitcast.11), channel_id=1, source_target_pairs={{0,32},{16,48},{32,0},{48,16},{2,34},{18,50},{34,2},{50,18},{4,36}... | collective-permute-start | bytes 491528 | tf_op jit(solution)/shard_map/ppermute | solution.py:53
  27.8 2.3 %collective-permute-done.5 = bf16[128,640]{1,0:T(8,128)(2,1)S(1)} collective-permute-done((bf16[128,640]{1,0:T(8,128)(2,1)S(1)}, bf16[128,640]{1,0:T(8,128)(2,1)S(1)}, u32[]{:S(2)}, u32[]{:S(2)}) %collective-permute-start.5) | collective-permute-done | bytes 163872 | tf_op jit(solution)/shard_map/ppermute | solution.py:53
  30.1 2.5 %collective-permute-start.9 = (bf16[256,640]{1,0:T(8,128)(2,1)S(1)}, bf16[256,640]{1,0:T(8,128)(2,1)S(1)}, u32[]{:S(2)}, u32[]{:S(2)}) collective-permute-start(bf16[256,640]{1,0:T(8,128)(2,1)S(1)} %constant_dynamic-update-slice_fusion.2.refs_1_.plane_b), channel_id=1, source_target_pairs={{0,192},{64,0},{128,64},{192,128},{2,194},{66,2},{130,66},{194,130... | collective-permute-start | bytes 983048 | tf_op jit(solution)/shard_map/ppermute | solution.py:53
  33.4 1.3 %collective-permute-start.7 = (bf16[256,640]{1,0:T(8,128)(2,1)S(1)}, bf16[256,640]{1,0:T(8,128)(2,1)S(1)}, u32[]{:S(2)}, u32[]{:S(2)}) collective-permute-start(bf16[256,640]{1,0:T(8,128)(2,1)S(1)} %constant_dynamic-update-slice_fusion.2.refs_1_.plane_b), channel_id=1, source_target_pairs={{0,64},{64,128},{128,192},{192,0},{2,66},{66,130},{130,194},{194,2... | collective-permute-start | bytes 983048 | tf_op jit(solution)/shard_map/ppermute | solution.py:53
  34.7 1.5 %collective-permute-start.8 = (bf16[256,640]{1,0:T(8,128)(2,1)S(1)}, bf16[256,640]{1,0:T(8,128)(2,1)S(1)}, u32[]{:S(2)}, u32[]{:S(2)}) collective-permute-start(bf16[256,640]{1,0:T(8,128)(2,1)S(1)} %constant_dynamic-update-slice_fusion.refs_0_.plane_a), channel_id=1, source_target_pairs={{0,192},{64,0},{128,64},{192,128},{2,194},{66,2},{130,66},{194,130... | collective-permute-start | bytes 983048 | tf_op jit(solution)/shard_map/ppermute | solution.py:53
  36.6 3.1 %collective-permute-start.11 = (bf16[256,640]{1,0:T(8,128)(2,1)S(1)}, bf16[256,640]{1,0:T(8,128)(2,1)S(1)}, u32[]{:S(2)}, u32[]{:S(2)}) collective-permute-start(bf16[256,640]{1,0:T(8,128)(2,1)S(1)} %collective-permute-done.9.refs_5_), channel_id=1, source_target_pairs={{0,192},{64,0},{128,64},{192,128},{2,194},{66,2},{130,66},{194,130... | collective-permute-start | bytes 983048 | tf_op jit(solution)/shard_map/ppermute | solution.py:53
  40.2 2.5 %collective-permute-start.12 = (bf16[128,512]{1,0:T(8,128)(2,1)S(1)}, bf16[128,512]{1,0:T(8,128)(2,1)S(1)}, u32[]{:S(2)}, u32[]{:S(2)}) collective-permute-start(bf16[128,512]{1,0:T(8,128)(2,1)S(1)} %get-tuple-element.43), channel_id=1, source_target_pairs={{0,1},{1,0},{2,3},{3,2},{4,5},{5,4},{6,7},{7,6},{8,9},{9,8},{10,11... | collective-permute-start | bytes 393224 | tf_op jit(solution)/shard_map/ppermute | solution.py:53
  42.9 1.1 shard_map.158
  44.8 2.7 %collective-permute-done.10.far_a = bf16[256,640]{1,0:T(8,128)(2,1)S(1)} collective-permute-done((bf16[256,640]{1,0:T(8,128)(2,1)S(1)}, bf16[256,640]{1,0:T(8,128)(2,1)S(1)}, u32[]{:S(2)}, u32[]{:S(2)}) %collective-permute-start.10) | collective-permute-done | bytes 327712 | tf_op jit(solution)/shard_map/ppermute | solution.py:53
  47.6 3.9 %shard_map.160.down = bf16[256,640]{1,0:T(8,128)(2,1)S(1)} custom-call(s32[2]{0:T(128)S(1)} %pad_add_fusion.members, bf16[256,512]{1,0:T(8,128)(2,1)S(1)} %get-tuple-element.25.scaled2, f32[256,640]{1,0:T(8,128)S(1)} %shard_map.159.partial, bf16[256,640]{1,0:T(8,128)(2,1)S(1)} %collective-permute-done.10.far_a, ...), custom_call_target="tpu_custom_call" | custom-call | tf_op jit(solution)/shard_map/pallas_call | solution.py:315
  51.6 2.7 %collective-permute-start.15 = (bf16[256,640]{1,0:T(8,128)(2,1)S(1)}, bf16[256,640]{1,0:T(8,128)(2,1)S(1)}, u32[]{:S(2)}, u32[]{:S(2)}) collective-permute-start(bf16[256,640]{1,0:T(8,128)(2,1)S(1)} %shard_map.160.down), channel_id=1, source_target_pairs={{0,192},{64,0},{128,64},{192,128},{2,194},{66,2},{130,66},{194,130... | collective-permute-start | bytes 983048 | tf_op jit(solution)/shard_map/ppermute | solution.py:53
  54.3 1.4 %collective-permute-start.18 = (bf16[256,512]{1,0:T(8,128)(2,1)S(1)}, bf16[256,512]{1,0:T(8,128)(2,1)S(1)}, u32[]{:S(2)}, u32[]{:S(2)}) collective-permute-start(bf16[256,512]{1,0:T(8,128)(2,1)S(1)} %get-tuple-element.28.scaled3), channel_id=1, source_target_pairs={{0,64},{64,128},{128,192},{192,0},{2,66},{66,130},{130,194},{194,2... | collective-permute-start | bytes 786440 | tf_op jit(solution)/shard_map/ppermute | solution.py:53
  55.7 3.3 %collective-permute-done.13.down3 = bf16[256,640]{1,0:T(8,128)(2,1)S(1)} collective-permute-done((bf16[256,640]{1,0:T(8,128)(2,1)S(1)}, bf16[256,640]{1,0:T(8,128)(2,1)S(1)}, u32[]{:S(2)}, u32[]{:S(2)}) %collective-permute-start.13) | collective-permute-done | bytes 327712 | tf_op jit(solution)/shard_map/ppermute | solution.py:53
  59.2 2.7 %collective-permute-start.16 = (bf16[128,640]{1,0:T(8,128)(2,1)S(1)}, bf16[128,640]{1,0:T(8,128)(2,1)S(1)}, u32[]{:S(2)}, u32[]{:S(2)}) collective-permute-start(bf16[128,640]{1,0:T(8,128)(2,1)S(1)} %slice.82), channel_id=1, source_target_pairs={{0,192},{64,0},{128,64},{192,128},{2,194},{66,2},{130,66},{194,130... | collective-permute-start | bytes 491528 | tf_op jit(solution)/shard_map/ppermute | solution.py:53
  62.5 1.4 %collective-permute-done.17.scaled1 = bf16[256,512]{1,0:T(8,128)(2,1)S(1)} collective-permute-done((bf16[256,512]{1,0:T(8,128)(2,1)S(1)}, bf16[256,512]{1,0:T(8,128)(2,1)S(1)}, u32[]{:S(2)}, u32[]{:S(2)}) %collective-permute-start.17) | collective-permute-done | bytes 262176 | tf_op jit(solution)/shard_map/ppermute | solution.py:53
  66.4 1.2 %shard_map.163 = (f32[128,640]{1,0:T(8,128)S(1)}, bf16[128,640]{1,0:T(8,128)(2,1)S(1)}, bf16[128,640]{1,0:T(8,128)(2,1)S(1)}, bf16[128,640]{1,0:T(8,128)(2,1)S(1)}) custom-call(s32[16]{0:T(128)S(1)} %fusion.4.tile_of, bf16[256,512]{1,0:T(8,128)(2,1)S(1)} %collective-permute-done.2.scaled, bf16[128,640]{1,0:T(8,128)(2,1)S(1)} %collective-permute-done.14.down_a, ...), custom_call_target="tpu_custom_call" | custom-call | tf_op jit(solution)/shard_map/pallas_call | solution.py:315
  68.3 1.9 %collective-permute-start.20 = (bf16[128,640]{1,0:T(8,128)(2,1)S(1)}, bf16[128,640]{1,0:T(8,128)(2,1)S(1)}, u32[]{:S(2)}, u32[]{:S(2)}) collective-permute-start(bf16[128,640]{1,0:T(8,128)(2,1)S(1)} %get-tuple-element.39), channel_id=1, source_target_pairs={{0,48},{16,0},{32,16},{48,32},{2,50},{18,2},{34,18},{50,34},{4,52}... | collective-permute-start | bytes 491528 | tf_op jit(solution)/shard_map/ppermute | solution.py:53
  70.5 2.9 %collective-permute-done.19 = bf16[128,640]{1,0:T(8,128)(2,1)S(1)} collective-permute-done((bf16[128,640]{1,0:T(8,128)(2,1)S(1)}, bf16[128,640]{1,0:T(8,128)(2,1)S(1)}, u32[]{:S(2)}, u32[]{:S(2)}) %collective-permute-start.19) | collective-permute-done | bytes 163872 | tf_op jit(solution)/shard_map/ppermute | solution.py:53
  73.4 1.5 %collective-permute-done.20 = bf16[128,640]{1,0:T(8,128)(2,1)S(1)} collective-permute-done((bf16[128,640]{1,0:T(8,128)(2,1)S(1)}, bf16[128,640]{1,0:T(8,128)(2,1)S(1)}, u32[]{:S(2)}, u32[]{:S(2)}) %collective-permute-start.20) | collective-permute-done | bytes 163872 | tf_op jit(solution)/shard_map/ppermute | solution.py:53
  75.7 20.7 %all_to_all.15.pieces = bf16[16,8,640]{2,1,0:T(8,128)(2,1)S(1)} all-to-all(bf16[16,8,640]{2,1,0:T(8,128)(2,1)S(1)} %fusion), channel_id=1, replica_groups={{0,1,2,3,4,5,6,7,8,9,10,11,12,13,14,15},{16,17,18,19,20,21,22,23,24,25,..., dimensions={0} | all-to-all | bytes 327680 | tf_op jit(solution)/shard_map/all_to_all | solution.py:462
  96.7 19.3 %all_to_all.16 = f32[256,1,128]{2,1,0:T(1,128)S(1)} all-to-all(f32[256,1,128]{2,1,0:T(1,128)S(1)} %broadcast_in_dim.17), channel_id=1, replica_groups=mesh['fsdp'=256] {'fsdp'}, dimensions={0} | all-to-all | bytes 262144 | tf_op jit(solution)/shard_map/all_to_all | solution.py:473
  116.1 1.6 %shard_map.165 = (f32[8,1152]{1,0:T(8,128)}, f32[4,2048]{1,0:T(4,128)}, f32[4,1152]{1,0:T(4,128)}) custom-call(f32[256,128]{1,0:T(8,128)S(1)} %bitcast.8, f32[8,1152]{1,0:T(8,128)S(1)} %get-tuple-element.42.grad_rows, f32[8,1152]{1,0:T(8,128)S(1)} %copy-done.1, f32[8,1152]{1,0:T(8,128)S(1)} %copy-done.2, f32[4,2048]{1,0:T(4,128)S(1)} %copy-done.3, ...), custom_call_target="tpu_custom_call" | custom-call | tf_op jit(solution)/shard_map/pallas_call | solution.py:315
  (87 shorter events, 14.8 us)
Async XLA Ops:
  2.2 19.6 %all-to-all-start = ((bf16[16,8,640]{2,1,0:T(8,128)(2,1)}), bf16[16,8,640]{2,1,0:T(8,128)(2,1)S(1)}, u32[]{:S(2)}, u32[]{:S(2)}) async-start(bf16[16,8,640]{2,1,0:T(8,128)(2,1)} %shard_map.157), calls=%async_computation | async-start | bytes 327680 | tf_op jit(solution)/shard_map/all_to_all | solution.py:383
  12.9 1.6 %collective-permute-start.1 = (f32[8,128]{1,0:T(8,128)S(1)}, f32[8,128]{1,0:T(8,128)S(1)}, u32[]{:S(2)}, u32[]{:S(2)}) collective-permute-start(f32[8,128]{1,0:T(8,128)S(1)} %broadcast_in_dim.14), channel_id=1, source_target_pairs={{0,1},{1,0},{2,3},{3,2},{4,5},{5,4},{6,7},{7,6},{8,9},{9,8},{10,11... | collective-permute-start | bytes 12296 | tf_op jit(solution)/shard_map/ppermute | solution.py:53
  21.8 6.0 %collective-permute-start.4 = (bf16[128,640]{1,0:T(8,128)(2,1)S(1)}, bf16[128,640]{1,0:T(8,128)(2,1)S(1)}, u32[]{:S(2)}, u32[]{:S(2)}) collective-permute-start(bf16[128,640]{1,0:T(8,128)(2,1)S(1)} %bitcast.11), channel_id=1, source_target_pairs={{0,32},{16,48},{32,0},{48,16},{2,34},{18,50},{34,2},{50,18},{4,36}... | collective-permute-start | bytes 491528 | tf_op jit(solution)/shard_map/ppermute | solution.py:53
  25.5 4.5 %collective-permute-start.5 = (bf16[128,640]{1,0:T(8,128)(2,1)S(1)}, bf16[128,640]{1,0:T(8,128)(2,1)S(1)}, u32[]{:S(2)}, u32[]{:S(2)}) collective-permute-start(bf16[128,640]{1,0:T(8,128)(2,1)S(1)} %bitcast.12), channel_id=1, source_target_pairs={{0,48},{16,0},{32,16},{48,32},{2,50},{18,2},{34,18},{50,34},{4,52}... | collective-permute-start | bytes 491528 | tf_op jit(solution)/shard_map/ppermute | solution.py:53
  26.4 6.2 %collective-permute-start.3 = (bf16[128,640]{1,0:T(8,128)(2,1)S(1)}, bf16[128,640]{1,0:T(8,128)(2,1)S(1)}, u32[]{:S(2)}, u32[]{:S(2)}) collective-permute-start(bf16[128,640]{1,0:T(8,128)(2,1)S(1)} %bitcast.14), channel_id=1, source_target_pairs={{0,16},{16,32},{32,48},{48,0},{2,18},{18,34},{34,50},{50,2},{4,20}... | collective-permute-start | bytes 491528 | tf_op jit(solution)/shard_map/ppermute | solution.py:53
  27.2 13.0 %collective-permute-start = (bf16[128,2048]{1,0:T(8,128)(2,1)S(1)}, bf16[128,2048]{1,0:T(8,128)(2,1)S(1)}, u32[]{:S(2)}, u32[]{:S(2)}) collective-permute-start(bf16[128,2048]{1,0:T(8,128)(2,1)S(1)} %copy-done), channel_id=1, source_target_pairs={{0,1},{1,0},{2,3},{3,2},{4,5},{5,4},{6,7},{7,6},{8,9},{9,8},{10,11... | collective-permute-start | bytes 1572872 | tf_op jit(solution)/shard_map/ppermute | solution.py:53
  30.1 6.5 %collective-permute-start.9 = (bf16[256,640]{1,0:T(8,128)(2,1)S(1)}, bf16[256,640]{1,0:T(8,128)(2,1)S(1)}, u32[]{:S(2)}, u32[]{:S(2)}) collective-permute-start(bf16[256,640]{1,0:T(8,128)(2,1)S(1)} %constant_dynamic-update-slice_fusion.2.refs_1_.plane_b), channel_id=1, source_target_pairs={{0,192},{64,0},{128,64},{192,128},{2,194},{66,2},{130,66},{194,130... | collective-permute-start | bytes 983048 | tf_op jit(solution)/shard_map/ppermute | solution.py:53
  32.6 7.5 %collective-permute-start.6 = (bf16[256,640]{1,0:T(8,128)(2,1)S(1)}, bf16[256,640]{1,0:T(8,128)(2,1)S(1)}, u32[]{:S(2)}, u32[]{:S(2)}) collective-permute-start(bf16[256,640]{1,0:T(8,128)(2,1)S(1)} %constant_dynamic-update-slice_fusion.refs_0_.plane_a), channel_id=1, source_target_pairs={{0,64},{64,128},{128,192},{192,0},{2,66},{66,130},{130,194},{194,2... | collective-permute-start | bytes 983048 | tf_op jit(solution)/shard_map/ppermute | solution.py:53
  33.4 10.6 %collective-permute-start.7 = (bf16[256,640]{1,0:T(8,128)(2,1)S(1)}, bf16[256,640]{1,0:T(8,128)(2,1)S(1)}, u32[]{:S(2)}, u32[]{:S(2)}) collective-permute-start(bf16[256,640]{1,0:T(8,128)(2,1)S(1)} %constant_dynamic-update-slice_fusion.2.refs_1_.plane_b), channel_id=1, source_target_pairs={{0,64},{64,128},{128,192},{192,0},{2,66},{66,130},{130,194},{194,2... | collective-permute-start | bytes 983048 | tf_op jit(solution)/shard_map/ppermute | solution.py:53
  34.7 9.3 %collective-permute-start.8 = (bf16[256,640]{1,0:T(8,128)(2,1)S(1)}, bf16[256,640]{1,0:T(8,128)(2,1)S(1)}, u32[]{:S(2)}, u32[]{:S(2)}) collective-permute-start(bf16[256,640]{1,0:T(8,128)(2,1)S(1)} %constant_dynamic-update-slice_fusion.refs_0_.plane_a), channel_id=1, source_target_pairs={{0,192},{64,0},{128,64},{192,128},{2,194},{66,2},{130,66},{194,130... | collective-permute-start | bytes 983048 | tf_op jit(solution)/shard_map/ppermute | solution.py:53
  36.6 8.2 %collective-permute-start.11 = (bf16[256,640]{1,0:T(8,128)(2,1)S(1)}, bf16[256,640]{1,0:T(8,128)(2,1)S(1)}, u32[]{:S(2)}, u32[]{:S(2)}) collective-permute-start(bf16[256,640]{1,0:T(8,128)(2,1)S(1)} %collective-permute-done.9.refs_5_), channel_id=1, source_target_pairs={{0,192},{64,0},{128,64},{192,128},{2,194},{66,2},{130,66},{194,130... | collective-permute-start | bytes 983048 | tf_op jit(solution)/shard_map/ppermute | solution.py:53
  40.1 7.4 %collective-permute-start.10 = (bf16[256,640]{1,0:T(8,128)(2,1)S(1)}, bf16[256,640]{1,0:T(8,128)(2,1)S(1)}, u32[]{:S(2)}, u32[]{:S(2)}) collective-permute-start(bf16[256,640]{1,0:T(8,128)(2,1)S(1)} %collective-permute-done.6.refs_2_), channel_id=1, source_target_pairs={{0,64},{64,128},{128,192},{192,0},{2,66},{66,130},{130,194},{194,2... | collective-permute-start | bytes 983048 | tf_op jit(solution)/shard_map/ppermute | solution.py:53
  40.2 4.6 %collective-permute-start.12 = (bf16[128,512]{1,0:T(8,128)(2,1)S(1)}, bf16[128,512]{1,0:T(8,128)(2,1)S(1)}, u32[]{:S(2)}, u32[]{:S(2)}) collective-permute-start(bf16[128,512]{1,0:T(8,128)(2,1)S(1)} %get-tuple-element.43), channel_id=1, source_target_pairs={{0,1},{1,0},{2,3},{3,2},{4,5},{5,4},{6,7},{7,6},{8,9},{9,8},{10,11... | collective-permute-start | bytes 393224 | tf_op jit(solution)/shard_map/ppermute | solution.py:53
  51.5 7.5 %collective-permute-start.13 = (bf16[256,640]{1,0:T(8,128)(2,1)S(1)}, bf16[256,640]{1,0:T(8,128)(2,1)S(1)}, u32[]{:S(2)}, u32[]{:S(2)}) collective-permute-start(bf16[256,640]{1,0:T(8,128)(2,1)S(1)} %shard_map.160.down), channel_id=1, source_target_pairs={{0,64},{64,128},{128,192},{192,0},{2,66},{66,130},{130,194},{194,2... | collective-permute-start | bytes 983048 | tf_op jit(solution)/shard_map/ppermute | solution.py:53
  51.6 7.5 %collective-permute-start.15 = (bf16[256,640]{1,0:T(8,128)(2,1)S(1)}, bf16[256,640]{1,0:T(8,128)(2,1)S(1)}, u32[]{:S(2)}, u32[]{:S(2)}) collective-permute-start(bf16[256,640]{1,0:T(8,128)(2,1)S(1)} %shard_map.160.down), channel_id=1, source_target_pairs={{0,192},{64,0},{128,64},{192,128},{2,194},{66,2},{130,66},{194,130... | collective-permute-start | bytes 983048 | tf_op jit(solution)/shard_map/ppermute | solution.py:53
  54.3 9.6 %collective-permute-start.17 = (bf16[256,512]{1,0:T(8,128)(2,1)S(1)}, bf16[256,512]{1,0:T(8,128)(2,1)S(1)}, u32[]{:S(2)}, u32[]{:S(2)}) collective-permute-start(bf16[256,512]{1,0:T(8,128)(2,1)S(1)} %get-tuple-element.27.scaled1), channel_id=1, source_target_pairs={{0,192},{64,0},{128,64},{192,128},{2,194},{66,2},{130,66},{194,130... | collective-permute-start | bytes 786440 | tf_op jit(solution)/shard_map/ppermute | solution.py:53
  54.3 10.3 %collective-permute-start.18 = (bf16[256,512]{1,0:T(8,128)(2,1)S(1)}, bf16[256,512]{1,0:T(8,128)(2,1)S(1)}, u32[]{:S(2)}, u32[]{:S(2)}) collective-permute-start(bf16[256,512]{1,0:T(8,128)(2,1)S(1)} %get-tuple-element.28.scaled3), channel_id=1, source_target_pairs={{0,64},{64,128},{128,192},{192,0},{2,66},{66,130},{130,194},{194,2... | collective-permute-start | bytes 786440 | tf_op jit(solution)/shard_map/ppermute | solution.py:53
  55.7 10.0 %collective-permute-start.2 = (bf16[256,512]{1,0:T(8,128)(2,1)S(1)}, bf16[256,512]{1,0:T(8,128)(2,1)S(1)}, u32[]{:S(2)}, u32[]{:S(2)}) collective-permute-start(bf16[256,512]{1,0:T(8,128)(2,1)S(1)} %get-tuple-element.25.scaled2), channel_id=1, source_target_pairs={{0,128},{64,192},{128,0},{192,64},{2,130},{66,194},{130,2},{194,66... | collective-permute-start | bytes 786440 | tf_op jit(solution)/shard_map/ppermute | solution.py:53
  59.0 7.4 %collective-permute-start.14 = (bf16[128,640]{1,0:T(8,128)(2,1)S(1)}, bf16[128,640]{1,0:T(8,128)(2,1)S(1)}, u32[]{:S(2)}, u32[]{:S(2)}) collective-permute-start(bf16[128,640]{1,0:T(8,128)(2,1)S(1)} %slice.81), channel_id=1, source_target_pairs={{0,64},{64,128},{128,192},{192,0},{2,66},{66,130},{130,194},{194,2... | collective-permute-start | bytes 491528 | tf_op jit(solution)/shard_map/ppermute | solution.py:53
  59.2 7.2 %collective-permute-start.16 = (bf16[128,640]{1,0:T(8,128)(2,1)S(1)}, bf16[128,640]{1,0:T(8,128)(2,1)S(1)}, u32[]{:S(2)}, u32[]{:S(2)}) collective-permute-start(bf16[128,640]{1,0:T(8,128)(2,1)S(1)} %slice.82), channel_id=1, source_target_pairs={{0,192},{64,0},{128,64},{192,128},{2,194},{66,2},{130,66},{194,130... | collective-permute-start | bytes 491528 | tf_op jit(solution)/shard_map/ppermute | solution.py:53
  67.6 48.4 %copy-start.1 = (f32[8,1152]{1,0:T(8,128)S(1)}, f32[8,1152]{1,0:T(8,128)}, u32[]{:S(2)}) copy-start(f32[8,1152]{1,0:T(8,128)} %weight_first.1) | copy-start | bytes 110596
  67.7 5.8 %collective-permute-start.19 = (bf16[128,640]{1,0:T(8,128)(2,1)S(1)}, bf16[128,640]{1,0:T(8,128)(2,1)S(1)}, u32[]{:S(2)}, u32[]{:S(2)}) collective-permute-start(bf16[128,640]{1,0:T(8,128)(2,1)S(1)} %get-tuple-element.38), channel_id=1, source_target_pairs={{0,32},{16,48},{32,0},{48,16},{2,34},{18,50},{34,2},{50,18},{4,36}... | collective-permute-start | bytes 491528 | tf_op jit(solution)/shard_map/ppermute | solution.py:53
  68.3 6.7 %collective-permute-start.20 = (bf16[128,640]{1,0:T(8,128)(2,1)S(1)}, bf16[128,640]{1,0:T(8,128)(2,1)S(1)}, u32[]{:S(2)}, u32[]{:S(2)}) collective-permute-start(bf16[128,640]{1,0:T(8,128)(2,1)S(1)} %get-tuple-element.39), channel_id=1, source_target_pairs={{0,48},{16,0},{32,16},{48,32},{2,50},{18,2},{34,18},{50,34},{4,52}... | collective-permute-start | bytes 491528 | tf_op jit(solution)/shard_map/ppermute | solution.py:53
  70.2 5.4 %collective-permute-start.21 = (bf16[128,640]{1,0:T(8,128)(2,1)S(1)}, bf16[128,640]{1,0:T(8,128)(2,1)S(1)}, u32[]{:S(2)}, u32[]{:S(2)}) collective-permute-start(bf16[128,640]{1,0:T(8,128)(2,1)S(1)} %get-tuple-element.40), channel_id=1, source_target_pairs={{0,16},{16,32},{32,48},{48,0},{2,18},{18,34},{34,50},{50,2},{4,20}... | collective-permute-start | bytes 491528 | tf_op jit(solution)/shard_map/ppermute | solution.py:53
  (11 other events, 396.3 us)

commit v3 on v2

--- a/solution.py
+++ b/solution.py
@@ -198,23 +198,20 @@
     tails[...] = down[:SEQ, 512:].astype(f32)
 
 
-def middle_kernel(
-    scaled1, down1, scaled3, down3, plane_a, plane_b, grads_in, totals_in, tails_in, grads, totals, tails
+def middle_kernel(scaled, down, plane_a, plane_b, grads_in, totals_in, tails_in, grads, totals, tails):
+    total = (grads_in[...], totals_in[...], None)
+    total = weight_terms(scaled[...], down[...], (plane_a, plane_b), total)
+    grads[...], totals[...] = total[:2]
+    tails[...] = tails_in[...] + down[:SEQ, 512:].astype(f32)
+
+
+def last_kernel(
+    tile_of, scaled1, down1, scaled3, down3, plane_a, plane_b, grads_in, totals_in, tails_in, rates, *parts
 ):
     total = (grads_in[...], totals_in[...], None)
-    for scaled, down in ((scaled1, down1), (scaled3, down3)):
-        total = weight_terms(scaled[...], down[...], (plane_a, plane_b), total)
-    grads[...], totals[...] = total[:2]
-    tails[...] = tails_in[...] + down1[:SEQ, 512:].astype(f32) + down3[:SEQ, 512:].astype(f32)
-
-
-def last_kernel(
-    tile_of, scaled, down_a, down_b, plane_a, plane_b, grads_in, totals_in, tails_in, rates, *parts
-):
-    total = (grads_in[...], totals_in[...], None)
-    down = jnp.concatenate([down_a[...], down_b[...]], axis=0)
-    grads, totals, _ = weight_terms(scaled[...], down, (plane_a, plane_b), total)
-    tails = tails_in[...] + down_a[:, 512:].astype(f32)
+    total = weight_terms(scaled1[...], down1[...], (plane_a, plane_b), total)
+    grads, totals, _ = weight_terms(scaled3[...], down3[...], (plane_a, plane_b), total)
+    tails = tails_in[...] + down1[:SEQ, 512:].astype(f32) + down3[:SEQ, 512:].astype(f32)
     tails = tails + pltpu.roll(tails, 108, 1)
     lane = lax.broadcasted_iota(jnp.int32, (SEQ, 128), 1)
     for i, result in enumerate(parts):
@@ -383,9 +380,7 @@
     column = lax.all_to_all(
         spread, AXIS, split_axis=0, concat_axis=0, tiled=True, axis_index_groups=COLUMNS
     ).reshape(NZ * 16, LANES)
-    column, tokens, cotangent, member_ids = lax.optimization_barrier(
-        (column, tokens, cotangent, member_ids)
-    )
+    column, cotangent = lax.optimization_barrier((column, cotangent))
     others = [shift(column, INNER_RINGS, j) for j in (1, 2, 3)]
     plane_a = jnp.concatenate([column, others[0]], axis=0)
     plane_b = jnp.concatenate(others[1:], axis=0)
@@ -438,26 +433,21 @@
         [scaled[2], partial, far_a, far_b, slopes, bias, cosine, sine, cot_own, cot_partner],
         jax.ShapeDtypeStruct((2 * SEQ, LANES), bf16),
     )
-    down_back = shift(down, OUTER_RINGS, 1)
-    down_ahead = shift(down, OUTER_RINGS, -1)
+    down_of = [shift(down, OUTER_RINGS, -j) for j in (1, 2, 3)]
     sums = [
         jax.ShapeDtypeStruct((512, LANES), f32),
         jax.ShapeDtypeStruct((8, 512), f32),
         jax.ShapeDtypeStruct((SEQ, 128), f32),
     ]
     near = call(near_kernel, [], [scaled[0], down, plane_a, plane_b], sums)
-    down_far_a = shift(down_back[:SEQ], OUTER_RINGS, 1)
-    down_far_b = shift(down_ahead[SEQ:], OUTER_RINGS, -1)
-    middle = call(
-        middle_kernel, [], [far_scaled[0], down_ahead, far_scaled[2], down_back, plane_a, plane_b, *near], sums
-    )
+    middle = call(middle_kernel, [], [far_scaled[1], down_of[1], plane_a, plane_b, *near], sums)
     parts = call(
         last_kernel,
         [tile_of],
-        [far_scaled[1], down_far_a, down_far_b, plane_a, plane_b, *middle, factors],
+        [far_scaled[0], down_of[0], far_scaled[2], down_of[2], plane_a, plane_b, *middle, factors],
         [jax.ShapeDtypeStruct((SEQ, LANES), f32)] + [jax.ShapeDtypeStruct((SEQ, LANES), bf16)] * 3,
     )
-    got = [shift(parts[j], INNER_RINGS, -j) for j in (2, 1, 3)]
+    got = [shift(parts[j], INNER_RINGS, -j) for j in (1, 2, 3)]
     column_sum = parts[0] + sum(g.astype(f32) for g in got)
     pieces = lax.all_to_all(
         column_sum.astype(bf16).reshape(2 * NZ, 8, LANES),

time: 118 us -> 124 us (1.051)
  waiting for transfers between devices: 23.1 us -> 35.6 us
  starting transfers between devices: 36.5 us -> 32.4 us
  blocking collectives: 40 us -> 37.7 us
    ppermute x22 -> x21, waiting for transfers between devices: 17.2 us -> 29.7 us  [shift(): return lax.ppermute(array, AXIS, pairs)]
    all_to_all x1, starting transfers between devices: 10.1 us -> 7.31 us  [per_device(): lax.all_to_all(spread, AXIS, split_axis=0, concat_axis=0, tiled=True, axi...]
    all_to_all x1, blocking collectives: 20.7 us -> 18.4 us  [per_device(): lax.all_to_all(column_sum.astype(bf16).reshape(2 * NZ, 8, LANES), AXIS, s...]
    ppermute x22 -> x21, starting transfers between devices: 26.4 us -> 25.1 us  [shift(): return lax.ppermute(array, AXIS, pairs)]
  transfers between devices with their start and end apart: 23 -> 22, of which waited for: 13 -> 11; matrix products, arithmetic and copies ran while one was open for 3% -> 3% of each run, Pallas kernels for 3% -> 6%
where the time goes in v3:
time: 124 us
  blocking collectives  37.7 us (30%)
  waiting for transfers between devices  35.6 us (29%)
  starting transfers between devices  32.4 us (26%)
  Pallas kernels  11.4 us (9%)
  local copies, waits for them, and re-layouts  2.57 us (2%)
  between operations  2.22 us (2%)
  other arithmetic  1.86 us (2%)
    ppermute x21, waiting for transfers between devices, shift(): return lax.ppermute(array, AXIS, pairs)  29.7 us
    ppermute x21, starting transfers between devices, shift(): return lax.ppermute(array, AXIS, pairs)  25.1 us
    all_to_all x1, blocking collectives, per_device(): lax.all_to_all(jnp.broadcast_to(packed[:, None], (256, 1, 128)), AXIS, sp...  19.3 us
    all_to_all x1, blocking collectives, per_device(): lax.all_to_all(column_sum.astype(bf16).reshape(2 * NZ, 8, LANES), AXIS, s...  18.4 us
    pallas_call x9, Pallas kernels, call(): pl.pallas_call(kernel, in_specs=[SMEM] * len(scalars) + [VMEM] * len(arra...  11.4 us
    all_to_all x1, starting transfers between devices, per_device(): lax.all_to_all(spread, AXIS, split_axis=0, concat_axis=0, tiled=True, axi...  7.31 us
    all_to_all x1, waiting for transfers between devices, per_device(): lax.all_to_all(spread, AXIS, split_axis=0, concat_axis=0, tiled=True, axi...  5.92 us
  transfers between devices with their start and end apart: 22, of which 11 were waited for; matrix products, arithmetic and copies ran while one was open for 3% of the time, Pallas kernels for 6%

profile of v3, /device:TPU:1, one launch (start us, length us, event | category | flops | bytes accessed | tf_op | source)
XLA Modules:
  0.0 123.7 jit_solution(8304331633072286386)
XLA Ops:
  1.3 3.3 %collective-permute-start.1 = (f32[8,128]{1,0:T(8,128)S(1)}, f32[8,128]{1,0:T(8,128)S(1)}, u32[]{:S(2)}, u32[]{:S(2)}) collective-permute-start(f32[8,128]{1,0:T(8,128)S(1)} %broadcast_in_dim.14), channel_id=1, source_target_pairs={{0,1},{1,0},{2,3},{3,2},{4,5},{5,4},{6,7},{7,6},{8,9},{9,8},{10,11... | collective-permute-start | bytes 12296 | tf_op jit(solution)/shard_map/ppermute | solution.py:53
  6.1 7.3 %all-to-all-start = ((bf16[16,8,640]{2,1,0:T(8,128)(2,1)}), bf16[16,8,640]{2,1,0:T(8,128)(2,1)S(1)}, u32[]{:S(2)}, u32[]{:S(2)}) async-start(bf16[16,8,640]{2,1,0:T(8,128)(2,1)} %shard_map.158), calls=%async_computation | async-start | bytes 327680 | tf_op jit(solution)/shard_map/all_to_all | solution.py:380
  17.1 5.9 %all-to-all-done = bf16[16,8,640]{2,1,0:T(8,128)(2,1)S(1)} async-done(((bf16[16,8,640]{2,1,0:T(8,128)(2,1)}), bf16[16,8,640]{2,1,0:T(8,128)(2,1)S(1)}, u32[]{:S(2)}, u32[]{:S(2)}) %all-to-all-start) | async-done | bytes 163872 | tf_op jit(solution)/shard_map/all_to_all | solution.py:380
  23.0 2.9 %collective-permute-start.4 = (bf16[128,640]{1,0:T(8,128)(2,1)S(1)}, bf16[128,640]{1,0:T(8,128)(2,1)S(1)}, u32[]{:S(2)}, u32[]{:S(2)}) collective-permute-start(bf16[128,640]{1,0:T(8,128)(2,1)S(1)} %bitcast.11), channel_id=1, source_target_pairs={{0,32},{16,48},{32,0},{48,16},{2,34},{18,50},{34,2},{50,18},{4,36}... | collective-permute-start | bytes 491528 | tf_op jit(solution)/shard_map/ppermute | solution.py:53
  27.5 1.4 %collective-permute-done.4 = bf16[128,640]{1,0:T(8,128)(2,1)S(1)} collective-permute-done((bf16[128,640]{1,0:T(8,128)(2,1)S(1)}, bf16[128,640]{1,0:T(8,128)(2,1)S(1)}, u32[]{:S(2)}, u32[]{:S(2)}) %collective-permute-start.4) | collective-permute-done | bytes 163872 | tf_op jit(solution)/shard_map/ppermute | solution.py:53
  29.0 2.1 %collective-permute-done.5 = bf16[128,640]{1,0:T(8,128)(2,1)S(1)} collective-permute-done((bf16[128,640]{1,0:T(8,128)(2,1)S(1)}, bf16[128,640]{1,0:T(8,128)(2,1)S(1)}, u32[]{:S(2)}, u32[]{:S(2)}) %collective-permute-start.5) | collective-permute-done | bytes 163872 | tf_op jit(solution)/shard_map/ppermute | solution.py:53
  31.0 2.5 %collective-permute-start.9 = (bf16[256,640]{1,0:T(8,128)(2,1)S(1)}, bf16[256,640]{1,0:T(8,128)(2,1)S(1)}, u32[]{:S(2)}, u32[]{:S(2)}) collective-permute-start(bf16[256,640]{1,0:T(8,128)(2,1)S(1)} %constant_dynamic-update-slice_fusion.2.refs_1_.plane_b), channel_id=1, source_target_pairs={{0,192},{64,0},{128,64},{192,128},{2,194},{66,2},{130,66},{194,130... | collective-permute-start | bytes 983048 | tf_op jit(solution)/shard_map/ppermute | solution.py:53
  34.3 1.4 %collective-permute-start.12 = (bf16[128,512]{1,0:T(8,128)(2,1)S(1)}, bf16[128,512]{1,0:T(8,128)(2,1)S(1)}, u32[]{:S(2)}, u32[]{:S(2)}) collective-permute-start(bf16[128,512]{1,0:T(8,128)(2,1)S(1)} %get-tuple-element.39), channel_id=1, source_target_pairs={{0,1},{1,0},{2,3},{3,2},{4,5},{5,4},{6,7},{7,6},{8,9},{9,8},{10,11... | collective-permute-start | bytes 393224 | tf_op jit(solution)/shard_map/ppermute | solution.py:53
  35.7 2.3 %collective-permute-start.8 = (bf16[256,640]{1,0:T(8,128)(2,1)S(1)}, bf16[256,640]{1,0:T(8,128)(2,1)S(1)}, u32[]{:S(2)}, u32[]{:S(2)}) collective-permute-start(bf16[256,640]{1,0:T(8,128)(2,1)S(1)} %constant_dynamic-update-slice_fusion.refs_0_.plane_a), channel_id=1, source_target_pairs={{0,192},{64,0},{128,64},{192,128},{2,194},{66,2},{130,66},{194,130... | collective-permute-start | bytes 983048 | tf_op jit(solution)/shard_map/ppermute | solution.py:53
  39.9 7.3 %collective-permute-done.6.refs_2_ = bf16[256,640]{1,0:T(8,128)(2,1)S(1)} collective-permute-done((bf16[256,640]{1,0:T(8,128)(2,1)S(1)}, bf16[256,640]{1,0:T(8,128)(2,1)S(1)}, u32[]{:S(2)}, u32[]{:S(2)}) %collective-permute-start.6) | collective-permute-done | bytes 327712 | tf_op jit(solution)/shard_map/ppermute | solution.py:53
  47.3 1.5 %collective-permute-start.10 = (bf16[256,640]{1,0:T(8,128)(2,1)S(1)}, bf16[256,640]{1,0:T(8,128)(2,1)S(1)}, u32[]{:S(2)}, u32[]{:S(2)}) collective-permute-start(bf16[256,640]{1,0:T(8,128)(2,1)S(1)} %collective-permute-done.6.refs_2_), channel_id=1, source_target_pairs={{0,64},{64,128},{128,192},{192,0},{2,66},{66,130},{130,194},{194,2... | collective-permute-start | bytes 983048 | tf_op jit(solution)/shard_map/ppermute | solution.py:53
  49.7 3.8 %collective-permute-done.11.far_b = bf16[256,640]{1,0:T(8,128)(2,1)S(1)} collective-permute-done((bf16[256,640]{1,0:T(8,128)(2,1)S(1)}, bf16[256,640]{1,0:T(8,128)(2,1)S(1)}, u32[]{:S(2)}, u32[]{:S(2)}) %collective-permute-start.11) | collective-permute-done | bytes 327712 | tf_op jit(solution)/shard_map/ppermute | solution.py:53
  54.7 4.0 %shard_map.160.down = bf16[256,640]{1,0:T(8,128)(2,1)S(1)} custom-call(s32[2]{0:T(128)S(1)} %pad_add_fusion.members, bf16[256,512]{1,0:T(8,128)(2,1)S(1)} %get-tuple-element.22.scaled2, f32[256,640]{1,0:T(8,128)S(1)} %shard_map.159.partial, bf16[256,640]{1,0:T(8,128)(2,1)S(1)} %collective-permute-done.10.far_a, ...), custom_call_target="tpu_custom_call" | custom-call | tf_op jit(solution)/shard_map/pallas_call | solution.py:312
  59.3 2.1 %collective-permute-start.13 = (bf16[256,640]{1,0:T(8,128)(2,1)S(1)}, bf16[256,640]{1,0:T(8,128)(2,1)S(1)}, u32[]{:S(2)}, u32[]{:S(2)}) collective-permute-start(bf16[256,640]{1,0:T(8,128)(2,1)S(1)} %shard_map.160.down), channel_id=1, source_target_pairs={{0,192},{64,0},{128,64},{192,128},{2,194},{66,2},{130,66},{194,130... | collective-permute-start | bytes 983048 | tf_op jit(solution)/shard_map/ppermute | solution.py:53
  61.4 2.7 %collective-permute-start.2 = (bf16[256,512]{1,0:T(8,128)(2,1)S(1)}, bf16[256,512]{1,0:T(8,128)(2,1)S(1)}, u32[]{:S(2)}, u32[]{:S(2)}) collective-permute-start(bf16[256,512]{1,0:T(8,128)(2,1)S(1)} %get-tuple-element.21.scaled1), channel_id=1, source_target_pairs={{0,192},{64,0},{128,64},{192,128},{2,194},{66,2},{130,66},{194,130... | collective-permute-start | bytes 786440 | tf_op jit(solution)/shard_map/ppermute | solution.py:53
  64.8 1.7 %collective-permute-done.17.down = bf16[256,640]{1,0:T(8,128)(2,1)S(1)} collective-permute-done((bf16[256,640]{1,0:T(8,128)(2,1)S(1)}, bf16[256,640]{1,0:T(8,128)(2,1)S(1)}, u32[]{:S(2)}, u32[]{:S(2)}) %collective-permute-start.17) | collective-permute-done | bytes 327712 | tf_op jit(solution)/shard_map/ppermute | solution.py:53
  67.1 5.7 %collective-permute-done.14.scaled3 = bf16[256,512]{1,0:T(8,128)(2,1)S(1)} collective-permute-done((bf16[256,512]{1,0:T(8,128)(2,1)S(1)}, bf16[256,512]{1,0:T(8,128)(2,1)S(1)}, u32[]{:S(2)}, u32[]{:S(2)}) %collective-permute-start.14) | collective-permute-done | bytes 262176 | tf_op jit(solution)/shard_map/ppermute | solution.py:53
  72.8 1.6 %shard_map.163 = (f32[128,640]{1,0:T(8,128)S(1)}, bf16[128,640]{1,0:T(8,128)(2,1)S(1)}, bf16[128,640]{1,0:T(8,128)(2,1)S(1)}, bf16[128,640]{1,0:T(8,128)(2,1)S(1)}) custom-call(s32[16]{0:T(128)S(1)} %fusion.4.tile_of, bf16[256,512]{1,0:T(8,128)(2,1)S(1)} %collective-permute-done.2.scaled1, bf16[256,640]{1,0:T(8,128)(2,1)S(1)} %collective-permute-done.13.down1, ...), custom_call_target="tpu_custom_call" | custom-call | tf_op jit(solution)/shard_map/pallas_call | solution.py:312
  74.5 2.3 %collective-permute-start.18 = (bf16[128,640]{1,0:T(8,128)(2,1)S(1)}, bf16[128,640]{1,0:T(8,128)(2,1)S(1)}, u32[]{:S(2)}, u32[]{:S(2)}) collective-permute-start(bf16[128,640]{1,0:T(8,128)(2,1)S(1)} %get-tuple-element.34), channel_id=1, source_target_pairs={{0,48},{16,0},{32,16},{48,32},{2,50},{18,2},{34,18},{50,34},{4,52}... | collective-permute-start | bytes 491528 | tf_op jit(solution)/shard_map/ppermute | solution.py:53
  77.5 3.3 %collective-permute-done.18 = bf16[128,640]{1,0:T(8,128)(2,1)S(1)} collective-permute-done((bf16[128,640]{1,0:T(8,128)(2,1)S(1)}, bf16[128,640]{1,0:T(8,128)(2,1)S(1)}, u32[]{:S(2)}, u32[]{:S(2)}) %collective-permute-start.18) | collective-permute-done | bytes 163872 | tf_op jit(solution)/shard_map/ppermute | solution.py:53
  80.8 1.8 %collective-permute-done.19 = bf16[128,640]{1,0:T(8,128)(2,1)S(1)} collective-permute-done((bf16[128,640]{1,0:T(8,128)(2,1)S(1)}, bf16[128,640]{1,0:T(8,128)(2,1)S(1)}, u32[]{:S(2)}, u32[]{:S(2)}) %collective-permute-start.19) | collective-permute-done | bytes 163872 | tf_op jit(solution)/shard_map/ppermute | solution.py:53
  84.0 18.4 %all_to_all.15.pieces = bf16[16,8,640]{2,1,0:T(8,128)(2,1)S(1)} all-to-all(bf16[16,8,640]{2,1,0:T(8,128)(2,1)S(1)} %fusion), channel_id=1, replica_groups={{0,1,2,3,4,5,6,7,8,9,10,11,12,13,14,15},{16,17,18,19,20,21,22,23,24,25,..., dimensions={0} | all-to-all | bytes 327680 | tf_op jit(solution)/shard_map/all_to_all | solution.py:452
  102.7 19.3 %all_to_all.16 = f32[256,1,128]{2,1,0:T(1,128)S(1)} all-to-all(f32[256,1,128]{2,1,0:T(1,128)S(1)} %broadcast_in_dim.17), channel_id=1, replica_groups=mesh['fsdp'=256] {'fsdp'}, dimensions={0} | all-to-all | bytes 262144 | tf_op jit(solution)/shard_map/all_to_all | solution.py:463
  122.1 1.6 %shard_map.165 = (f32[8,1152]{1,0:T(8,128)}, f32[4,2048]{1,0:T(4,128)}, f32[4,1152]{1,0:T(4,128)}) custom-call(f32[256,128]{1,0:T(8,128)S(1)} %bitcast.8, f32[8,1152]{1,0:T(8,128)S(1)} %get-tuple-element.38.grad_rows, f32[8,1152]{1,0:T(8,128)S(1)} %copy-done.1, f32[8,1152]{1,0:T(8,128)S(1)} %copy-done.2, f32[4,2048]{1,0:T(4,128)S(1)} %copy-done.3, ...), custom_call_target="tpu_custom_call" | custom-call | tf_op jit(solution)/shard_map/pallas_call | solution.py:312
  (83 shorter events, 15.3 us)
Async XLA Ops:
  1.3 13.6 %collective-permute-start.1 = (f32[8,128]{1,0:T(8,128)S(1)}, f32[8,128]{1,0:T(8,128)S(1)}, u32[]{:S(2)}, u32[]{:S(2)}) collective-permute-start(f32[8,128]{1,0:T(8,128)S(1)} %broadcast_in_dim.14), channel_id=1, source_target_pairs={{0,1},{1,0},{2,3},{3,2},{4,5},{5,4},{6,7},{7,6},{8,9},{9,8},{10,11... | collective-permute-start | bytes 12296 | tf_op jit(solution)/shard_map/ppermute | solution.py:53
  4.6 31.1 %collective-permute-start = (bf16[128,2048]{1,0:T(8,128)(2,1)}, bf16[128,2048]{1,0:T(8,128)(2,1)S(1)}, u32[]{:S(2)}, u32[]{:S(2)}) collective-permute-start(bf16[128,2048]{1,0:T(8,128)(2,1)} %own.1), channel_id=1, source_target_pairs={{0,1},{1,0},{2,3},{3,2},{4,5},{5,4},{6,7},{7,6},{8,9},{9,8},{10,11... | collective-permute-start | bytes 1572872 | tf_op jit(solution)/shard_map/ppermute | solution.py:53
  6.1 16.8 %all-to-all-start = ((bf16[16,8,640]{2,1,0:T(8,128)(2,1)}), bf16[16,8,640]{2,1,0:T(8,128)(2,1)S(1)}, u32[]{:S(2)}, u32[]{:S(2)}) async-start(bf16[16,8,640]{2,1,0:T(8,128)(2,1)} %shard_map.158), calls=%async_computation | async-start | bytes 327680 | tf_op jit(solution)/shard_map/all_to_all | solution.py:380
  23.0 6.0 %collective-permute-start.4 = (bf16[128,640]{1,0:T(8,128)(2,1)S(1)}, bf16[128,640]{1,0:T(8,128)(2,1)S(1)}, u32[]{:S(2)}, u32[]{:S(2)}) collective-permute-start(bf16[128,640]{1,0:T(8,128)(2,1)S(1)} %bitcast.11), channel_id=1, source_target_pairs={{0,32},{16,48},{32,0},{48,16},{2,34},{18,50},{34,2},{50,18},{4,36}... | collective-permute-start | bytes 491528 | tf_op jit(solution)/shard_map/ppermute | solution.py:53
  26.0 5.1 %collective-permute-start.5 = (bf16[128,640]{1,0:T(8,128)(2,1)S(1)}, bf16[128,640]{1,0:T(8,128)(2,1)S(1)}, u32[]{:S(2)}, u32[]{:S(2)}) collective-permute-start(bf16[128,640]{1,0:T(8,128)(2,1)S(1)} %bitcast.12), channel_id=1, source_target_pairs={{0,48},{16,0},{32,16},{48,32},{2,50},{18,2},{34,18},{50,34},{4,52}... | collective-permute-start | bytes 491528 | tf_op jit(solution)/shard_map/ppermute | solution.py:53
  26.8 6.8 %collective-permute-start.3 = (bf16[128,640]{1,0:T(8,128)(2,1)S(1)}, bf16[128,640]{1,0:T(8,128)(2,1)S(1)}, u32[]{:S(2)}, u32[]{:S(2)}) collective-permute-start(bf16[128,640]{1,0:T(8,128)(2,1)S(1)} %bitcast.14), channel_id=1, source_target_pairs={{0,16},{16,32},{32,48},{48,0},{2,18},{18,34},{34,50},{50,2},{4,20}... | collective-permute-start | bytes 491528 | tf_op jit(solution)/shard_map/ppermute | solution.py:53
  31.0 8.1 %collective-permute-start.9 = (bf16[256,640]{1,0:T(8,128)(2,1)S(1)}, bf16[256,640]{1,0:T(8,128)(2,1)S(1)}, u32[]{:S(2)}, u32[]{:S(2)}) collective-permute-start(bf16[256,640]{1,0:T(8,128)(2,1)S(1)} %constant_dynamic-update-slice_fusion.2.refs_1_.plane_b), channel_id=1, source_target_pairs={{0,192},{64,0},{128,64},{192,128},{2,194},{66,2},{130,66},{194,130... | collective-permute-start | bytes 983048 | tf_op jit(solution)/shard_map/ppermute | solution.py:53
  33.5 13.8 %collective-permute-start.7 = (bf16[256,640]{1,0:T(8,128)(2,1)S(1)}, bf16[256,640]{1,0:T(8,128)(2,1)S(1)}, u32[]{:S(2)}, u32[]{:S(2)}) collective-permute-start(bf16[256,640]{1,0:T(8,128)(2,1)S(1)} %constant_dynamic-update-slice_fusion.2.refs_1_.plane_b), channel_id=1, source_target_pairs={{0,64},{64,128},{128,192},{192,0},{2,66},{66,130},{130,194},{194,2... | collective-permute-start | bytes 983048 | tf_op jit(solution)/shard_map/ppermute | solution.py:53
  33.5 13.7 %collective-permute-start.6 = (bf16[256,640]{1,0:T(8,128)(2,1)S(1)}, bf16[256,640]{1,0:T(8,128)(2,1)S(1)}, u32[]{:S(2)}, u32[]{:S(2)}) collective-permute-start(bf16[256,640]{1,0:T(8,128)(2,1)S(1)} %constant_dynamic-update-slice_fusion.refs_0_.plane_a), channel_id=1, source_target_pairs={{0,64},{64,128},{128,192},{192,0},{2,66},{66,130},{130,194},{194,2... | collective-permute-start | bytes 983048 | tf_op jit(solution)/shard_map/ppermute | solution.py:53
  34.3 15.4 %collective-permute-start.12 = (bf16[128,512]{1,0:T(8,128)(2,1)S(1)}, bf16[128,512]{1,0:T(8,128)(2,1)S(1)}, u32[]{:S(2)}, u32[]{:S(2)}) collective-permute-start(bf16[128,512]{1,0:T(8,128)(2,1)S(1)} %get-tuple-element.39), channel_id=1, source_target_pairs={{0,1},{1,0},{2,3},{3,2},{4,5},{5,4},{6,7},{7,6},{8,9},{9,8},{10,11... | collective-permute-start | bytes 393224 | tf_op jit(solution)/shard_map/ppermute | solution.py:53
  35.7 13.2 %collective-permute-start.8 = (bf16[256,640]{1,0:T(8,128)(2,1)S(1)}, bf16[256,640]{1,0:T(8,128)(2,1)S(1)}, u32[]{:S(2)}, u32[]{:S(2)}) collective-permute-start(bf16[256,640]{1,0:T(8,128)(2,1)S(1)} %constant_dynamic-update-slice_fusion.refs_0_.plane_a), channel_id=1, source_target_pairs={{0,192},{64,0},{128,64},{192,128},{2,194},{66,2},{130,66},{194,130... | collective-permute-start | bytes 983048 | tf_op jit(solution)/shard_map/ppermute | solution.py:53
  39.2 22.3 %collective-permute-start.16 = (bf16[256,512]{1,0:T(8,128)(2,1)S(1)}, bf16[256,512]{1,0:T(8,128)(2,1)S(1)}, u32[]{:S(2)}, u32[]{:S(2)}) collective-permute-start(bf16[256,512]{1,0:T(8,128)(2,1)S(1)} %get-tuple-element.22.scaled2), channel_id=1, source_target_pairs={{0,128},{64,192},{128,0},{192,64},{2,130},{66,194},{130,2},{194,66... | collective-permute-start | bytes 786440 | tf_op jit(solution)/shard_map/ppermute | solution.py:53
  47.3 6.2 %collective-permute-start.11 = (bf16[256,640]{1,0:T(8,128)(2,1)S(1)}, bf16[256,640]{1,0:T(8,128)(2,1)S(1)}, u32[]{:S(2)}, u32[]{:S(2)}) collective-permute-start(bf16[256,640]{1,0:T(8,128)(2,1)S(1)} %collective-permute-done.9.refs_5_), channel_id=1, source_target_pairs={{0,192},{64,0},{128,64},{192,128},{2,194},{66,2},{130,66},{194,130... | collective-permute-start | bytes 983048 | tf_op jit(solution)/shard_map/ppermute | solution.py:53
  47.3 7.4 %collective-permute-start.10 = (bf16[256,640]{1,0:T(8,128)(2,1)S(1)}, bf16[256,640]{1,0:T(8,128)(2,1)S(1)}, u32[]{:S(2)}, u32[]{:S(2)}) collective-permute-start(bf16[256,640]{1,0:T(8,128)(2,1)S(1)} %collective-permute-done.6.refs_2_), channel_id=1, source_target_pairs={{0,64},{64,128},{128,192},{192,0},{2,66},{66,130},{130,194},{194,2... | collective-permute-start | bytes 983048 | tf_op jit(solution)/shard_map/ppermute | solution.py:53
  58.7 7.8 %collective-permute-start.17 = (bf16[256,640]{1,0:T(8,128)(2,1)S(1)}, bf16[256,640]{1,0:T(8,128)(2,1)S(1)}, u32[]{:S(2)}, u32[]{:S(2)}) collective-permute-start(bf16[256,640]{1,0:T(8,128)(2,1)S(1)} %shard_map.160.down), channel_id=1, source_target_pairs={{0,128},{64,192},{128,0},{192,64},{2,130},{66,194},{130,2},{194,66... | collective-permute-start | bytes 983048 | tf_op jit(solution)/shard_map/ppermute | solution.py:53
  59.3 13.5 %collective-permute-start.13 = (bf16[256,640]{1,0:T(8,128)(2,1)S(1)}, bf16[256,640]{1,0:T(8,128)(2,1)S(1)}, u32[]{:S(2)}, u32[]{:S(2)}) collective-permute-start(bf16[256,640]{1,0:T(8,128)(2,1)S(1)} %shard_map.160.down), channel_id=1, source_target_pairs={{0,192},{64,0},{128,64},{192,128},{2,194},{66,2},{130,66},{194,130... | collective-permute-start | bytes 983048 | tf_op jit(solution)/shard_map/ppermute | solution.py:53
  61.4 11.4 %collective-permute-start.15 = (bf16[256,640]{1,0:T(8,128)(2,1)S(1)}, bf16[256,640]{1,0:T(8,128)(2,1)S(1)}, u32[]{:S(2)}, u32[]{:S(2)}) collective-permute-start(bf16[256,640]{1,0:T(8,128)(2,1)S(1)} %shard_map.160.down), channel_id=1, source_target_pairs={{0,64},{64,128},{128,192},{192,0},{2,66},{66,130},{130,194},{194,2... | collective-permute-start | bytes 983048 | tf_op jit(solution)/shard_map/ppermute | solution.py:53
  61.4 11.4 %collective-permute-start.14 = (bf16[256,512]{1,0:T(8,128)(2,1)S(1)}, bf16[256,512]{1,0:T(8,128)(2,1)S(1)}, u32[]{:S(2)}, u32[]{:S(2)}) collective-permute-start(bf16[256,512]{1,0:T(8,128)(2,1)S(1)} %get-tuple-element.24.scaled3), channel_id=1, source_target_pairs={{0,64},{64,128},{128,192},{192,0},{2,66},{66,130},{130,194},{194,2... | collective-permute-start | bytes 786440 | tf_op jit(solution)/shard_map/ppermute | solution.py:53
  61.4 11.4 %collective-permute-start.2 = (bf16[256,512]{1,0:T(8,128)(2,1)S(1)}, bf16[256,512]{1,0:T(8,128)(2,1)S(1)}, u32[]{:S(2)}, u32[]{:S(2)}) collective-permute-start(bf16[256,512]{1,0:T(8,128)(2,1)S(1)} %get-tuple-element.21.scaled1), channel_id=1, source_target_pairs={{0,192},{64,0},{128,64},{192,128},{2,194},{66,2},{130,66},{194,130... | collective-permute-start | bytes 786440 | tf_op jit(solution)/shard_map/ppermute | solution.py:53
  74.5 47.6 %copy-start.1 = (f32[8,1152]{1,0:T(8,128)S(1)}, f32[8,1152]{1,0:T(8,128)}, u32[]{:S(2)}) copy-start(f32[8,1152]{1,0:T(8,128)} %weight_first.1) | copy-start | bytes 110596
  74.5 47.6 %copy-start.2 = (f32[8,1152]{1,0:T(8,128)S(1)}, f32[8,1152]{1,0:T(8,128)}, u32[]{:S(2)}) copy-start(f32[8,1152]{1,0:T(8,128)} %weight_second.1) | copy-start | bytes 110596
  74.5 6.3 %collective-permute-start.18 = (bf16[128,640]{1,0:T(8,128)(2,1)S(1)}, bf16[128,640]{1,0:T(8,128)(2,1)S(1)}, u32[]{:S(2)}, u32[]{:S(2)}) collective-permute-start(bf16[128,640]{1,0:T(8,128)(2,1)S(1)} %get-tuple-element.34), channel_id=1, source_target_pairs={{0,48},{16,0},{32,16},{48,32},{2,50},{18,2},{34,18},{50,34},{4,52}... | collective-permute-start | bytes 491528 | tf_op jit(solution)/shard_map/ppermute | solution.py:53
  76.8 5.8 %collective-permute-start.19 = (bf16[128,640]{1,0:T(8,128)(2,1)S(1)}, bf16[128,640]{1,0:T(8,128)(2,1)S(1)}, u32[]{:S(2)}, u32[]{:S(2)}) collective-permute-start(bf16[128,640]{1,0:T(8,128)(2,1)S(1)} %get-tuple-element.35), channel_id=1, source_target_pairs={{0,32},{16,48},{32,0},{48,16},{2,34},{18,50},{34,2},{50,18},{4,36}... | collective-permute-start | bytes 491528 | tf_op jit(solution)/shard_map/ppermute | solution.py:53
  76.8 7.1 %collective-permute-start.20 = (bf16[128,640]{1,0:T(8,128)(2,1)S(1)}, bf16[128,640]{1,0:T(8,128)(2,1)S(1)}, u32[]{:S(2)}, u32[]{:S(2)}) collective-permute-start(bf16[128,640]{1,0:T(8,128)(2,1)S(1)} %get-tuple-element.36), channel_id=1, source_target_pairs={{0,16},{16,32},{32,48},{48,0},{2,18},{18,34},{34,50},{50,2},{4,20}... | collective-permute-start | bytes 491528 | tf_op jit(solution)/shard_map/ppermute | solution.py:53
  (10 other events, 323.1 us)

commit v4 on v3

--- a/solution.py
+++ b/solution.py
@@ -206,12 +206,11 @@
 
 
 def last_kernel(
-    tile_of, scaled1, down1, scaled3, down3, plane_a, plane_b, grads_in, totals_in, tails_in, rates, *parts
+    tile_of, scaled, down, plane_a, plane_b, grads_in, totals_in, tails_in, rates, *parts
 ):
     total = (grads_in[...], totals_in[...], None)
-    total = weight_terms(scaled1[...], down1[...], (plane_a, plane_b), total)
-    grads, totals, _ = weight_terms(scaled3[...], down3[...], (plane_a, plane_b), total)
-    tails = tails_in[...] + down1[:SEQ, 512:].astype(f32) + down3[:SEQ, 512:].astype(f32)
+    grads, totals, _ = weight_terms(scaled[...], down[...], (plane_a, plane_b), total)
+    tails = tails_in[...] + down[:SEQ, 512:].astype(f32)
     tails = tails + pltpu.roll(tails, 108, 1)
     lane = lax.broadcasted_iota(jnp.int32, (SEQ, 128), 1)
     for i, result in enumerate(parts):
@@ -380,7 +379,9 @@
     column = lax.all_to_all(
         spread, AXIS, split_axis=0, concat_axis=0, tiled=True, axis_index_groups=COLUMNS
     ).reshape(NZ * 16, LANES)
-    column, cotangent = lax.optimization_barrier((column, cotangent))
+    column, tokens, cotangent, member_ids = lax.optimization_barrier(
+        (column, tokens, cotangent, member_ids)
+    )
     others = [shift(column, INNER_RINGS, j) for j in (1, 2, 3)]
     plane_a = jnp.concatenate([column, others[0]], axis=0)
     plane_b = jnp.concatenate(others[1:], axis=0)
@@ -440,11 +441,13 @@
         jax.ShapeDtypeStruct((SEQ, 128), f32),
     ]
     near = call(near_kernel, [], [scaled[0], down, plane_a, plane_b], sums)
-    middle = call(middle_kernel, [], [far_scaled[1], down_of[1], plane_a, plane_b, *near], sums)
+    middle = near
+    for j in (2, 3):
+        middle = call(middle_kernel, [], [far_scaled[j - 1], down_of[j - 1], plane_a, plane_b, *middle], sums)
     parts = call(
         last_kernel,
         [tile_of],
-        [far_scaled[0], down_of[0], far_scaled[2], down_of[2], plane_a, plane_b, *middle, factors],
+        [far_scaled[0], down_of[0], plane_a, plane_b, *middle, factors],
         [jax.ShapeDtypeStruct((SEQ, LANES), f32)] + [jax.ShapeDtypeStruct((SEQ, LANES), bf16)] * 3,
     )
     got = [shift(parts[j], INNER_RINGS, -j) for j in (1, 2, 3)]

time: 124 us -> 118 us (0.952)
  blocking collectives: 37.7 us -> 32.6 us
  waiting for transfers between devices: 35.6 us -> 34 us
    all_to_all x1, blocking collectives: 18.4 us -> 15.1 us  [per_device(): lax.all_to_all(column_sum.astype(bf16).reshape(2 * NZ, 8, LANES), AXIS, s...]
    all_to_all x1, starting transfers between devices: 7.31 us -> 10.1 us  [per_device(): lax.all_to_all(spread, AXIS, split_axis=0, concat_axis=0, tiled=True, axi...]
    ppermute x21, starting transfers between devices: 25.1 us -> 22.7 us  [shift(): return lax.ppermute(array, AXIS, pairs)]
    all_to_all x1, blocking collectives: 19.3 us -> 17.5 us  [per_device(): lax.all_to_all(jnp.broadcast_to(packed[:, None], (256, 1, 128)), AXIS, sp...]
    pallas_call x9 -> x10, Pallas kernels: 11.4 us -> 11.5 us  [call(): pl.pallas_call(kernel, in_specs=[SMEM] * len(scalars) + [VMEM] * len(arra...]
  transfers between devices with their start and end apart: 22 -> 22, of which waited for: 11 -> 12; matrix products, arithmetic and copies ran while one was open for 3% -> 3% of each run, Pallas kernels for 6% -> 7%
where the time goes in v4:
time: 118 us
  waiting for transfers between devices  34 us (29%)
  starting transfers between devices  32.8 us (28%)
  blocking collectives  32.6 us (28%)
  Pallas kernels  11.5 us (10%)
  local copies, waits for them, and re-layouts  2.62 us (2%)
  between operations  2.27 us (2%)
  other arithmetic  1.86 us (2%)
    ppermute x21, waiting for transfers between devices, shift(): return lax.ppermute(array, AXIS, pairs)  29 us
    ppermute x21, starting transfers between devices, shift(): return lax.ppermute(array, AXIS, pairs)  22.7 us
    all_to_all x1, blocking collectives, per_device(): lax.all_to_all(jnp.broadcast_to(packed[:, None], (256, 1, 128)), AXIS, sp...  17.5 us
    all_to_all x1, blocking collectives, per_device(): lax.all_to_all(column_sum.astype(bf16).reshape(2 * NZ, 8, LANES), AXIS, s...  15.1 us
    pallas_call x10, Pallas kernels, call(): pl.pallas_call(kernel, in_specs=[SMEM] * len(scalars) + [VMEM] * len(arra...  11.5 us
    all_to_all x1, starting transfers between devices, per_device(): lax.all_to_all(spread, AXIS, split_axis=0, concat_axis=0, tiled=True, axi...  10.1 us
    all_to_all x1, waiting for transfers between devices, per_device(): lax.all_to_all(spread, AXIS, split_axis=0, concat_axis=0, tiled=True, axi...  5.09 us
  transfers between devices with their start and end apart: 22, of which 12 were waited for; matrix products, arithmetic and copies ran while one was open for 3% of the time, Pallas kernels for 7%

profile of v4, /device:TPU:1, one launch (start us, length us, event | category | flops | bytes accessed | tf_op | source)
XLA Modules:
  0.0 117.7 jit_solution(1479083465339526260)
XLA Ops:
  2.2 10.1 %all-to-all-start = ((bf16[16,8,640]{2,1,0:T(8,128)(2,1)}), bf16[16,8,640]{2,1,0:T(8,128)(2,1)S(1)}, u32[]{:S(2)}, u32[]{:S(2)}) async-start(bf16[16,8,640]{2,1,0:T(8,128)(2,1)} %shard_map.157), calls=%async_computation | async-start | bytes 327680 | tf_op jit(solution)/shard_map/all_to_all | solution.py:379
  16.7 5.1 %all-to-all-done = bf16[16,8,640]{2,1,0:T(8,128)(2,1)S(1)} async-done(((bf16[16,8,640]{2,1,0:T(8,128)(2,1)}), bf16[16,8,640]{2,1,0:T(8,128)(2,1)S(1)}, u32[]{:S(2)}, u32[]{:S(2)}) %all-to-all-start) | async-done | bytes 163872 | tf_op jit(solution)/shard_map/all_to_all | solution.py:379
  21.8 2.9 %collective-permute-start.4 = (bf16[128,640]{1,0:T(8,128)(2,1)S(1)}, bf16[128,640]{1,0:T(8,128)(2,1)S(1)}, u32[]{:S(2)}, u32[]{:S(2)}) collective-permute-start(bf16[128,640]{1,0:T(8,128)(2,1)S(1)} %bitcast.11), channel_id=1, source_target_pairs={{0,32},{16,48},{32,0},{48,16},{2,34},{18,50},{34,2},{50,18},{4,36}... | collective-permute-start | bytes 491528 | tf_op jit(solution)/shard_map/ppermute | solution.py:53
  27.8 2.1 %collective-permute-done.5 = bf16[128,640]{1,0:T(8,128)(2,1)S(1)} collective-permute-done((bf16[128,640]{1,0:T(8,128)(2,1)S(1)}, bf16[128,640]{1,0:T(8,128)(2,1)S(1)}, u32[]{:S(2)}, u32[]{:S(2)}) %collective-permute-start.5) | collective-permute-done | bytes 163872 | tf_op jit(solution)/shard_map/ppermute | solution.py:53
  29.9 2.5 %collective-permute-start.9 = (bf16[256,640]{1,0:T(8,128)(2,1)S(1)}, bf16[256,640]{1,0:T(8,128)(2,1)S(1)}, u32[]{:S(2)}, u32[]{:S(2)}) collective-permute-start(bf16[256,640]{1,0:T(8,128)(2,1)S(1)} %constant_dynamic-update-slice_fusion.2.refs_1_.plane_b), channel_id=1, source_target_pairs={{0,192},{64,0},{128,64},{192,128},{2,194},{66,2},{130,66},{194,130... | collective-permute-start | bytes 983048 | tf_op jit(solution)/shard_map/ppermute | solution.py:53
  33.1 1.4 %collective-permute-start.12 = (bf16[128,512]{1,0:T(8,128)(2,1)S(1)}, bf16[128,512]{1,0:T(8,128)(2,1)S(1)}, u32[]{:S(2)}, u32[]{:S(2)}) collective-permute-start(bf16[128,512]{1,0:T(8,128)(2,1)S(1)} %get-tuple-element.49), channel_id=1, source_target_pairs={{0,1},{1,0},{2,3},{3,2},{4,5},{5,4},{6,7},{7,6},{8,9},{9,8},{10,11... | collective-permute-start | bytes 393224 | tf_op jit(solution)/shard_map/ppermute | solution.py:53
  34.5 1.8 %collective-permute-done.9.refs_5_ = bf16[256,640]{1,0:T(8,128)(2,1)S(1)} collective-permute-done((bf16[256,640]{1,0:T(8,128)(2,1)S(1)}, bf16[256,640]{1,0:T(8,128)(2,1)S(1)}, u32[]{:S(2)}, u32[]{:S(2)}) %collective-permute-start.9) | collective-permute-done | bytes 327712 | tf_op jit(solution)/shard_map/ppermute | solution.py:53
  36.3 3.1 %collective-permute-start.8 = (bf16[256,640]{1,0:T(8,128)(2,1)S(1)}, bf16[256,640]{1,0:T(8,128)(2,1)S(1)}, u32[]{:S(2)}, u32[]{:S(2)}) collective-permute-start(bf16[256,640]{1,0:T(8,128)(2,1)S(1)} %constant_dynamic-update-slice_fusion.refs_0_.plane_a), channel_id=1, source_target_pairs={{0,192},{64,0},{128,64},{192,128},{2,194},{66,2},{130,66},{194,130... | collective-permute-start | bytes 983048 | tf_op jit(solution)/shard_map/ppermute | solution.py:53
  39.5 3.8 %collective-permute-done.6.refs_2_ = bf16[256,640]{1,0:T(8,128)(2,1)S(1)} collective-permute-done((bf16[256,640]{1,0:T(8,128)(2,1)S(1)}, bf16[256,640]{1,0:T(8,128)(2,1)S(1)}, u32[]{:S(2)}, u32[]{:S(2)}) %collective-permute-start.6) | collective-permute-done | bytes 327712 | tf_op jit(solution)/shard_map/ppermute | solution.py:53
  43.3 1.5 %collective-permute-start.10 = (bf16[256,640]{1,0:T(8,128)(2,1)S(1)}, bf16[256,640]{1,0:T(8,128)(2,1)S(1)}, u32[]{:S(2)}, u32[]{:S(2)}) collective-permute-start(bf16[256,640]{1,0:T(8,128)(2,1)S(1)} %collective-permute-done.6.refs_2_), channel_id=1, source_target_pairs={{0,64},{64,128},{128,192},{192,0},{2,66},{66,130},{130,194},{194,2... | collective-permute-start | bytes 983048 | tf_op jit(solution)/shard_map/ppermute | solution.py:53
  47.1 2.4 %collective-permute-done.11.far_b = bf16[256,640]{1,0:T(8,128)(2,1)S(1)} collective-permute-done((bf16[256,640]{1,0:T(8,128)(2,1)S(1)}, bf16[256,640]{1,0:T(8,128)(2,1)S(1)}, u32[]{:S(2)}, u32[]{:S(2)}) %collective-permute-start.11) | collective-permute-done | bytes 327712 | tf_op jit(solution)/shard_map/ppermute | solution.py:53
  49.5 4.0 %collective-permute-done.10.far_a = bf16[256,640]{1,0:T(8,128)(2,1)S(1)} collective-permute-done((bf16[256,640]{1,0:T(8,128)(2,1)S(1)}, bf16[256,640]{1,0:T(8,128)(2,1)S(1)}, u32[]{:S(2)}, u32[]{:S(2)}) %collective-permute-start.10) | collective-permute-done | bytes 327712 | tf_op jit(solution)/shard_map/ppermute | solution.py:53
  53.5 3.9 %shard_map.160.down = bf16[256,640]{1,0:T(8,128)(2,1)S(1)} custom-call(s32[2]{0:T(128)S(1)} %pad_add_fusion.members, bf16[256,512]{1,0:T(8,128)(2,1)S(1)} %get-tuple-element.29.scaled2, f32[256,640]{1,0:T(8,128)S(1)} %shard_map.159.partial, bf16[256,640]{1,0:T(8,128)(2,1)S(1)} %collective-permute-done.10.far_a, ...), custom_call_target="tpu_custom_call" | custom-call | tf_op jit(solution)/shard_map/pallas_call | solution.py:311
  57.7 2.7 %collective-permute-start.13 = (bf16[256,640]{1,0:T(8,128)(2,1)S(1)}, bf16[256,640]{1,0:T(8,128)(2,1)S(1)}, u32[]{:S(2)}, u32[]{:S(2)}) collective-permute-start(bf16[256,640]{1,0:T(8,128)(2,1)S(1)} %shard_map.160.down), channel_id=1, source_target_pairs={{0,192},{64,0},{128,64},{192,128},{2,194},{66,2},{130,66},{194,130... | collective-permute-start | bytes 983048 | tf_op jit(solution)/shard_map/ppermute | solution.py:53
  60.3 2.7 %collective-permute-start.2 = (bf16[256,512]{1,0:T(8,128)(2,1)S(1)}, bf16[256,512]{1,0:T(8,128)(2,1)S(1)}, u32[]{:S(2)}, u32[]{:S(2)}) collective-permute-start(bf16[256,512]{1,0:T(8,128)(2,1)S(1)} %get-tuple-element.28.scaled1), channel_id=1, source_target_pairs={{0,192},{64,0},{128,64},{192,128},{2,194},{66,2},{130,66},{194,130... | collective-permute-start | bytes 786440 | tf_op jit(solution)/shard_map/ppermute | solution.py:53
  63.7 1.7 %collective-permute-done.17.down = bf16[256,640]{1,0:T(8,128)(2,1)S(1)} collective-permute-done((bf16[256,640]{1,0:T(8,128)(2,1)S(1)}, bf16[256,640]{1,0:T(8,128)(2,1)S(1)}, u32[]{:S(2)}, u32[]{:S(2)}) %collective-permute-start.17) | collective-permute-done | bytes 327712 | tf_op jit(solution)/shard_map/ppermute | solution.py:53
  66.0 5.4 %collective-permute-done.14.scaled = bf16[256,512]{1,0:T(8,128)(2,1)S(1)} collective-permute-done((bf16[256,512]{1,0:T(8,128)(2,1)S(1)}, bf16[256,512]{1,0:T(8,128)(2,1)S(1)}, u32[]{:S(2)}, u32[]{:S(2)}) %collective-permute-start.14) | collective-permute-done | bytes 262176 | tf_op jit(solution)/shard_map/ppermute | solution.py:53
  73.4 2.3 %collective-permute-start.18 = (bf16[128,640]{1,0:T(8,128)(2,1)S(1)}, bf16[128,640]{1,0:T(8,128)(2,1)S(1)}, u32[]{:S(2)}, u32[]{:S(2)}) collective-permute-start(bf16[128,640]{1,0:T(8,128)(2,1)S(1)} %get-tuple-element.44), channel_id=1, source_target_pairs={{0,48},{16,0},{32,16},{48,32},{2,50},{18,2},{34,18},{50,34},{4,52}... | collective-permute-start | bytes 491528 | tf_op jit(solution)/shard_map/ppermute | solution.py:53
  76.3 3.3 %collective-permute-done.18 = bf16[128,640]{1,0:T(8,128)(2,1)S(1)} collective-permute-done((bf16[128,640]{1,0:T(8,128)(2,1)S(1)}, bf16[128,640]{1,0:T(8,128)(2,1)S(1)}, u32[]{:S(2)}, u32[]{:S(2)}) %collective-permute-start.18) | collective-permute-done | bytes 163872 | tf_op jit(solution)/shard_map/ppermute | solution.py:53
  79.7 1.8 %collective-permute-done.19 = bf16[128,640]{1,0:T(8,128)(2,1)S(1)} collective-permute-done((bf16[128,640]{1,0:T(8,128)(2,1)S(1)}, bf16[128,640]{1,0:T(8,128)(2,1)S(1)}, u32[]{:S(2)}, u32[]{:S(2)}) %collective-permute-start.19) | collective-permute-done | bytes 163872 | tf_op jit(solution)/shard_map/ppermute | solution.py:53
  81.4 1.7 %collective-permute-done.20 = bf16[128,640]{1,0:T(8,128)(2,1)S(1)} collective-permute-done((bf16[128,640]{1,0:T(8,128)(2,1)S(1)}, bf16[128,640]{1,0:T(8,128)(2,1)S(1)}, u32[]{:S(2)}, u32[]{:S(2)}) %collective-permute-start.20) | collective-permute-done | bytes 163872 | tf_op jit(solution)/shard_map/ppermute | solution.py:53
  83.2 15.1 %all_to_all.15.pieces = bf16[16,8,640]{2,1,0:T(8,128)(2,1)S(1)} all-to-all(bf16[16,8,640]{2,1,0:T(8,128)(2,1)S(1)} %fusion), channel_id=1, replica_groups={{0,1,2,3,4,5,6,7,8,9,10,11,12,13,14,15},{16,17,18,19,20,21,22,23,24,25,..., dimensions={0} | all-to-all | bytes 327680 | tf_op jit(solution)/shard_map/all_to_all | solution.py:455
  98.5 17.5 %all_to_all.16 = f32[256,1,128]{2,1,0:T(1,128)S(1)} all-to-all(f32[256,1,128]{2,1,0:T(1,128)S(1)} %broadcast_in_dim.17), channel_id=1, replica_groups=mesh['fsdp'=256] {'fsdp'}, dimensions={0} | all-to-all | bytes 262144 | tf_op jit(solution)/shard_map/all_to_all | solution.py:466
  116.1 1.6 %shard_map.166 = (f32[8,1152]{1,0:T(8,128)}, f32[4,2048]{1,0:T(4,128)}, f32[4,1152]{1,0:T(4,128)}) custom-call(f32[256,128]{1,0:T(8,128)S(1)} %bitcast.8, f32[8,1152]{1,0:T(8,128)S(1)} %get-tuple-element.48.grad_rows, f32[8,1152]{1,0:T(8,128)S(1)} %copy-done.1, f32[8,1152]{1,0:T(8,128)S(1)} %copy-done.2, f32[4,2048]{1,0:T(4,128)S(1)} %copy-done.3, ...), custom_call_target="tpu_custom_call" | custom-call | tf_op jit(solution)/shard_map/pallas_call | solution.py:311
  (84 shorter events, 15.1 us)
Async XLA Ops:
  2.2 19.6 %all-to-all-start = ((bf16[16,8,640]{2,1,0:T(8,128)(2,1)}), bf16[16,8,640]{2,1,0:T(8,128)(2,1)S(1)}, u32[]{:S(2)}, u32[]{:S(2)}) async-start(bf16[16,8,640]{2,1,0:T(8,128)(2,1)} %shard_map.157), calls=%async_computation | async-start | bytes 327680 | tf_op jit(solution)/shard_map/all_to_all | solution.py:379
  12.9 1.6 %collective-permute-start.1 = (f32[8,128]{1,0:T(8,128)S(1)}, f32[8,128]{1,0:T(8,128)S(1)}, u32[]{:S(2)}, u32[]{:S(2)}) collective-permute-start(f32[8,128]{1,0:T(8,128)S(1)} %broadcast_in_dim.14), channel_id=1, source_target_pairs={{0,1},{1,0},{2,3},{3,2},{4,5},{5,4},{6,7},{7,6},{8,9},{9,8},{10,11... | collective-permute-start | bytes 12296 | tf_op jit(solution)/shard_map/ppermute | solution.py:53
  21.8 6.0 %collective-permute-start.4 = (bf16[128,640]{1,0:T(8,128)(2,1)S(1)}, bf16[128,640]{1,0:T(8,128)(2,1)S(1)}, u32[]{:S(2)}, u32[]{:S(2)}) collective-permute-start(bf16[128,640]{1,0:T(8,128)(2,1)S(1)} %bitcast.11), channel_id=1, source_target_pairs={{0,32},{16,48},{32,0},{48,16},{2,34},{18,50},{34,2},{50,18},{4,36}... | collective-permute-start | bytes 491528 | tf_op jit(solution)/shard_map/ppermute | solution.py:53
  24.8 5.1 %collective-permute-start.5 = (bf16[128,640]{1,0:T(8,128)(2,1)S(1)}, bf16[128,640]{1,0:T(8,128)(2,1)S(1)}, u32[]{:S(2)}, u32[]{:S(2)}) collective-permute-start(bf16[128,640]{1,0:T(8,128)(2,1)S(1)} %bitcast.12), channel_id=1, source_target_pairs={{0,48},{16,0},{32,16},{48,32},{2,50},{18,2},{34,18},{50,34},{4,52}... | collective-permute-start | bytes 491528 | tf_op jit(solution)/shard_map/ppermute | solution.py:53
  25.6 6.8 %collective-permute-start.3 = (bf16[128,640]{1,0:T(8,128)(2,1)S(1)}, bf16[128,640]{1,0:T(8,128)(2,1)S(1)}, u32[]{:S(2)}, u32[]{:S(2)}) collective-permute-start(bf16[128,640]{1,0:T(8,128)(2,1)S(1)} %bitcast.14), channel_id=1, source_target_pairs={{0,16},{16,32},{32,48},{48,0},{2,18},{18,34},{34,50},{50,2},{4,20}... | collective-permute-start | bytes 491528 | tf_op jit(solution)/shard_map/ppermute | solution.py:53
  26.3 16.9 %collective-permute-start = (bf16[128,2048]{1,0:T(8,128)(2,1)S(1)}, bf16[128,2048]{1,0:T(8,128)(2,1)S(1)}, u32[]{:S(2)}, u32[]{:S(2)}) collective-permute-start(bf16[128,2048]{1,0:T(8,128)(2,1)S(1)} %copy-done), channel_id=1, source_target_pairs={{0,1},{1,0},{2,3},{3,2},{4,5},{5,4},{6,7},{7,6},{8,9},{9,8},{10,11... | collective-permute-start | bytes 1572872 | tf_op jit(solution)/shard_map/ppermute | solution.py:53
  29.9 6.5 %collective-permute-start.9 = (bf16[256,640]{1,0:T(8,128)(2,1)S(1)}, bf16[256,640]{1,0:T(8,128)(2,1)S(1)}, u32[]{:S(2)}, u32[]{:S(2)}) collective-permute-start(bf16[256,640]{1,0:T(8,128)(2,1)S(1)} %constant_dynamic-update-slice_fusion.2.refs_1_.plane_b), channel_id=1, source_target_pairs={{0,192},{64,0},{128,64},{192,128},{2,194},{66,2},{130,66},{194,130... | collective-permute-start | bytes 983048 | tf_op jit(solution)/shard_map/ppermute | solution.py:53
  32.3 13.5 %collective-permute-start.7 = (bf16[256,640]{1,0:T(8,128)(2,1)S(1)}, bf16[256,640]{1,0:T(8,128)(2,1)S(1)}, u32[]{:S(2)}, u32[]{:S(2)}) collective-permute-start(bf16[256,640]{1,0:T(8,128)(2,1)S(1)} %constant_dynamic-update-slice_fusion.2.refs_1_.plane_b), channel_id=1, source_target_pairs={{0,64},{64,128},{128,192},{192,0},{2,66},{66,130},{130,194},{194,2... | collective-permute-start | bytes 983048 | tf_op jit(solution)/shard_map/ppermute | solution.py:53
  32.4 10.9 %collective-permute-start.6 = (bf16[256,640]{1,0:T(8,128)(2,1)S(1)}, bf16[256,640]{1,0:T(8,128)(2,1)S(1)}, u32[]{:S(2)}, u32[]{:S(2)}) collective-permute-start(bf16[256,640]{1,0:T(8,128)(2,1)S(1)} %constant_dynamic-update-slice_fusion.refs_0_.plane_a), channel_id=1, source_target_pairs={{0,64},{64,128},{128,192},{192,0},{2,66},{66,130},{130,194},{194,2... | collective-permute-start | bytes 983048 | tf_op jit(solution)/shard_map/ppermute | solution.py:53
  33.1 14.0 %collective-permute-start.12 = (bf16[128,512]{1,0:T(8,128)(2,1)S(1)}, bf16[128,512]{1,0:T(8,128)(2,1)S(1)}, u32[]{:S(2)}, u32[]{:S(2)}) collective-permute-start(bf16[128,512]{1,0:T(8,128)(2,1)S(1)} %get-tuple-element.49), channel_id=1, source_target_pairs={{0,1},{1,0},{2,3},{3,2},{4,5},{5,4},{6,7},{7,6},{8,9},{9,8},{10,11... | collective-permute-start | bytes 393224 | tf_op jit(solution)/shard_map/ppermute | solution.py:53
  36.3 10.0 %collective-permute-start.8 = (bf16[256,640]{1,0:T(8,128)(2,1)S(1)}, bf16[256,640]{1,0:T(8,128)(2,1)S(1)}, u32[]{:S(2)}, u32[]{:S(2)}) collective-permute-start(bf16[256,640]{1,0:T(8,128)(2,1)S(1)} %constant_dynamic-update-slice_fusion.refs_0_.plane_a), channel_id=1, source_target_pairs={{0,192},{64,0},{128,64},{192,128},{2,194},{66,2},{130,66},{194,130... | collective-permute-start | bytes 983048 | tf_op jit(solution)/shard_map/ppermute | solution.py:53
  43.3 6.2 %collective-permute-start.11 = (bf16[256,640]{1,0:T(8,128)(2,1)S(1)}, bf16[256,640]{1,0:T(8,128)(2,1)S(1)}, u32[]{:S(2)}, u32[]{:S(2)}) collective-permute-start(bf16[256,640]{1,0:T(8,128)(2,1)S(1)} %collective-permute-done.9.refs_5_), channel_id=1, source_target_pairs={{0,192},{64,0},{128,64},{192,128},{2,194},{66,2},{130,66},{194,130... | collective-permute-start | bytes 983048 | tf_op jit(solution)/shard_map/ppermute | solution.py:53
  43.3 10.2 %collective-permute-start.10 = (bf16[256,640]{1,0:T(8,128)(2,1)S(1)}, bf16[256,640]{1,0:T(8,128)(2,1)S(1)}, u32[]{:S(2)}, u32[]{:S(2)}) collective-permute-start(bf16[256,640]{1,0:T(8,128)(2,1)S(1)} %collective-permute-done.6.refs_2_), channel_id=1, source_target_pairs={{0,64},{64,128},{128,192},{192,0},{2,66},{66,130},{130,194},{194,2... | collective-permute-start | bytes 983048 | tf_op jit(solution)/shard_map/ppermute | solution.py:53
  45.9 14.5 %collective-permute-start.16 = (bf16[256,512]{1,0:T(8,128)(2,1)S(1)}, bf16[256,512]{1,0:T(8,128)(2,1)S(1)}, u32[]{:S(2)}, u32[]{:S(2)}) collective-permute-start(bf16[256,512]{1,0:T(8,128)(2,1)S(1)} %get-tuple-element.29.scaled2), channel_id=1, source_target_pairs={{0,128},{64,192},{128,0},{192,64},{2,130},{66,194},{130,2},{194,66... | collective-permute-start | bytes 786440 | tf_op jit(solution)/shard_map/ppermute | solution.py:53
  57.5 7.9 %collective-permute-start.17 = (bf16[256,640]{1,0:T(8,128)(2,1)S(1)}, bf16[256,640]{1,0:T(8,128)(2,1)S(1)}, u32[]{:S(2)}, u32[]{:S(2)}) collective-permute-start(bf16[256,640]{1,0:T(8,128)(2,1)S(1)} %shard_map.160.down), channel_id=1, source_target_pairs={{0,128},{64,192},{128,0},{192,64},{2,130},{66,194},{130,2},{194,66... | collective-permute-start | bytes 983048 | tf_op jit(solution)/shard_map/ppermute | solution.py:53
  57.6 13.8 %collective-permute-start.15 = (bf16[256,640]{1,0:T(8,128)(2,1)S(1)}, bf16[256,640]{1,0:T(8,128)(2,1)S(1)}, u32[]{:S(2)}, u32[]{:S(2)}) collective-permute-start(bf16[256,640]{1,0:T(8,128)(2,1)S(1)} %shard_map.160.down), channel_id=1, source_target_pairs={{0,64},{64,128},{128,192},{192,0},{2,66},{66,130},{130,194},{194,2... | collective-permute-start | bytes 983048 | tf_op jit(solution)/shard_map/ppermute | solution.py:53
  57.7 14.4 %collective-permute-start.13 = (bf16[256,640]{1,0:T(8,128)(2,1)S(1)}, bf16[256,640]{1,0:T(8,128)(2,1)S(1)}, u32[]{:S(2)}, u32[]{:S(2)}) collective-permute-start(bf16[256,640]{1,0:T(8,128)(2,1)S(1)} %shard_map.160.down), channel_id=1, source_target_pairs={{0,192},{64,0},{128,64},{192,128},{2,194},{66,2},{130,66},{194,130... | collective-permute-start | bytes 983048 | tf_op jit(solution)/shard_map/ppermute | solution.py:53
  60.3 11.1 %collective-permute-start.14 = (bf16[256,512]{1,0:T(8,128)(2,1)S(1)}, bf16[256,512]{1,0:T(8,128)(2,1)S(1)}, u32[]{:S(2)}, u32[]{:S(2)}) collective-permute-start(bf16[256,512]{1,0:T(8,128)(2,1)S(1)} %get-tuple-element.31.scaled3), channel_id=1, source_target_pairs={{0,64},{64,128},{128,192},{192,0},{2,66},{66,130},{130,194},{194,2... | collective-permute-start | bytes 786440 | tf_op jit(solution)/shard_map/ppermute | solution.py:53
  60.3 11.7 %collective-permute-start.2 = (bf16[256,512]{1,0:T(8,128)(2,1)S(1)}, bf16[256,512]{1,0:T(8,128)(2,1)S(1)}, u32[]{:S(2)}, u32[]{:S(2)}) collective-permute-start(bf16[256,512]{1,0:T(8,128)(2,1)S(1)} %get-tuple-element.28.scaled1), channel_id=1, source_target_pairs={{0,192},{64,0},{128,64},{192,128},{2,194},{66,2},{130,66},{194,130... | collective-permute-start | bytes 786440 | tf_op jit(solution)/shard_map/ppermute | solution.py:53
  73.3 42.8 %copy-start.1 = (f32[8,1152]{1,0:T(8,128)S(1)}, f32[8,1152]{1,0:T(8,128)}, u32[]{:S(2)}) copy-start(f32[8,1152]{1,0:T(8,128)} %weight_first.1) | copy-start | bytes 110596
  73.3 42.7 %copy-start.2 = (f32[8,1152]{1,0:T(8,128)S(1)}, f32[8,1152]{1,0:T(8,128)}, u32[]{:S(2)}) copy-start(f32[8,1152]{1,0:T(8,128)} %weight_second.1) | copy-start | bytes 110596
  73.4 6.3 %collective-permute-start.18 = (bf16[128,640]{1,0:T(8,128)(2,1)S(1)}, bf16[128,640]{1,0:T(8,128)(2,1)S(1)}, u32[]{:S(2)}, u32[]{:S(2)}) collective-permute-start(bf16[128,640]{1,0:T(8,128)(2,1)S(1)} %get-tuple-element.44), channel_id=1, source_target_pairs={{0,48},{16,0},{32,16},{48,32},{2,50},{18,2},{34,18},{50,34},{4,52}... | collective-permute-start | bytes 491528 | tf_op jit(solution)/shard_map/ppermute | solution.py:53
  75.7 5.8 %collective-permute-start.19 = (bf16[128,640]{1,0:T(8,128)(2,1)S(1)}, bf16[128,640]{1,0:T(8,128)(2,1)S(1)}, u32[]{:S(2)}, u32[]{:S(2)}) collective-permute-start(bf16[128,640]{1,0:T(8,128)(2,1)S(1)} %get-tuple-element.45), channel_id=1, source_target_pairs={{0,32},{16,48},{32,0},{48,16},{2,34},{18,50},{34,2},{50,18},{4,36}... | collective-permute-start | bytes 491528 | tf_op jit(solution)/shard_map/ppermute | solution.py:53
  75.7 7.4 %collective-permute-start.20 = (bf16[128,640]{1,0:T(8,128)(2,1)S(1)}, bf16[128,640]{1,0:T(8,128)(2,1)S(1)}, u32[]{:S(2)}, u32[]{:S(2)}) collective-permute-start(bf16[128,640]{1,0:T(8,128)(2,1)S(1)} %get-tuple-element.46), channel_id=1, source_target_pairs={{0,16},{16,32},{32,48},{48,0},{2,18},{18,34},{34,50},{50,2},{4,20}... | collective-permute-start | bytes 491528 | tf_op jit(solution)/shard_map/ppermute | solution.py:53
  (10 other events, 321.5 us)
